TPU v7x, 32 devices: a whole 2x2x4 slice. The times are simulated.
32 devices in a mesh: ctx: 8 (over y, x, core), fsdp: 4 (over z).
Axes of the slice: x: 2, y: 2, z: 4, core: 2. Of those that a mesh axis runs over, the one named last changes fastest.
Arguments:
- block_input: bfloat16 [4096, 2048], P(('ctx', 'fsdp')), may hold values from -6 to 6
- positions: int32 [4096], P(('ctx', 'fsdp')), may hold values from 0 to 4095, as said below
- query_weight: bfloat16 [2048, 2048], P(None, 'fsdp'), may hold values from -0.125 to 0.125
- key_weight: bfloat16 [2048, 2048], P(None, 'fsdp'), may hold values from -0.125 to 0.125
- value_weight: bfloat16 [2048, 2048], P(None, 'fsdp'), may hold values from -0.125 to 0.125
- output_weight: bfloat16 [2048, 2048], P('fsdp'), may hold values from -0.125 to 0.125
- query_gain: float32 [2048], replicated, may hold values from 0.7 to 6.5
- key_gain: float32 [2048], replicated, may hold values from 0.7 to 6.5
- attn_gain: float32 [2048], replicated, may hold values from 0.1 to 1.9
- mlp_gain: float32 [2048], replicated, may hold values from 0.1 to 1.9
- gate_weight: bfloat16 [2048, 8192], P(None, 'fsdp'), may hold values from -0.125 to 0.125
- up_weight: bfloat16 [2048, 8192], P(None, 'fsdp'), may hold values from -0.125 to 0.125
- down_weight: bfloat16 [8192, 2048], P('fsdp'), may hold values from -0.0625 to 0.0625
- cotangent: bfloat16 [4096, 2048], P(('ctx', 'fsdp')), may hold values from -6 to 6
Outputs:
- block_output: bfloat16 [4096, 2048], P(('ctx', 'fsdp'))
- input_grad: float32 [4096, 2048], P(('ctx', 'fsdp'))
- query_weight_grad: float32 [2048, 2048], P('ctx', 'fsdp')
- key_weight_grad: float32 [2048, 2048], P('ctx', 'fsdp')
- value_weight_grad: float32 [2048, 2048], P('ctx', 'fsdp')
- output_weight_grad: float32 [2048, 2048], P('fsdp', 'ctx')
- query_gain_grad: float32 [2048], P('ctx')
- key_gain_grad: float32 [2048], P('ctx')
- attn_gain_grad: float32 [2048], P('ctx')
- mlp_gain_grad: float32 [2048], P('ctx')
- gate_weight_grad: float32 [2048, 8192], P('ctx', 'fsdp')
- up_weight_grad: float32 [2048, 8192], P('ctx', 'fsdp')
- down_weight_grad: float32 [8192, 2048], P('fsdp', 'ctx')
Inputs may be any that keep to these rules, and one draw needn't show every extreme that they name: positions hold every number below 4096 once, in runs of 256 consecutive numbers each starting at a multiple of 256; the order of the runs is arbitrary.
All inputs are finite; a program needn't handle non-finite values.
Results may differ from a plain program's by a relative error of at most 0.04.
Values may be sent and summed in bfloat16 or wider, within the bound.
A program may use at most 384 MiB of HBM per device.

v0:
```python
import functools
import math

import jax
import jax.numpy as jnp
from jax import lax
from jax.experimental import pallas as pl
from jax.experimental.pallas import tpu as pltpu
from jax.sharding import PartitionSpec as P


HD = 128
norm_eps = 1e-06
rope_base = 500000.0
big_negative = -1e30
LOG2E = math.log2(math.e)
BF = jnp.bfloat16
F32 = jnp.float32


def mm(left, right):
    return jnp.dot(left, right, preferred_element_type=F32)


def contract_rows(left, right):
    return lax.dot_general(left, right, (((0,), (0,)), ((), ())), preferred_element_type=F32)


def contract_cols(left, right):
    return lax.dot_general(left, right, (((1,), (1,)), ((), ())), preferred_element_type=F32)


def gate(x, *tokens):
    return lax.optimization_barrier((x, *tokens))[0]


def shift(x, n, by):
    return lax.ppermute(x, "fsdp", [(i, (i + by) % n) for i in range(n)])


def ring_gather(x, n, around=None):
    slots = [x]
    for _ in range(n - 1):
        slots.append(shift(slots[-1], around or n, 1))
    return slots


def ring_scatter(part, n, under=(), started=None):
    if n == 1:
        return part(0)
    acc = part(1).astype(BF)
    if started is not None:
        started.append(acc)
    for s in range(2, n):
        acc = (shift(acc, n, 1).astype(F32) + part(s)).astype(BF)
    return gate(shift(acc, n, 1), *under).astype(F32) + part(0)


def slot_sum(x, n, flat=None):
    total, flat_total = x, flat
    cut = x.shape[-1]
    both = x if flat is None else jnp.concatenate([x, flat], axis=-1)
    for t in range(1, n):
        got = shift(both, n, t)
        total = total + jnp.roll(got[..., :cut], t, axis=0)
        if flat is not None:
            flat_total = flat_total + got[..., cut:]
    return total if flat is None else (total, flat_total)


def swap(x, n, bit):
    return lax.ppermute(x, "ctx", [(i, i ^ bit) for i in range(n)])


def bit_orders(n):
    bits = []
    b = 2
    while b < n:
        bits.append(b)
        b *= 2
    return bits, bits[::-1]


def halving(part, me, n, order, under=()):
    seq = ([1] if n > 1 else []) + list(order[::-1])
    block = part.shape[0] // n
    levels = len(seq)
    masks = [
        sum(seq[k] for k in range(levels) if t >> (levels - 1 - k) & 1) for t in range(n)
    ]

    def blocks(ms):
        return jnp.concatenate(
            [lax.dynamic_slice_in_dim(part, (me ^ m) * block, block) for m in ms]
        )

    keep, away = blocks(masks[: n // 2]), blocks(masks[n // 2 :])
    for k, bit in enumerate(seq):
        got = swap(away.astype(BF), n, bit)
        if k == 0 and under:
            got = gate(got, *under)
        total = keep.astype(F32) + got.astype(F32)
        rest = total.shape[0] // 2
        if k < levels - 1:
            total = total.astype(BF)
            keep, away = total[:rest], total[rest:]
    return total


def distance(m):
    return bin(m >> 1).count("1")


def group_order(n):
    pairs = [(m, m + 1) if n > 1 else (m,) for m in range(0, n, 2)]
    return sorted(pairs, key=lambda g: (distance(g[0]), g[0]))


def came_from(m, order):
    if m & 1:
        return m ^ 1, 1
    bit = [b for b in order if m & b][-1]
    return m ^ bit, bit


def vmem(*_):
    return pl.BlockSpec(memory_space=pltpu.VMEM)


def prep_kernel(n, heads, *refs):
    q_refs, k_refs, v_refs = refs[:n], refs[n : 2 * n], refs[2 * n : 3 * n]
    qr_ref, kr_ref, qg_ref, kg_ref, cos_ref, sin_ref = refs[3 * n : 3 * n + 6]
    qo_ref, kva_ref, kvb_ref = refs[3 * n + 6 :]
    rows = q_refs[0].shape[0]
    half = n // 2
    for s in range(n):
        r = slice(s * rows, (s + 1) * rows)
        cosine, sine = cos_ref[r, :], sin_ref[r, :]
        out = kva_ref if s < half else kvb_ref
        o = slice((s % half) * rows, (s % half + 1) * rows)
        for h in range(heads):
            c = slice(h * HD, (h + 1) * HD)
            x = q_refs[s][:, c] * qr_ref[r, :] * qg_ref[:, c]
            qo_ref[r, c] = (x * cosine + pltpu.roll(x, HD // 2, 1) * sine).astype(BF)
            y = k_refs[s][:, c] * kr_ref[r, :] * kg_ref[:, c]
            out[o, c] = (y * cosine + pltpu.roll(y, HD // 2, 1) * sine).astype(BF)
            out[o, heads * HD + h * HD : heads * HD + (h + 1) * HD] = v_refs[s][:, c].astype(BF)


def key_mask(starts_ref, piece, slots, rows, qpos):
    parts = []
    for j in range(slots):
        row = lax.broadcasted_iota(jnp.int32, (rows, 1), 0)
        parts.append(row + starts_ref[piece * slots + j])
    return jnp.concatenate(parts, axis=0) <= qpos


def fwd_kernel(npieces, slots, first, last, *refs):
    starts_ref, q_ref, qpos_ref = refs[:3]
    k_refs = refs[3 : 3 + npieces]
    v_refs = refs[3 + npieces : 3 + 2 * npieces]
    rest = refs[3 + 2 * npieces :]
    if not first:
        m_in, l_in, a_in = rest[:3]
        rest = rest[3:]
    rows = k_refs[0].shape[0] // slots
    c2 = LOG2E / math.sqrt(HD)
    q = q_ref[...]
    qpos = qpos_ref[...]
    scores = []
    top = None if first else m_in[0]
    for i in range(npieces):
        s = contract_cols(k_refs[i][...], q)
        s = jnp.where(key_mask(starts_ref, i, slots, rows, qpos), s, big_negative)
        scores.append(s)
        t = jnp.max(s, axis=0, keepdims=True)
        top = t if top is None else jnp.maximum(top, t)
    total = None
    acc = None
    for i in range(npieces):
        p = jnp.exp2((scores[i] - top) * c2)
        t = jnp.sum(p, axis=0, keepdims=True)
        a = contract_rows(v_refs[i][...], p.astype(BF))
        total = t if total is None else total + t
        acc = a if acc is None else acc + a
    if not first:
        alpha = jnp.exp2((m_in[0] - top) * c2)
        total = total + l_in[0] * alpha
        acc = acc + a_in[...] * alpha
    if last:
        mix_ref, mixb_ref, log_ref = rest
        mix = (acc / total).T
        mix_ref[...] = mix
        mixb_ref[...] = mix.astype(BF)
        log_ref[0] = top * c2 + jnp.log2(total)
    else:
        m_out, l_out, a_out = rest
        m_out[0] = top
        l_out[0] = total
        a_out[...] = acc


def attend(starts, q, qpos, kv, carry, heads, slots, last):
    span = q.shape[0]
    first = carry is None
    np_ = len(kv)
    pr = kv[0].shape[0]
    row = pl.BlockSpec((1, 1, span), lambda h: (h, 0, 0))
    accs = pl.BlockSpec((HD, span), lambda h: (h, 0))
    specs = [
        pl.BlockSpec(memory_space=pltpu.SMEM),
        pl.BlockSpec((span, HD), lambda h: (0, h)),
        pl.BlockSpec((1, span), lambda h: (0, 0)),
    ]
    specs += [pl.BlockSpec((pr, HD), lambda h: (0, h))] * np_
    specs += [pl.BlockSpec((pr, HD), lambda h: (0, heads + h))] * np_
    args = [starts, q, qpos, *kv, *kv]
    if not first:
        specs += [row, row, accs]
        args += list(carry)
    rshape = jax.ShapeDtypeStruct((heads, 1, span), F32)
    if last:
        mix = pl.BlockSpec((span, HD), lambda h: (0, h))
        outs = [mix, mix, row]
        shapes = [
            jax.ShapeDtypeStruct((span, heads * HD), F32),
            jax.ShapeDtypeStruct((span, heads * HD), BF),
            rshape,
        ]
    else:
        outs = [row, row, accs]
        shapes = [rshape, rshape, jax.ShapeDtypeStruct((heads * HD, span), F32)]
    keys = np_ * pr
    return pl.pallas_call(
        functools.partial(fwd_kernel, np_, slots, first, last),
        grid=(heads,),
        in_specs=specs,
        out_specs=outs,
        out_shape=shapes,
        cost_estimate=pl.CostEstimate(
            flops=8 * span * keys * HD * heads,
            bytes_accessed=4 * keys * heads * HD,
            transcendentals=span * keys * heads,
        ),
    )(*args)


def bwd_kernel(npieces, slots, heads, first, *refs):
    starts_ref, q_ref, do_ref, mix_ref, log_ref, qpos_ref = refs[:6]
    k_refs = refs[6 : 6 + npieces]
    v_refs = refs[6 + npieces : 6 + 2 * npieces]
    rest = refs[6 + 2 * npieces :]
    if not first:
        dq_in = rest[0]
        rest = rest[1:]
    dq_ref, out_refs = rest[0], rest[1:]
    h = pl.program_id(0)
    rows = k_refs[0].shape[0] // slots
    scale = 1.0 / math.sqrt(HD)
    c2 = LOG2E * scale
    q = q_ref[...]
    do = do_ref[...]
    delta = jnp.sum((do.astype(F32) * mix_ref[...]).T, axis=0, keepdims=True)
    log2 = log_ref[0]
    qpos = qpos_ref[...]
    dq = None
    for i in range(npieces):
        k = k_refs[i][...]
        s = contract_cols(k, q) * c2 - log2
        s = jnp.where(key_mask(starts_ref, i, slots, rows, qpos), s, big_negative)
        p = jnp.exp2(s)
        dp = contract_cols(v_refs[i][...], do)
        ds = (p * (dp - delta)).astype(BF)
        t = contract_rows(k, ds)
        dq = t if dq is None else dq + t
        kc = pl.ds(pl.multiple_of(h * HD, HD), HD)
        vc = pl.ds(pl.multiple_of((heads + h) * HD, HD), HD)
        out_refs[i][:, kc] = (mm(ds, q) * scale).astype(BF)
        out_refs[i][:, vc] = mm(p.astype(BF), do).astype(BF)
    dq = dq * scale
    dq_ref[...] = dq if first else dq + dq_in[...]


def attend_back(starts, q, do, mix, log, qpos, kv, dq, heads, slots):
    span = q.shape[0]
    first = dq is None
    np_ = len(kv)
    pr = kv[0].shape[0]
    head = pl.BlockSpec((span, HD), lambda h: (0, h))
    accs = pl.BlockSpec((HD, span), lambda h: (h, 0))
    specs = [
        pl.BlockSpec(memory_space=pltpu.SMEM),
        head,
        head,
        head,
        pl.BlockSpec((1, 1, span), lambda h: (h, 0, 0)),
        pl.BlockSpec((1, span), lambda h: (0, 0)),
    ]
    specs += [pl.BlockSpec((pr, HD), lambda h: (0, h))] * np_
    specs += [pl.BlockSpec((pr, HD), lambda h: (0, heads + h))] * np_
    args = [starts, q, do, mix, log, qpos, *kv, *kv]
    if not first:
        specs.append(accs)
        args.append(dq)
    keys = np_ * pr
    return pl.pallas_call(
        functools.partial(bwd_kernel, np_, slots, heads, first),
        grid=(heads,),
        in_specs=specs,
        out_specs=[accs] + [pl.BlockSpec((pr, 2 * heads * HD), lambda h: (0, 0))] * np_,
        out_shape=[jax.ShapeDtypeStruct((heads * HD, span), F32)]
        + [jax.ShapeDtypeStruct((pr, 2 * heads * HD), BF)] * np_,
        cost_estimate=pl.CostEstimate(
            flops=20 * span * keys * HD * heads,
            bytes_accessed=8 * keys * heads * HD,
            transcendentals=span * keys * heads,
        ),
    )(*args)


def turn_back(x, cosine, sine):
    return x * cosine - pltpu.roll(x, HD // 2, 1) * sine


def unrotate_kernel(n, heads, transposed, *refs):
    nd = 1 if transposed else 2
    d_refs = refs[:nd]
    raw_refs = refs[nd : nd + n]
    r_ref, g_ref, cos_ref, sin_ref, w_ref, inner_ref, gain_ref = refs[nd + n :]
    rows = raw_refs[0].shape[0]
    half = n // 2
    for h in range(heads):
        c = slice(h * HD, (h + 1) * HD)
        gain_sum = None
        whole = d_refs[0][c, :].T if transposed else None
        for s in range(n):
            r = slice(s * rows, (s + 1) * rows)
            if transposed:
                d = whole[r, :]
            else:
                o = slice((s % half) * rows, (s % half + 1) * rows)
                d = d_refs[0 if s < half else 1][o, c].astype(F32)
            grad = turn_back(d, cos_ref[r, :], sin_ref[r, :])
            raw = raw_refs[s][:, c]
            weighted = grad * g_ref[:, c]
            w_ref[r, c] = weighted
            t = jnp.sum(weighted * raw, axis=1, keepdims=True)
            inner_ref[r, :] = t if h == 0 else inner_ref[r, :] + t
            u = jnp.sum(grad * raw * r_ref[r, :], axis=0, keepdims=True)
            gain_sum = u if gain_sum is None else gain_sum + u
        gain_ref[:, c] = gain_sum


def unrotate(d, raw, rms, gain, cosine, sine, heads, transposed):
    n = len(raw)
    span = n * raw[0].shape[0]
    units = heads * HD
    return pl.pallas_call(
        functools.partial(unrotate_kernel, n, heads, transposed),
        in_specs=[vmem()] * (len(d) + n + 4),
        out_specs=[vmem()] * 3,
        out_shape=[
            jax.ShapeDtypeStruct((span, units), F32),
            jax.ShapeDtypeStruct((span, 1), F32),
            jax.ShapeDtypeStruct((1, units), F32),
        ],
    )(*d, *raw, rms, gain, cosine, sine)


def norm_back(raw, rms_inv, gain, grad_out):
    weighted = gain * grad_out
    inner = jnp.sum(weighted * raw, axis=1, keepdims=True)
    width = raw.shape[1]
    return (
        rms_inv[:, None] * weighted - raw * (rms_inv * rms_inv * rms_inv)[:, None] * inner / width
    )


def local(
    nc,
    nf,
    block_input,
    positions,
    query_weight,
    key_weight,
    value_weight,
    output_weight,
    query_gain,
    key_gain,
    attn_gain,
    mlp_gain,
    gate_weight,
    up_weight,
    down_weight,
    cotangent,
):
    rows, width = block_input.shape
    span = rows * nf
    units = query_weight.shape[1]
    heads = units // HD
    half = nf // 2
    me_c = lax.axis_index("ctx")
    me_f = lax.axis_index("fsdp")
    unit_start = me_f * units

    x_slots = [block_input]
    begin = positions[:1]
    begins = None
    for s in range(1, nf):
        got = shift(x_slots[-1], nf, 1)
        if s == min(2, nf - 1):
            begin, x_last = lax.optimization_barrier((begin, mm(x_slots[-1], query_weight)))
            begins = jnp.concatenate([begin] + [shift(begin, nf, t) for t in range(1, nf)])[None, :]
            b = 1
            while b < nc:
                begins = jnp.concatenate([begins, swap(begins, nc, b)])
                b *= 2
        if s == nf - 1:
            got, begins = lax.optimization_barrier((got, begins))
        x_slots.append(got)

    row_pos = (begins[0][:, None] + jnp.arange(rows)[None, :]).reshape(span)
    freqs = jnp.exp(-math.log(rope_base) * 2.0 * jnp.arange(HD // 2).astype(F32) / HD)
    angles = row_pos.astype(F32)[:, None] * freqs[None, :]
    cosine, sine = jnp.cos(angles), jnp.sin(angles)
    cosine = jnp.concatenate([cosine, cosine], axis=1)
    sine = jnp.concatenate([-sine, sine], axis=1)
    qpos = row_pos[None, :]

    q_raw = [mm(x, query_weight) for x in x_slots]
    q_raw[min(2, nf - 1) - 1] = x_last
    k_raw = [mm(x, key_weight) for x in x_slots]
    v_raw = [mm(x, value_weight) for x in x_slots]
    squares = jnp.stack(
        [
            jnp.stack([jnp.sum(q * q, axis=1), jnp.sum(k * k, axis=1)])
            for q, k in zip(q_raw, k_raw)
        ]
    )
    squares = slot_sum(squares, nf)
    query_rms = lax.rsqrt(squares[:, 0].reshape(span, 1) / width + norm_eps)
    key_rms = lax.rsqrt(squares[:, 1].reshape(span, 1) / width + norm_eps)
    query_scale = lax.dynamic_slice_in_dim(query_gain, unit_start, units)[None, :]
    key_scale = lax.dynamic_slice_in_dim(key_gain, unit_start, units)[None, :]

    query_rot, kv_a, kv_b = pl.pallas_call(
        functools.partial(prep_kernel, nf, heads),
        in_specs=[vmem()] * (3 * nf + 6),
        out_specs=[vmem()] * 3,
        out_shape=[jax.ShapeDtypeStruct((span, units), BF)]
        + [jax.ShapeDtypeStruct((span // 2, 2 * units), BF)] * 2,
    )(*q_raw, *k_raw, *v_raw, query_rms, key_rms, query_scale, key_scale, cosine, sine)

    orders = bit_orders(nc)
    groups = group_order(nc)
    pieces = [{0: kv_a}, {0: kv_b}]

    def fetch(i, m, token):
        if m not in pieces[i]:
            src, bit = came_from(m, orders[i])
            have = fetch(i, src, token)
            if token is not None:
                have = gate(have, token)
            pieces[i][m] = swap(have, nc, bit)
        return pieces[i][m]

    def group_inputs(group):
        kv = [pieces[0][m] for m in group] + [pieces[1][m] for m in group]
        starts = jnp.concatenate(
            [begins[m, :half] for m in group] + [begins[m, half:] for m in group]
        )
        return starts, kv

    carry = None
    tokens = []
    for group in groups:
        for m in group:
            for i in range(2):
                far = distance(m)
                if far < 2:
                    fetch(i, m, None)
                else:
                    fetch(i, m, tokens[1] if m & 1 else tokens[0])
        starts, kv = group_inputs(group)
        carry = attend(
            starts, query_rot, qpos, kv, carry, heads, half, group is groups[-1]
        )
        tokens.append(carry[0])
    mixture, mixture_b, log_total = carry

    def rows_of(x, s):
        return x[s * rows : (s + 1) * rows]

    attn_out = ring_scatter(lambda s: mm(rows_of(mixture_b, s), output_weight), nf)
    attn_rms = lax.rsqrt(jnp.mean(attn_out * attn_out, axis=1) + norm_eps)
    hidden_state = block_input.astype(F32) + attn_out * attn_rms[:, None] * attn_gain[None, :]
    state_slots = ring_gather(hidden_state.astype(BF), nf)
    gate_pre = [mm(x, gate_weight) for x in state_slots]
    up_pre = [mm(x, up_weight) for x in state_slots]
    activated = [(jax.nn.silu(g) * u).astype(BF) for g, u in zip(gate_pre, up_pre)]
    mlp_out = ring_scatter(lambda s: mm(activated[s], down_weight), nf)
    mlp_rms = lax.rsqrt(jnp.mean(mlp_out * mlp_out, axis=1) + norm_eps)
    block_output = (hidden_state + mlp_out * mlp_rms[:, None] * mlp_gain[None, :]).astype(BF)
    upstream = cotangent.astype(F32)
    mlp_gain_part = jnp.sum(upstream * mlp_out * mlp_rms[:, None], axis=0)
    mlp_grad_b = norm_back(mlp_out, mlp_rms, mlp_gain[None, :], upstream).astype(BF)

    def ctx_scatter(x):
        return lax.psum_scatter(x, "ctx", scatter_dimension=0, tiled=True)

    def slot_grads(s, rows_in):
        activ_grad = contract_cols(rows_in, down_weight)
        sg = jax.nn.sigmoid(gate_pre[s])
        g = (activ_grad * up_pre[s] * sg * (1.0 + gate_pre[s] * (1.0 - sg))).astype(BF)
        return g, (activ_grad * gate_pre[s] * sg).astype(BF)

    def state_part(g, u):
        return contract_cols(g, gate_weight) + contract_cols(u, up_weight)

    grad_slots, gate_grads, up_grads = [mlp_grad_b], [], []
    acc = None
    for s in range(nf):
        got = shift(grad_slots[-1], nf, 1) if s < nf - 1 else None
        g, u = slot_grads(s, grad_slots[s])
        if s == 1:
            acc = state_part(g, u).astype(BF)
        elif s > 1:
            acc = (shift(acc, nf, 1).astype(F32) + state_part(g, u)).astype(BF)
        if got is not None:
            got, g, u = lax.optimization_barrier((got, g, u))
            grad_slots.append(got)
        gate_grads.append(g)
        up_grads.append(u)
    down_part = contract_rows(jnp.concatenate(grad_slots), jnp.concatenate(activated)).astype(BF)
    state_grad = state_part(gate_grads[0], up_grads[0])
    if nf > 1:
        got = shift(acc, nf, 1)
        state_grad = got.astype(F32) + state_grad
    state_grad = upstream + state_grad
    down_sum = ctx_scatter(down_part)

    attn_gain_part = jnp.sum(state_grad * attn_out * attn_rms[:, None], axis=0)
    attn_grad_b = norm_back(attn_out, attn_rms, attn_gain[None, :], state_grad).astype(BF)
    gate_up_part = contract_rows(
        jnp.concatenate(state_slots),
        jnp.concatenate([jnp.concatenate(gate_grads), jnp.concatenate(up_grads)], axis=1),
    ).astype(BF)
    gate_up_sum = ctx_scatter(gate_up_part)
    first_hop = shift(attn_grad_b, nf, 1)
    proj_slots = [attn_grad_b] + ring_gather(first_hop, nf - 1, around=nf)
    mixture_grad_b = jnp.concatenate(
        [contract_cols(x, output_weight).astype(BF) for x in proj_slots]
    )

    dq = None
    sums = [{}, {}]

    def send(i, m):
        into, bit = came_from(m, orders[i])
        got = swap(sums[i].pop(m), nc, bit)
        sums[i][into] = (sums[i][into].astype(F32) + got.astype(F32)).astype(BF)
        return got

    waits = []
    for gi, group in enumerate(groups[::-1]):
        starts, kv = group_inputs(group)
        if gi:
            dq = gate(dq, *waits[gi - 1])
        dq, *out = attend_back(
            starts, query_rot, mixture_grad_b, mixture, log_total, qpos, kv, dq, heads, half
        )
        for m, a, b in zip(group, out[: len(group)], out[len(group) :]):
            sums[0][m], sums[1][m] = a, b
        waits.append([send(i, m) for i in range(2) for m in group if m & 1])
    hops = []
    for far in range(max(distance(m) for m in range(nc)), 0, -1):
        for i in range(2):
            for m in [m for m in sums[i] if distance(m) == far]:
                got = send(i, m)
                if m == orders[i][-1]:
                    hops.append(got)
    dq = gate(dq, *hops)
    own_a, own_b = sums[0][0], sums[1][0]

    def unit_full(x):
        return lax.dynamic_update_slice_in_dim(jnp.zeros((width,), F32), x, unit_start, 0)

    def norm_grads(weighted, inner, raw, rms):
        cube = rms * rms * rms
        return [
            (
                rows_of(rms, s) * rows_of(weighted, s)
                - raw[s] * rows_of(cube, s) * inner[s][:, None] / width
            ).astype(BF)
            for s in range(nf)
        ]

    def spread(*vectors):
        return jnp.stack([v.reshape(nf, width // nf) for v in vectors], axis=1).reshape(nf, -1)

    def gathered(flat, count):
        return flat.reshape(nf, count, width // nf).transpose(1, 0, 2).reshape(count, width)

    query_weighted, query_inner, query_gain_part = unrotate(
        [dq], q_raw, query_rms, query_scale, cosine, sine, heads, True
    )
    query_inner, early_gains = slot_sum(
        query_inner.reshape(nf, rows),
        nf,
        spread(unit_full(query_gain_part[0]), attn_gain_part, mlp_gain_part),
    )
    query_grads = norm_grads(query_weighted, query_inner, q_raw, query_rms)

    x_rows = jnp.concatenate(x_slots)
    q_part = contract_rows(x_rows, jnp.concatenate(query_grads)).astype(BF)
    o_part = contract_rows(jnp.concatenate(proj_slots), mixture_b).astype(BF)
    qo_part = jnp.concatenate([q_part, o_part], axis=1)
    qo_part, down_sum, own_a, own_b = lax.optimization_barrier((qo_part, down_sum, own_a, own_b))
    qo_grad = ctx_scatter(qo_part).astype(F32)
    query_grad, output_grad = qo_grad[:, :units], qo_grad[:, units:].T

    key_weighted, key_inner, key_gain_part = unrotate(
        [own_a, own_b], k_raw, key_rms, key_scale, cosine, sine, heads, False
    )
    key_inner, key_gain_sum = slot_sum(
        key_inner.reshape(nf, rows), nf, spread(unit_full(key_gain_part[0]))
    )
    key_grads = norm_grads(key_weighted, key_inner, k_raw, key_rms)
    own = jnp.concatenate([own_a[:, units:], own_b[:, units:]])
    value_grads = [rows_of(own, s) for s in range(nf)]

    started = []
    input_grad = state_grad + ring_scatter(
        lambda s: contract_cols(query_grads[s], query_weight)
        + contract_cols(key_grads[s], key_weight)
        + contract_cols(value_grads[s], value_weight),
        nf,
        started=started,
    )
    k_rows, v_rows, *_ = lax.optimization_barrier((jnp.concatenate(key_grads), own, *started))
    k_part = contract_rows(x_rows, k_rows).astype(BF)
    v_part = contract_rows(x_rows, v_rows).astype(BF)
    key_grad = halving(k_part, me_c, nc, orders[0])
    value_grad = halving(v_part, me_c, nc, orders[1], (gate_up_sum,))
    gains = jnp.concatenate([gathered(early_gains, 3), gathered(key_gain_sum, 1)])
    gains_own = halving(gains.T, me_c, nc, orders[0]).T
    down_grad = down_sum.astype(F32).T
    ff = gate_weight.shape[1]
    gate_up = gate_up_sum.astype(F32)
    gate_grad, up_grad = gate_up[:, :ff], gate_up[:, ff:]
    return (
        block_output,
        input_grad,
        query_grad,
        key_grad,
        value_grad,
        output_grad,
        gains_own[0],
        gains_own[3],
        gains_own[1],
        gains_own[2],
        gate_grad,
        up_grad,
        down_grad,
    )


def solution(mesh):
    def layer(*args):
        return local(mesh.shape["ctx"], mesh.shape["fsdp"], *args)

    return jax.shard_map(
        layer,
        mesh=mesh,
        in_specs=(
            P(("ctx", "fsdp"), None),
            P(("ctx", "fsdp")),
            P(None, "fsdp"),
            P(None, "fsdp"),
            P(None, "fsdp"),
            P("fsdp", None),
            P(),
            P(),
            P(),
            P(),
            P(None, "fsdp"),
            P(None, "fsdp"),
            P("fsdp", None),
            P(("ctx", "fsdp"), None),
        ),
        out_specs=(
            P(("ctx", "fsdp"), None),
            P(("ctx", "fsdp"), None),
            P("ctx", "fsdp"),
            P("ctx", "fsdp"),
            P("ctx", "fsdp"),
            P("fsdp", "ctx"),
            P("ctx"),
            P("ctx"),
            P("ctx"),
            P("ctx"),
            P("ctx", "fsdp"),
            P("ctx", "fsdp"),
            P("fsdp", "ctx"),
        ),
        check_vma=False,
    )
```

profile of v0, /device:TPU:0, one launch (start us, length us, event | category | flops | bytes accessed | tf_op | source)
XLA Modules:
  0.0 662.4 jit_solution(15816054912487820729)
XLA Ops:
  18.4 6.1 collective-permute-done
  48.1 10.2 %collective-permute-done.2 = bf16[128,2048]{1,0:T(8,128)(2,1)S(1)} collective-permute-done((bf16[128,2048]{1,0:T(8,128)(2,1)S(1)}, bf16[128,2048]{1,0:T(8,128)(2,1)S(1)}, u32[]{:S(2)}, u32[]{:S(2)}) %collective-permute-start.2) | collective-permute-done | bytes 524320 | tf_op jit(solution)/shard_map/ppermute | solution.py:38
  70.9 5.9 shard_map.237
  81.7 10.4 %collective-permute-done.12.refs_3_.refs_7_.refs_6_.refs_10_ = bf16[256,1024]{1,0:T(8,128)(2,1)} collective-permute-done((bf16[256,1024]{1,0:T(8,128)(2,1)}, bf16[256,1024]{1,0:T(8,128)(2,1)}, u32[]{:S(2)}, u32[]{:S(2)}) %collective-permute-start.12) | collective-permute-done | bytes 524320 | tf_op jit(solution)/shard_map/ppermute | solution.py:72
  92.1 10.7 %collective-permute-done.17.refs_5_.refs_9_.refs_8_.refs_12_ = bf16[256,1024]{1,0:T(8,128)(2,1)} collective-permute-done((bf16[256,1024]{1,0:T(8,128)(2,1)}, bf16[256,1024]{1,0:T(8,128)(2,1)}, u32[]{:S(2)}, u32[]{:S(2)}) %collective-permute-start.17) | collective-permute-done | bytes 524320 | tf_op jit(solution)/shard_map/ppermute | solution.py:72
  102.8 6.9 %shard_map.238 = (f32[4,1,512]{2,1,0:T(1,128)}, f32[4,1,512]{2,1,0:T(1,128)}, f32[512,512]{1,0:T(8,128)}) custom-call(s32[8]{0:T(128)} %pad_add_fusion.4.refs_0_, bf16[512,512]{1,0:T(8,128)(2,1)} %get-tuple-element.86.refs_1_, s32[1,512]{1,0:T(1,128)} %bitcast.295, bf16[256,1024]{1,0:T(8,128)(2,1)} %get-tuple-element.87.refs_3_.refs_7_.refs_6_.refs_10_, ...), custom_call_target="tpu_custom_call" | custom-call | flops 2147483648 | bytes 2097152 | tf_op jit(solution)/shard_map/pallas_call | solution.py:234
  113.9 7.3 %shard_map.239 = (f32[4,1,512]{2,1,0:T(1,128)}, f32[4,1,512]{2,1,0:T(1,128)}, f32[512,512]{1,0:T(8,128)}) custom-call(s32[8]{0:T(128)} %pad_add_fusion.5.refs_0_, bf16[512,512]{1,0:T(8,128)(2,1)} %get-tuple-element.86.refs_1_, s32[1,512]{1,0:T(1,128)} %bitcast.296, bf16[256,1024]{1,0:T(8,128)(2,1)} %collective-permute-done.12.refs_3_.refs_7_.refs_6_.refs_10_, ...), custom_call_target="tpu_custom_call" | custom-call | flops 2147483648 | bytes 2097152 | tf_op jit(solution)/shard_map/pallas_call | solution.py:234
  127.6 7.2 %shard_map.240 = (f32[4,1,512]{2,1,0:T(1,128)}, f32[4,1,512]{2,1,0:T(1,128)}, f32[512,512]{1,0:T(8,128)}) custom-call(s32[8]{0:T(128)} %pad_add_fusion.6.refs_0_, bf16[512,512]{1,0:T(8,128)(2,1)} %get-tuple-element.86.refs_1_, s32[1,512]{1,0:T(1,128)} %bitcast.297, bf16[256,1024]{1,0:T(8,128)(2,1)} %collective-permute-done.23.refs_3_.refs_7_.refs_6_.refs_10_, ...), custom_call_target="tpu_custom_call" | custom-call | flops 2147483648 | bytes 2097152 | tf_op jit(solution)/shard_map/pallas_call | solution.py:234
  134.9 7.5 %shard_map.241 = (f32[512,512]{1,0:T(8,128)}, bf16[512,512]{1,0:T(8,128)(2,1)}, f32[4,1,512]{2,1,0:T(1,128)}) custom-call(s32[8]{0:T(128)} %pad_add_fusion.3.refs_0_, bf16[512,512]{1,0:T(8,128)(2,1)} %get-tuple-element.86.refs_1_, s32[1,512]{1,0:T(1,128)} %bitcast.298, bf16[256,1024]{1,0:T(8,128)(2,1)} %collective-permute-done.15.refs_3_.refs_7_.refs_6_.refs_10_, ...), custom_call_target="tpu_custom_call" | custom-call | flops 2147483648 | bytes 2097152 | tf_op jit(solution)/shard_map/pallas_call | solution.py:234
  144.7 16.1 %collective-permute-done.26 = bf16[128,2048]{1,0:T(8,128)(2,1)S(1)} collective-permute-done((bf16[128,2048]{1,0:T(8,128)(2,1)S(1)}, bf16[128,2048]{1,0:T(8,128)(2,1)S(1)}, u32[]{:S(2)}, u32[]{:S(2)}) %collective-permute-start.26) | collective-permute-done | bytes 524320 | tf_op jit(solution)/shard_map/ppermute | solution.py:38
  161.4 15.3 %collective-permute-done.27 = bf16[128,2048]{1,0:T(8,128)(2,1)S(1)} collective-permute-done((bf16[128,2048]{1,0:T(8,128)(2,1)S(1)}, bf16[128,2048]{1,0:T(8,128)(2,1)S(1)}, u32[]{:S(2)}, u32[]{:S(2)}) %collective-permute-start.27) | collective-permute-done | bytes 524320 | tf_op jit(solution)/shard_map/ppermute | solution.py:38
  177.2 14.4 %collective-permute-done.28 = bf16[128,2048]{1,0:T(8,128)(2,1)S(1)} collective-permute-done((bf16[128,2048]{1,0:T(8,128)(2,1)S(1)}, bf16[128,2048]{1,0:T(8,128)(2,1)S(1)}, u32[]{:S(2)}, u32[]{:S(2)}) %collective-permute-start.28) | collective-permute-done | bytes 524320 | tf_op jit(solution)/shard_map/ppermute | solution.py:38
  194.4 12.2 %collective-permute-done.29 = bf16[128,2048]{1,0:T(8,128)(2,1)S(1)} collective-permute-done((bf16[128,2048]{1,0:T(8,128)(2,1)S(1)}, bf16[128,2048]{1,0:T(8,128)(2,1)S(1)}, u32[]{:S(2)}, u32[]{:S(2)}) %collective-permute-start.29) | collective-permute-done | bytes 524320 | tf_op jit(solution)/shard_map/ppermute | solution.py:38
  211.9 11.4 %collective-permute-done.31 = bf16[128,2048]{1,0:T(8,128)(2,1)S(1)} collective-permute-done((bf16[128,2048]{1,0:T(8,128)(2,1)S(1)}, bf16[128,2048]{1,0:T(8,128)(2,1)S(1)}, u32[]{:S(2)}, u32[]{:S(2)}) %collective-permute-start.31) | collective-permute-done | bytes 524320 | tf_op jit(solution)/shard_map/ppermute | solution.py:38
  226.9 7.5 %collective-permute-done.30 = bf16[128,2048]{1,0:T(8,128)(2,1)S(1)} collective-permute-done((bf16[128,2048]{1,0:T(8,128)(2,1)S(1)}, bf16[128,2048]{1,0:T(8,128)(2,1)S(1)}, u32[]{:S(2)}, u32[]{:S(2)}) %collective-permute-start.30) | collective-permute-done | bytes 524320 | tf_op jit(solution)/shard_map/ppermute | solution.py:38
  236.0 9.7 %collective-permute-done.33 = bf16[128,2048]{1,0:T(8,128)(2,1)S(1)} collective-permute-done((bf16[128,2048]{1,0:T(8,128)(2,1)S(1)}, bf16[128,2048]{1,0:T(8,128)(2,1)S(1)}, u32[]{:S(2)}, u32[]{:S(2)}) %collective-permute-start.33) | collective-permute-done | bytes 524320 | tf_op jit(solution)/shard_map/ppermute | solution.py:38
  255.7 9.4 %collective-permute-done.34 = bf16[128,2048]{1,0:T(8,128)(2,1)S(1)} collective-permute-done((bf16[128,2048]{1,0:T(8,128)(2,1)S(1)}, bf16[128,2048]{1,0:T(8,128)(2,1)S(1)}, u32[]{:S(2)}, u32[]{:S(2)}) %collective-permute-start.34) | collective-permute-done | bytes 524320 | tf_op jit(solution)/shard_map/ppermute | solution.py:38
  268.4 4.1 multiply_convert_fusion.6
  272.5 7.7 %collective-permute-done.35 = bf16[128,2048]{1,0:T(8,128)(2,1)S(1)} collective-permute-done((bf16[128,2048]{1,0:T(8,128)(2,1)S(1)}, bf16[128,2048]{1,0:T(8,128)(2,1)S(1)}, u32[]{:S(2)}, u32[]{:S(2)}) %collective-permute-start.35) | collective-permute-done | bytes 524320 | tf_op jit(solution)/shard_map/ppermute | solution.py:38
  280.5 4.0 multiply_convert_fusion.4
  284.5 9.1 %collective-permute-done.37 = bf16[128,2048]{1,0:T(8,128)(2,1)S(1)} collective-permute-done((bf16[128,2048]{1,0:T(8,128)(2,1)S(1)}, bf16[128,2048]{1,0:T(8,128)(2,1)S(1)}, u32[]{:S(2)}, u32[]{:S(2)}) %collective-permute-start.37) | collective-permute-done | bytes 524320 | tf_op jit(solution)/shard_map/ppermute | solution.py:38
  293.6 4.1 multiply_convert_fusion.2
  297.7 6.9 %collective-permute-done.39 = bf16[128,2048]{1,0:T(8,128)(2,1)S(1)} collective-permute-done((bf16[128,2048]{1,0:T(8,128)(2,1)S(1)}, bf16[128,2048]{1,0:T(8,128)(2,1)S(1)}, u32[]{:S(2)}, u32[]{:S(2)}) %collective-permute-start.39) | collective-permute-done | bytes 524320 | tf_op jit(solution)/shard_map/ppermute | solution.py:38
  305.4 6.8 %convolution_convert_fusion.1 = bf16[2048,2048]{1,0:T(8,128)(2,1)} fusion(bf16[128,2048]{1,0:T(8,128)(2,1)S(1)} %collective-permute-done.39, bf16[128,2048]{1,0:T(8,128)(2,1)S(1)} %collective-permute-done.37, bf16[128,2048]{1,0:T(8,128)(2,1)S(1)} %collective-permute-done.35, bf16[128,2048]{1,0:T(8,128)(2,1)S(1)} %get-tuple-element.212, ...), kind=kOutput, calls=%fused_computation.1 | convolution fusion | flops 4315938816 | bytes 12582912 | tf_op jit(solution)/shard_map/dot_general | solution.py:26
  312.6 8.8 %multiply_convert_fusion = (bf16[128,2048]{1,0:T(8,128)(2,1)}, bf16[128,2048]{1,0:T(8,128)(2,1)}) fusion(f32[128,2048]{1,0:T(8,128)} %copy-done.48, f32[128,2048]{1,0:T(8,128)} %get-tuple-element.308, bf16[128,2048]{1,0:T(8,128)(2,1)} %copy-done.82, bf16[2048,2048]{1,0:T(8,128)(2,1)} %param.26), kind=kOutput, calls=%fused_computation.108 | convolution fusion | flops 1077149696 | bytes 12058624 | tf_op jit(solution)/shard_map/dot_general | solution.py:30
  321.3 16.2 %convolution_convert_fusion = bf16[2048,4096]{1,0:T(8,128)(2,1)} fusion(bf16[128,2048]{1,0:T(8,128)(2,1)} %get-tuple-element.204, bf16[128,2048]{1,0:T(8,128)(2,1)} %get-tuple-element.148, bf16[128,2048]{1,0:T(8,128)(2,1)} %get-tuple-element.147, bf16[128,2048]{1,0:T(8,128)(2,1)} %get-tuple-element.107, bf16[128,2048]{1,0:T(8,128)(2,1)} %get-tuple-element.205, ...), kind=kOutput, calls=%fused_computation | convolution fusion | flops 8640266240 | bytes 23068672 | tf_op jit(solution)/shard_map/dot_general | solution.py:26
  337.6 6.6 fusion.137
  344.2 6.7 %fusion.15 = bf16[128,2048]{1,0:T(8,128)(2,1)S(1)} fusion(f32[128,2048]{1,0:T(8,128)S(1)} %fusion.137, bf16[128,2048]{1,0:T(8,128)(2,1)S(1)} %copy-done.57, bf16[2048,2048]{1,0:T(8,128)(2,1)} %param.25), kind=kOutput, calls=%fused_computation.35 | convolution fusion | flops 1074266112 | bytes 10485760 | tf_op jit(solution)/shard_map/dot_general | solution.py:30
  354.4 11.1 %collective-permute-done.36 = bf16[128,2048]{1,0:T(8,128)(2,1)S(1)} collective-permute-done((bf16[128,2048]{1,0:T(8,128)(2,1)S(1)}, bf16[128,2048]{1,0:T(8,128)(2,1)S(1)}, u32[]{:S(2)}, u32[]{:S(2)}) %collective-permute-start.36) | collective-permute-done | bytes 524320 | tf_op jit(solution)/shard_map/ppermute | solution.py:38
  374.3 9.6 %collective-permute-done.38 = bf16[128,2048]{1,0:T(8,128)(2,1)S(1)} collective-permute-done((bf16[128,2048]{1,0:T(8,128)(2,1)S(1)}, bf16[128,2048]{1,0:T(8,128)(2,1)S(1)}, u32[]{:S(2)}, u32[]{:S(2)}) %collective-permute-start.38) | collective-permute-done | bytes 524320 | tf_op jit(solution)/shard_map/ppermute | solution.py:38
  387.2 11.5 %collective-permute-done.40 = bf16[128,2048]{1,0:T(8,128)(2,1)S(1)} collective-permute-done((bf16[128,2048]{1,0:T(8,128)(2,1)S(1)}, bf16[128,2048]{1,0:T(8,128)(2,1)S(1)}, u32[]{:S(2)}, u32[]{:S(2)}) %collective-permute-start.40) | collective-permute-done | bytes 524320 | tf_op jit(solution)/shard_map/ppermute | solution.py:38
  407.2 9.5 %collective-permute-done.41 = bf16[128,2048]{1,0:T(8,128)(2,1)} collective-permute-done((bf16[128,2048]{1,0:T(8,128)(2,1)}, bf16[128,2048]{1,0:T(8,128)(2,1)}, u32[]{:S(2)}, u32[]{:S(2)}) %collective-permute-start.41) | collective-permute-done | bytes 524320 | tf_op jit(solution)/shard_map/ppermute | solution.py:38
  419.5 9.7 %collective-permute-done.42 = bf16[128,2048]{1,0:T(8,128)(2,1)S(1)} collective-permute-done((bf16[128,2048]{1,0:T(8,128)(2,1)}, bf16[128,2048]{1,0:T(8,128)(2,1)S(1)}, u32[]{:S(2)}, u32[]{:S(2)}) %collective-permute-start.42) | collective-permute-done | bytes 524320 | tf_op jit(solution)/shard_map/ppermute | solution.py:38
  432.2 8.0 %collective-permute-done.43 = bf16[128,2048]{1,0:T(8,128)(2,1)S(1)} collective-permute-done((bf16[128,2048]{1,0:T(8,128)(2,1)S(1)}, bf16[128,2048]{1,0:T(8,128)(2,1)S(1)}, u32[]{:S(2)}, u32[]{:S(2)}) %collective-permute-start.43) | collective-permute-done | bytes 524320 | tf_op jit(solution)/shard_map/ppermute | solution.py:38
  441.9 10.4 %shard_map.242 = (f32[512,512]{1,0:T(8,128)}, bf16[256,1024]{1,0:T(8,128)(2,1)}, bf16[256,1024]{1,0:T(8,128)(2,1)}, bf16[256,1024]{1,0:T(8,128)(2,1)}, bf16[256,1024]{1,0:T(8,128)(2,1)}) custom-call(s32[8]{0:T(128)} %pad_add_fusion.3.refs_0_, bf16[512,512]{1,0:T(8,128)(2,1)} %get-tuple-element.86.refs_1_, bf16[512,512]{1,0:T(8,128)(2,1)} %pad_maximum_fusion.3.refs_2_, ...), custom_call_target="tpu_custom_call" | custom-call | flops 5368709120 | bytes 4194304 | tf_op jit(solution)/shard_map/pallas_call | solution.py:306
  455.3 10.6 %shard_map.243 = (f32[512,512]{1,0:T(8,128)}, bf16[256,1024]{1,0:T(8,128)(2,1)}, bf16[256,1024]{1,0:T(8,128)(2,1)}, bf16[256,1024]{1,0:T(8,128)(2,1)}, bf16[256,1024]{1,0:T(8,128)(2,1)}) custom-call(s32[8]{0:T(128)} %pad_add_fusion.6.refs_0_, bf16[512,512]{1,0:T(8,128)(2,1)} %get-tuple-element.86.refs_1_, bf16[512,512]{1,0:T(8,128)(2,1)} %pad_maximum_fusion.3.refs_2_, ...), custom_call_target="tpu_custom_call" | custom-call | flops 5368709120 | bytes 4194304 | tf_op jit(solution)/shard_map/pallas_call | solution.py:306
  466.5 4.3 convolution_convert_fusion.4
  473.9 10.9 %shard_map.244 = (f32[512,512]{1,0:T(8,128)}, bf16[256,1024]{1,0:T(8,128)(2,1)}, bf16[256,1024]{1,0:T(8,128)(2,1)}, bf16[256,1024]{1,0:T(8,128)(2,1)}, bf16[256,1024]{1,0:T(8,128)(2,1)}) custom-call(s32[8]{0:T(128)} %pad_add_fusion.5.refs_0_, bf16[512,512]{1,0:T(8,128)(2,1)} %get-tuple-element.86.refs_1_, bf16[512,512]{1,0:T(8,128)(2,1)} %pad_maximum_fusion.3.refs_2_, ...), custom_call_target="tpu_custom_call" | custom-call | flops 5368709120 | bytes 4194304 | tf_op jit(solution)/shard_map/pallas_call | solution.py:306
  491.3 5.5 collective-permute-done.56
  502.0 10.7 %shard_map.245 = (f32[512,512]{1,0:T(8,128)}, bf16[256,1024]{1,0:T(8,128)(2,1)}, bf16[256,1024]{1,0:T(8,128)(2,1)}, bf16[256,1024]{1,0:T(8,128)(2,1)}, bf16[256,1024]{1,0:T(8,128)(2,1)}) custom-call(s32[8]{0:T(128)} %pad_add_fusion.4.refs_0_, bf16[512,512]{1,0:T(8,128)(2,1)} %get-tuple-element.86.refs_1_, bf16[512,512]{1,0:T(8,128)(2,1)} %pad_maximum_fusion.3.refs_2_, ...), custom_call_target="tpu_custom_call" | custom-call | flops 5368709120 | bytes 4194304 | tf_op jit(solution)/shard_map/pallas_call | solution.py:306
  518.2 14.9 %collective-permute-done.51 = bf16[256,1024]{1,0:T(8,128)(2,1)S(1)} collective-permute-done((bf16[256,1024]{1,0:T(8,128)(2,1)}, bf16[256,1024]{1,0:T(8,128)(2,1)S(1)}, u32[]{:S(2)}, u32[]{:S(2)}) %collective-permute-start.51) | collective-permute-done | bytes 524320 | tf_op jit(solution)/shard_map/ppermute | solution.py:72
  533.1 5.1 shard_map.246
  540.2 3.4 collective-permute-start.54
  561.3 4.7 shard_map.247
  601.0 11.7 %collective-permute-done.65 = bf16[128,2048]{1,0:T(8,128)(2,1)S(1)} collective-permute-done((bf16[128,2048]{1,0:T(8,128)(2,1)S(1)}, bf16[128,2048]{1,0:T(8,128)(2,1)S(1)}, u32[]{:S(2)}, u32[]{:S(2)}) %collective-permute-start.65) | collective-permute-done | bytes 524320 | tf_op jit(solution)/shard_map/ppermute | solution.py:38
  614.1 5.9 collective-permute-done.68
  622.3 5.8 collective-permute-done.66
  650.3 4.5 collective-permute-done.72
  (509 shorter events, 229.7 us)
Async XLA Ops:
  7.2 554.1 %reduce-scatter.4.cloned.1.call-start = ((), (), s32[]{:S(2)}) async-start(), calls=%async_computation.3 | async-start | bytes 9437184 | tf_op jit(solution)/shard_map/reduce_scatter | solution.py:509
  7.3 17.3 %collective-permute-start = (bf16[128,2048]{1,0:T(8,128)(2,1)}, bf16[128,2048]{1,0:T(8,128)(2,1)S(1)}, u32[]{:S(2)}, u32[]{:S(2)}) collective-permute-start(bf16[128,2048]{1,0:T(8,128)(2,1)} %param.14), channel_id=1, source_target_pairs={{0,1},{1,2},{2,3},{3,0},{4,5},{5,6},{6,7},{7,4},{8,9},{9,10},{10,1... | collective-permute-start | bytes 1572872 | tf_op jit(solution)/shard_map/ppermute | solution.py:38
  30.2 13.8 %collective-permute-start.1 = (bf16[128,2048]{1,0:T(8,128)(2,1)S(1)}, bf16[128,2048]{1,0:T(8,128)(2,1)S(1)}, u32[]{:S(2)}, u32[]{:S(2)}) collective-permute-start(bf16[128,2048]{1,0:T(8,128)(2,1)S(1)} %collective-permute-done), channel_id=1, source_target_pairs={{0,1},{1,2},{2,3},{3,0},{4,5},{5,6},{6,7},{7,4},{8,9},{9,10},{10,1... | collective-permute-start | bytes 1572872 | tf_op jit(solution)/shard_map/ppermute | solution.py:38
  45.2 13.1 %collective-permute-start.2 = (bf16[128,2048]{1,0:T(8,128)(2,1)S(1)}, bf16[128,2048]{1,0:T(8,128)(2,1)S(1)}, u32[]{:S(2)}, u32[]{:S(2)}) collective-permute-start(bf16[128,2048]{1,0:T(8,128)(2,1)S(1)} %collective-permute-done.1), channel_id=1, source_target_pairs={{0,1},{1,2},{2,3},{3,0},{4,5},{5,6},{6,7},{7,4},{8,9},{9,10},{10,1... | collective-permute-start | bytes 1572872 | tf_op jit(solution)/shard_map/ppermute | solution.py:38
  76.9 15.2 %collective-permute-start.12 = (bf16[256,1024]{1,0:T(8,128)(2,1)}, bf16[256,1024]{1,0:T(8,128)(2,1)}, u32[]{:S(2)}, u32[]{:S(2)}) collective-permute-start(bf16[256,1024]{1,0:T(8,128)(2,1)} %get-tuple-element.87.refs_3_.refs_7_.refs_6_.refs_10_), channel_id=1, source_target_pairs={{0,8},{4,12},{8,0},{12,4},{16,24},{20,28},{24,16},{28,20},{1,9},{5... | collective-permute-start | bytes 1572872 | tf_op jit(solution)/shard_map/ppermute | solution.py:72
  78.5 24.3 %collective-permute-start.17 = (bf16[256,1024]{1,0:T(8,128)(2,1)}, bf16[256,1024]{1,0:T(8,128)(2,1)}, u32[]{:S(2)}, u32[]{:S(2)}) collective-permute-start(bf16[256,1024]{1,0:T(8,128)(2,1)} %get-tuple-element.88.refs_5_.refs_9_.refs_8_.refs_12_), channel_id=1, source_target_pairs={{0,8},{4,12},{8,0},{12,4},{16,24},{20,28},{24,16},{28,20},{1,9},{5... | collective-permute-start | bytes 1572872 | tf_op jit(solution)/shard_map/ppermute | solution.py:72
  79.0 23.8 %collective-permute-start.14 = (bf16[256,1024]{1,0:T(8,128)(2,1)}, bf16[256,1024]{1,0:T(8,128)(2,1)}, u32[]{:S(2)}, u32[]{:S(2)}) collective-permute-start(bf16[256,1024]{1,0:T(8,128)(2,1)} %get-tuple-element.88.refs_5_.refs_9_.refs_8_.refs_12_), channel_id=1, source_target_pairs={{0,4},{4,0},{8,12},{12,8},{16,20},{20,16},{24,28},{28,24},{1,5},{5... | collective-permute-start | bytes 1572872 | tf_op jit(solution)/shard_map/ppermute | solution.py:72
  79.0 32.3 %collective-permute-start.20 = (bf16[256,1024]{1,0:T(8,128)(2,1)}, bf16[256,1024]{1,0:T(8,128)(2,1)}, u32[]{:S(2)}, u32[]{:S(2)}) collective-permute-start(bf16[256,1024]{1,0:T(8,128)(2,1)} %get-tuple-element.88.refs_5_.refs_9_.refs_8_.refs_12_), channel_id=1, source_target_pairs={{0,16},{4,20},{8,24},{12,28},{16,0},{20,4},{24,8},{28,12},{1,17},{... | collective-permute-start | bytes 1572872 | tf_op jit(solution)/shard_map/ppermute | solution.py:72
  81.2 32.2 %collective-permute-start.23 = (bf16[256,1024]{1,0:T(8,128)(2,1)}, bf16[256,1024]{1,0:T(8,128)(2,1)}, u32[]{:S(2)}, u32[]{:S(2)}) collective-permute-start(bf16[256,1024]{1,0:T(8,128)(2,1)} %get-tuple-element.87.refs_3_.refs_7_.refs_6_.refs_10_), channel_id=1, source_target_pairs={{0,16},{4,20},{8,24},{12,28},{16,0},{20,4},{24,8},{28,12},{1,17},{... | collective-permute-start | bytes 1572872 | tf_op jit(solution)/shard_map/ppermute | solution.py:72
  92.1 21.3 %collective-permute-start.16 = (bf16[256,1024]{1,0:T(8,128)(2,1)}, bf16[256,1024]{1,0:T(8,128)(2,1)}, u32[]{:S(2)}, u32[]{:S(2)}) collective-permute-start(bf16[256,1024]{1,0:T(8,128)(2,1)} %collective-permute-done.12.refs_3_.refs_7_.refs_6_.refs_10_), channel_id=1, source_target_pairs={{0,4},{4,0},{8,12},{12,8},{16,20},{20,16},{24,28},{28,24},{1,5},{5... | collective-permute-start | bytes 1572872 | tf_op jit(solution)/shard_map/ppermute | solution.py:72
  109.7 14.7 %collective-permute-start.15 = (bf16[256,1024]{1,0:T(8,128)(2,1)}, bf16[256,1024]{1,0:T(8,128)(2,1)}, u32[]{:S(2)}, u32[]{:S(2)}) collective-permute-start(bf16[256,1024]{1,0:T(8,128)(2,1)} %collective-permute-done.12.refs_3_.refs_7_.refs_6_.refs_10_), channel_id=1, source_target_pairs={{0,16},{4,20},{8,24},{12,28},{16,0},{20,4},{24,8},{28,12},{1,17},{... | collective-permute-start | bytes 1572872 | tf_op jit(solution)/shard_map/ppermute | solution.py:72
  111.3 14.3 %collective-permute-start.21 = (bf16[256,1024]{1,0:T(8,128)(2,1)}, bf16[256,1024]{1,0:T(8,128)(2,1)}, u32[]{:S(2)}, u32[]{:S(2)}) collective-permute-start(bf16[256,1024]{1,0:T(8,128)(2,1)} %collective-permute-done.20.refs_5_.refs_9_.refs_8_.refs_12_), channel_id=1, source_target_pairs={{0,8},{4,12},{8,0},{12,4},{16,24},{20,28},{24,16},{28,20},{1,9},{5... | collective-permute-start | bytes 1572872 | tf_op jit(solution)/shard_map/ppermute | solution.py:72
  113.4 13.4 %collective-permute-start.25 = (bf16[256,1024]{1,0:T(8,128)(2,1)}, bf16[256,1024]{1,0:T(8,128)(2,1)S(1)}, u32[]{:S(2)}, u32[]{:S(2)}) collective-permute-start(bf16[256,1024]{1,0:T(8,128)(2,1)} %collective-permute-done.20.refs_5_.refs_9_.refs_8_.refs_12_), channel_id=1, source_target_pairs={{0,4},{4,0},{8,12},{12,8},{16,20},{20,16},{24,28},{28,24},{1,5},{5... | collective-permute-start | bytes 1572872 | tf_op jit(solution)/shard_map/ppermute | solution.py:72
  113.4 13.4 %collective-permute-start.24 = (bf16[256,1024]{1,0:T(8,128)(2,1)}, bf16[256,1024]{1,0:T(8,128)(2,1)}, u32[]{:S(2)}, u32[]{:S(2)}) collective-permute-start(bf16[256,1024]{1,0:T(8,128)(2,1)} %collective-permute-done.23.refs_3_.refs_7_.refs_6_.refs_10_), channel_id=1, source_target_pairs={{0,4},{4,0},{8,12},{12,8},{16,20},{20,16},{24,28},{28,24},{1,5},{5... | collective-permute-start | bytes 1572872 | tf_op jit(solution)/shard_map/ppermute | solution.py:72
  144.7 16.2 %collective-permute-start.26 = (bf16[128,2048]{1,0:T(8,128)(2,1)S(1)}, bf16[128,2048]{1,0:T(8,128)(2,1)S(1)}, u32[]{:S(2)}, u32[]{:S(2)}) collective-permute-start(bf16[128,2048]{1,0:T(8,128)(2,1)S(1)} %convolution_convert_fusion.7), channel_id=1, source_target_pairs={{0,1},{1,2},{2,3},{3,0},{4,5},{5,6},{6,7},{7,4},{8,9},{9,10},{10,1... | collective-permute-start | bytes 1572872 | tf_op jit(solution)/shard_map/ppermute | solution.py:38
  161.3 15.3 %collective-permute-start.27 = (bf16[128,2048]{1,0:T(8,128)(2,1)S(1)}, bf16[128,2048]{1,0:T(8,128)(2,1)S(1)}, u32[]{:S(2)}, u32[]{:S(2)}) collective-permute-start(bf16[128,2048]{1,0:T(8,128)(2,1)S(1)} %add_convert_fusion.26), channel_id=1, source_target_pairs={{0,1},{1,2},{2,3},{3,0},{4,5},{5,6},{6,7},{7,4},{8,9},{9,10},{10,1... | collective-permute-start | bytes 1572872 | tf_op jit(solution)/shard_map/ppermute | solution.py:38
  177.2 14.5 %collective-permute-start.28 = (bf16[128,2048]{1,0:T(8,128)(2,1)S(1)}, bf16[128,2048]{1,0:T(8,128)(2,1)S(1)}, u32[]{:S(2)}, u32[]{:S(2)}) collective-permute-start(bf16[128,2048]{1,0:T(8,128)(2,1)S(1)} %add_convert_fusion.25), channel_id=1, source_target_pairs={{0,1},{1,2},{2,3},{3,0},{4,5},{5,6},{6,7},{7,4},{8,9},{9,10},{10,1... | collective-permute-start | bytes 1572872 | tf_op jit(solution)/shard_map/ppermute | solution.py:38
  192.5 14.2 %collective-permute-start.29 = (bf16[128,2048]{1,0:T(8,128)(2,1)S(1)}, bf16[128,2048]{1,0:T(8,128)(2,1)S(1)}, u32[]{:S(2)}, u32[]{:S(2)}) collective-permute-start(bf16[128,2048]{1,0:T(8,128)(2,1)S(1)} %fusion.52), channel_id=1, source_target_pairs={{0,1},{1,2},{2,3},{3,0},{4,5},{5,6},{6,7},{7,4},{8,9},{9,10},{10,1... | collective-permute-start | bytes 1572872 | tf_op jit(solution)/shard_map/ppermute | solution.py:38
  206.6 16.6 %collective-permute-start.31 = (bf16[128,2048]{1,0:T(8,128)(2,1)S(1)}, bf16[128,2048]{1,0:T(8,128)(2,1)S(1)}, u32[]{:S(2)}, u32[]{:S(2)}) collective-permute-start(bf16[128,2048]{1,0:T(8,128)(2,1)S(1)} %collective-permute-done.29), channel_id=1, source_target_pairs={{0,1},{1,2},{2,3},{3,0},{4,5},{5,6},{6,7},{7,4},{8,9},{9,10},{10,1... | collective-permute-start | bytes 1572872 | tf_op jit(solution)/shard_map/ppermute | solution.py:38
  211.8 22.7 %collective-permute-start.30 = (bf16[128,2048]{1,0:T(8,128)(2,1)S(1)}, bf16[128,2048]{1,0:T(8,128)(2,1)S(1)}, u32[]{:S(2)}, u32[]{:S(2)}) collective-permute-start(bf16[128,2048]{1,0:T(8,128)(2,1)S(1)} %convolution_convert_fusion.6), channel_id=1, source_target_pairs={{0,1},{1,2},{2,3},{3,0},{4,5},{5,6},{6,7},{7,4},{8,9},{9,10},{10,1... | collective-permute-start | bytes 1572872 | tf_op jit(solution)/shard_map/ppermute | solution.py:38
  223.2 22.5 %collective-permute-start.33 = (bf16[128,2048]{1,0:T(8,128)(2,1)S(1)}, bf16[128,2048]{1,0:T(8,128)(2,1)S(1)}, u32[]{:S(2)}, u32[]{:S(2)}) collective-permute-start(bf16[128,2048]{1,0:T(8,128)(2,1)S(1)} %collective-permute-done.31), channel_id=1, source_target_pairs={{0,1},{1,2},{2,3},{3,0},{4,5},{5,6},{6,7},{7,4},{8,9},{9,10},{10,1... | collective-permute-start | bytes 1572872 | tf_op jit(solution)/shard_map/ppermute | solution.py:38
  235.7 17.3 %collective-permute-start.32 = (bf16[128,2048]{1,0:T(8,128)(2,1)S(1)}, bf16[128,2048]{1,0:T(8,128)(2,1)S(1)}, u32[]{:S(2)}, u32[]{:S(2)}) collective-permute-start(bf16[128,2048]{1,0:T(8,128)(2,1)S(1)} %add_convert_fusion.24), channel_id=1, source_target_pairs={{0,1},{1,2},{2,3},{3,0},{4,5},{5,6},{6,7},{7,4},{8,9},{9,10},{10,1... | collective-permute-start | bytes 1572872 | tf_op jit(solution)/shard_map/ppermute | solution.py:38
  280.2 13.4 %collective-permute-start.37 = (bf16[128,2048]{1,0:T(8,128)(2,1)S(1)}, bf16[128,2048]{1,0:T(8,128)(2,1)S(1)}, u32[]{:S(2)}, u32[]{:S(2)}) collective-permute-start(bf16[128,2048]{1,0:T(8,128)(2,1)S(1)} %collective-permute-done.35), channel_id=1, source_target_pairs={{0,1},{1,2},{2,3},{3,0},{4,5},{5,6},{6,7},{7,4},{8,9},{9,10},{10,1... | collective-permute-start | bytes 1572872 | tf_op jit(solution)/shard_map/ppermute | solution.py:38
  312.3 315.9 %reduce-scatter.8.cloned.1.call-start = ((), (), s32[]{:S(2)}) async-start(), calls=%async_computation.5 | async-start | bytes 18874368 | tf_op jit(solution)/shard_map/reduce_scatter | solution.py:509
  337.5 300.2 %reduce-scatter.6.cloned.1.call-start = ((), (), s32[]{:S(2)}) async-start(), calls=%async_computation.4 | async-start | bytes 4718592 | tf_op jit(solution)/shard_map/reduce_scatter | solution.py:509
  350.9 14.5 %collective-permute-start.36 = (bf16[128,2048]{1,0:T(8,128)(2,1)S(1)}, bf16[128,2048]{1,0:T(8,128)(2,1)S(1)}, u32[]{:S(2)}, u32[]{:S(2)}) collective-permute-start(bf16[128,2048]{1,0:T(8,128)(2,1)S(1)} %fusion.15), channel_id=1, source_target_pairs={{0,1},{1,2},{2,3},{3,0},{4,5},{5,6},{6,7},{7,4},{8,9},{9,10},{10,1... | collective-permute-start | bytes 1572872 | tf_op jit(solution)/shard_map/ppermute | solution.py:38
  368.4 15.5 %collective-permute-start.38 = (bf16[128,2048]{1,0:T(8,128)(2,1)S(1)}, bf16[128,2048]{1,0:T(8,128)(2,1)S(1)}, u32[]{:S(2)}, u32[]{:S(2)}) collective-permute-start(bf16[128,2048]{1,0:T(8,128)(2,1)S(1)} %add_convert_fusion.21), channel_id=1, source_target_pairs={{0,1},{1,2},{2,3},{3,0},{4,5},{5,6},{6,7},{7,4},{8,9},{9,10},{10,1... | collective-permute-start | bytes 1572872 | tf_op jit(solution)/shard_map/ppermute | solution.py:38
  384.1 14.7 %collective-permute-start.40 = (bf16[128,2048]{1,0:T(8,128)(2,1)S(1)}, bf16[128,2048]{1,0:T(8,128)(2,1)S(1)}, u32[]{:S(2)}, u32[]{:S(2)}) collective-permute-start(bf16[128,2048]{1,0:T(8,128)(2,1)S(1)} %add_convert_fusion.20), channel_id=1, source_target_pairs={{0,1},{1,2},{2,3},{3,0},{4,5},{5,6},{6,7},{7,4},{8,9},{9,10},{10,1... | collective-permute-start | bytes 1572872 | tf_op jit(solution)/shard_map/ppermute | solution.py:38
  403.1 13.7 %collective-permute-start.41 = (bf16[128,2048]{1,0:T(8,128)(2,1)}, bf16[128,2048]{1,0:T(8,128)(2,1)}, u32[]{:S(2)}, u32[]{:S(2)}) collective-permute-start(bf16[128,2048]{1,0:T(8,128)(2,1)} %subtract_convert_fusion), channel_id=1, source_target_pairs={{0,1},{1,2},{2,3},{3,0},{4,5},{5,6},{6,7},{7,4},{8,9},{9,10},{10,1... | collective-permute-start | bytes 1572872 | tf_op jit(solution)/shard_map/ppermute | solution.py:38
  416.7 12.5 %collective-permute-start.42 = (bf16[128,2048]{1,0:T(8,128)(2,1)}, bf16[128,2048]{1,0:T(8,128)(2,1)S(1)}, u32[]{:S(2)}, u32[]{:S(2)}) collective-permute-start(bf16[128,2048]{1,0:T(8,128)(2,1)} %collective-permute-done.41), channel_id=1, source_target_pairs={{0,1},{1,2},{2,3},{3,0},{4,5},{5,6},{6,7},{7,4},{8,9},{9,10},{10,1... | collective-permute-start | bytes 1572872 | tf_op jit(solution)/shard_map/ppermute | solution.py:38
  471.8 24.9 %collective-permute-start.56 = (bf16[256,1024]{1,0:T(8,128)(2,1)}, bf16[256,1024]{1,0:T(8,128)(2,1)}, u32[]{:S(2)}, u32[]{:S(2)}) collective-permute-start(bf16[256,1024]{1,0:T(8,128)(2,1)} %add_convert_fusion.14), channel_id=1, source_target_pairs={{0,16},{4,20},{8,24},{12,28},{16,0},{20,4},{24,8},{28,12},{1,17},{... | collective-permute-start | bytes 1572872 | tf_op jit(solution)/shard_map/ppermute | solution.py:72
  484.7 12.0 %collective-permute-start.48 = (bf16[256,1024]{1,0:T(8,128)(2,1)}, bf16[256,1024]{1,0:T(8,128)(2,1)S(1)}, u32[]{:S(2)}, u32[]{:S(2)}) collective-permute-start(bf16[256,1024]{1,0:T(8,128)(2,1)} %get-tuple-element.119), channel_id=1, source_target_pairs={{0,4},{4,0},{8,12},{12,8},{16,20},{20,16},{24,28},{28,24},{1,5},{5... | collective-permute-start | bytes 1572872 | tf_op jit(solution)/shard_map/ppermute | solution.py:72
  485.8 27.0 %collective-permute-start.59 = (bf16[256,1024]{1,0:T(8,128)(2,1)}, bf16[256,1024]{1,0:T(8,128)(2,1)}, u32[]{:S(2)}, u32[]{:S(2)}) collective-permute-start(bf16[256,1024]{1,0:T(8,128)(2,1)} %add_convert_fusion.9), channel_id=1, source_target_pairs={{0,8},{4,12},{8,0},{12,4},{16,24},{20,28},{24,16},{28,20},{1,9},{5... | collective-permute-start | bytes 1572872 | tf_op jit(solution)/shard_map/ppermute | solution.py:72
  487.0 13.6 %collective-permute-start.49 = (bf16[256,1024]{1,0:T(8,128)(2,1)}, bf16[256,1024]{1,0:T(8,128)(2,1)S(1)}, u32[]{:S(2)}, u32[]{:S(2)}) collective-permute-start(bf16[256,1024]{1,0:T(8,128)(2,1)} %get-tuple-element.120), channel_id=1, source_target_pairs={{0,4},{4,0},{8,12},{12,8},{16,20},{20,16},{24,28},{28,24},{1,5},{5... | collective-permute-start | bytes 1572872 | tf_op jit(solution)/shard_map/ppermute | solution.py:72
  489.4 28.8 %collective-permute-start.50 = (bf16[256,1024]{1,0:T(8,128)(2,1)}, bf16[256,1024]{1,0:T(8,128)(2,1)S(1)}, u32[]{:S(2)}, u32[]{:S(2)}) collective-permute-start(bf16[256,1024]{1,0:T(8,128)(2,1)} %add_convert_fusion.19), channel_id=1, source_target_pairs={{0,16},{4,20},{8,24},{12,28},{16,0},{20,4},{24,8},{28,12},{1,17},{... | collective-permute-start | bytes 1572872 | tf_op jit(solution)/shard_map/ppermute | solution.py:72
  498.9 44.7 %collective-permute-start.57 = (bf16[256,1024]{1,0:T(8,128)(2,1)}, bf16[256,1024]{1,0:T(8,128)(2,1)}, u32[]{:S(2)}, u32[]{:S(2)}) collective-permute-start(bf16[256,1024]{1,0:T(8,128)(2,1)} %add_convert_fusion.13), channel_id=1, source_target_pairs={{0,8},{4,12},{8,0},{12,4},{16,24},{20,28},{24,16},{28,20},{1,9},{5... | collective-permute-start | bytes 1572872 | tf_op jit(solution)/shard_map/ppermute | solution.py:72
  501.6 31.5 %collective-permute-start.51 = (bf16[256,1024]{1,0:T(8,128)(2,1)}, bf16[256,1024]{1,0:T(8,128)(2,1)S(1)}, u32[]{:S(2)}, u32[]{:S(2)}) collective-permute-start(bf16[256,1024]{1,0:T(8,128)(2,1)} %add_convert_fusion.18), channel_id=1, source_target_pairs={{0,8},{4,12},{8,0},{12,4},{16,24},{20,28},{24,16},{28,20},{1,9},{5... | collective-permute-start | bytes 1572872 | tf_op jit(solution)/shard_map/ppermute | solution.py:72
  512.7 30.9 %collective-permute-start.55 = (bf16[256,1024]{1,0:T(8,128)(2,1)}, bf16[256,1024]{1,0:T(8,128)(2,1)}, u32[]{:S(2)}, u32[]{:S(2)}) collective-permute-start(bf16[256,1024]{1,0:T(8,128)(2,1)} %get-tuple-element.130), channel_id=1, source_target_pairs={{0,4},{4,0},{8,12},{12,8},{16,20},{20,16},{24,28},{28,24},{1,5},{5... | collective-permute-start | bytes 1572872 | tf_op jit(solution)/shard_map/ppermute | solution.py:72
  515.2 31.4 %collective-permute-start.60 = (bf16[256,1024]{1,0:T(8,128)(2,1)}, bf16[256,1024]{1,0:T(8,128)(2,1)}, u32[]{:S(2)}, u32[]{:S(2)}) collective-permute-start(bf16[256,1024]{1,0:T(8,128)(2,1)} %add_convert_fusion.8), channel_id=1, source_target_pairs={{0,16},{4,20},{8,24},{12,28},{16,0},{20,4},{24,8},{28,12},{1,17},{... | collective-permute-start | bytes 1572872 | tf_op jit(solution)/shard_map/ppermute | solution.py:72
  518.2 28.4 %collective-permute-start.58 = (bf16[256,1024]{1,0:T(8,128)(2,1)}, bf16[256,1024]{1,0:T(8,128)(2,1)}, u32[]{:S(2)}, u32[]{:S(2)}) collective-permute-start(bf16[256,1024]{1,0:T(8,128)(2,1)} %get-tuple-element.134), channel_id=1, source_target_pairs={{0,4},{4,0},{8,12},{12,8},{16,20},{20,16},{24,28},{28,24},{1,5},{5... | collective-permute-start | bytes 1572872 | tf_op jit(solution)/shard_map/ppermute | solution.py:72
  581.9 14.5 %collective-permute-start.64 = (bf16[128,2048]{1,0:T(8,128)(2,1)S(1)}, bf16[128,2048]{1,0:T(8,128)(2,1)S(1)}, u32[]{:S(2)}, u32[]{:S(2)}) collective-permute-start(bf16[128,2048]{1,0:T(8,128)(2,1)S(1)} %fusion.16), channel_id=1, source_target_pairs={{0,1},{1,2},{2,3},{3,0},{4,5},{5,6},{6,7},{7,4},{8,9},{9,10},{10,1... | collective-permute-start | bytes 1572872 | tf_op jit(solution)/shard_map/ppermute | solution.py:38
  597.2 15.4 %collective-permute-start.65 = (bf16[128,2048]{1,0:T(8,128)(2,1)S(1)}, bf16[128,2048]{1,0:T(8,128)(2,1)S(1)}, u32[]{:S(2)}, u32[]{:S(2)}) collective-permute-start(bf16[128,2048]{1,0:T(8,128)(2,1)S(1)} %add_convert_fusion.5), channel_id=1, source_target_pairs={{0,1},{1,2},{2,3},{3,0},{4,5},{5,6},{6,7},{7,4},{8,9},{9,10},{10,1... | collective-permute-start | bytes 1572872 | tf_op jit(solution)/shard_map/ppermute | solution.py:38
  598.1 30.0 %collective-permute-start.70 = (bf16[1024,512]{1,0:T(8,128)(2,1)S(1)}, bf16[1024,512]{1,0:T(8,128)(2,1)}, u32[]{:S(2)}, u32[]{:S(2)}) collective-permute-start(bf16[1024,512]{1,0:T(8,128)(2,1)S(1)} %pad_maximum_fusion.2), channel_id=1, source_target_pairs={{0,4},{4,0},{8,12},{12,8},{16,20},{20,16},{24,28},{28,24},{1,5},{5... | collective-permute-start | bytes 3145736 | tf_op jit(solution)/shard_map/ppermute | solution.py:72
  598.5 15.0 %collective-permute-start.75 = (bf16[256,4]{0,1:T(4,128)(2,1)S(1)}, bf16[256,4]{0,1:T(4,128)(2,1)S(1)}, u32[]{:S(2)}, u32[]{:S(2)}) collective-permute-start(bf16[256,4]{0,1:T(4,128)(2,1)S(1)} %slice.537), channel_id=1, source_target_pairs={{0,8},{4,12},{8,0},{12,4},{16,24},{20,28},{24,16},{28,20},{1,9},{5... | collective-permute-start | bytes 6152 | tf_op jit(solution)/shard_map/ppermute | solution.py:72
  599.4 20.6 %collective-permute-start.68 = (bf16[512,512]{1,0:T(8,128)(2,1)S(1)}, bf16[512,512]{1,0:T(8,128)(2,1)S(1)}, u32[]{:S(2)}, u32[]{:S(2)}) collective-permute-start(bf16[512,512]{1,0:T(8,128)(2,1)S(1)} %slice.520), channel_id=1, source_target_pairs={{0,16},{4,20},{8,24},{12,28},{16,0},{20,4},{24,8},{28,12},{1,17},{... | collective-permute-start | bytes 1572872 | tf_op jit(solution)/shard_map/ppermute | solution.py:72
  613.4 14.7 %collective-permute-start.66 = (bf16[128,2048]{1,0:T(8,128)(2,1)S(1)}, bf16[128,2048]{1,0:T(8,128)(2,1)}, u32[]{:S(2)}, u32[]{:S(2)}) collective-permute-start(bf16[128,2048]{1,0:T(8,128)(2,1)S(1)} %add_convert_fusion.4), channel_id=1, source_target_pairs={{0,1},{1,2},{2,3},{3,0},{4,5},{5,6},{6,7},{7,4},{8,9},{9,10},{10,1... | collective-permute-start | bytes 1572872 | tf_op jit(solution)/shard_map/ppermute | solution.py:38
  620.9 15.0 %collective-permute-start.69 = (bf16[256,512]{1,0:T(8,128)(2,1)}, bf16[256,512]{1,0:T(8,128)(2,1)}, u32[]{:S(2)}, u32[]{:S(2)}) collective-permute-start(bf16[256,512]{1,0:T(8,128)(2,1)} %slice.522), channel_id=1, source_target_pairs={{0,8},{4,12},{8,0},{12,4},{16,24},{20,28},{24,16},{28,20},{1,9},{5... | collective-permute-start | bytes 786440 | tf_op jit(solution)/shard_map/ppermute | solution.py:72
  631.0 15.2 %collective-permute-start.71 = (bf16[512,512]{1,0:T(8,128)(2,1)}, bf16[512,512]{1,0:T(8,128)(2,1)}, u32[]{:S(2)}, u32[]{:S(2)}) collective-permute-start(bf16[512,512]{1,0:T(8,128)(2,1)} %slice.524), channel_id=1, source_target_pairs={{0,8},{4,12},{8,0},{12,4},{16,24},{20,28},{24,16},{28,20},{1,9},{5... | collective-permute-start | bytes 1572872 | tf_op jit(solution)/shard_map/ppermute | solution.py:72
  (129 other events, 1061.6 us)
Sparse Core Ops, SparseCore 0:
  312.4 68.7 reduce-scatter.3
  384.8 137.3 reduce-scatter.7
  572.9 64.2 reduce-scatter.5
where the time goes:
time: 668 us; the launch traced here: 662 us
  waiting for transfers between devices  289 us (43%)
  matrix products  145 us (22%)
  Pallas kernels  87.2 us (13%)
  starting transfers between devices  50.5 us (8%)
  other arithmetic  42.1 us (6%)
  local copies, waits for them, and re-layouts  31.9 us (5%)
  between operations  15.7 us (2%)
    ppermute x36, waiting for transfers between devices, shift(): return lax.ppermute(x, 'fsdp', [(i, (i + by) % n) for i in range(n)])  219 us
    dot_general x28, matrix products, contract_cols(): lax.dot_general(left, right, (((1,), (1,)), ((), ())), preferred_element_...  75.6 us
    ppermute x40, waiting for transfers between devices, swap(): return lax.ppermute(x, 'ctx', [(i, i ^ bit) for i in range(n)])  70.7 us
    pallas_call x4, Pallas kernels, attend_back(): pl.pallas_call(functools.partial(bwd_kernel, np_, slots, heads, first), g...  42.6 us
    dot_general x28, matrix products, mm(): return jnp.dot(left, right, preferred_element_type=F32)  38.6 us
    dot_general x6, matrix products, contract_rows(): lax.dot_general(left, right, (((0,), (0,)), ((), ())), preferred_element_...  31.3 us
    pallas_call x4, Pallas kernels, attend(): pl.pallas_call(functools.partial(fwd_kernel, np_, slots, first, last), gr...  28.9 us
    ppermute x40, starting transfers between devices, swap(): return lax.ppermute(x, 'ctx', [(i, i ^ bit) for i in range(n)])  25.2 us
  transfers between devices with their start and end apart: 79, of which 42 were waited for; matrix products, arithmetic and copies ran while one was open for 29% of the time, Pallas kernels for 11%

commit v1 on v0

--- a/solution.py
+++ b/solution.py
@@ -81,7 +81,7 @@
     return bits, bits[::-1]
 
 
-def halving(part, me, n, order, under=()):
+def halving(part, me, n, order, marks=None):
     seq = ([1] if n > 1 else []) + list(order[::-1])
     block = part.shape[0] // n
     levels = len(seq)
@@ -97,12 +97,12 @@
     keep, away = blocks(masks[: n // 2]), blocks(masks[n // 2 :])
     for k, bit in enumerate(seq):
         got = swap(away.astype(BF), n, bit)
-        if k == 0 and under:
-            got = gate(got, *under)
         total = keep.astype(F32) + got.astype(F32)
         rest = total.shape[0] // 2
         if k < levels - 1:
             total = total.astype(BF)
+            if marks is not None:
+                marks[k].append(total)
             keep, away = total[:rest], total[rest:]
     return total
 
@@ -531,23 +531,37 @@
             grad_slots.append(got)
         gate_grads.append(g)
         up_grads.append(u)
-    down_part = contract_rows(jnp.concatenate(grad_slots), jnp.concatenate(activated)).astype(BF)
+    grad_rows = jnp.concatenate(grad_slots)
+    activ_rows = jnp.concatenate(activated)
+    wide = activ_rows.shape[1] // 2
+    down_parts = [
+        contract_rows(grad_rows, activ_rows[:, i * wide : (i + 1) * wide]).astype(BF)
+        for i in range(2)
+    ]
     state_grad = state_part(gate_grads[0], up_grads[0])
     if nf > 1:
         got = shift(acc, nf, 1)
         state_grad = got.astype(F32) + state_grad
     state_grad = upstream + state_grad
-    down_sum = ctx_scatter(down_part)
+    marks = [[] for _ in range(nc)]
+    down_grad = jnp.concatenate(
+        [
+            halving(p, me_c, nc, order, marks)
+            for p, order in zip(down_parts, bit_orders(nc))
+        ],
+        axis=1,
+    ).T
 
     attn_gain_part = jnp.sum(state_grad * attn_out * attn_rms[:, None], axis=0)
     attn_grad_b = norm_back(attn_out, attn_rms, attn_gain[None, :], state_grad).astype(BF)
     gate_up_part = contract_rows(
-        jnp.concatenate(state_slots),
+        jnp.concatenate(state_slots[:-1] + [gate(state_slots[-1], *marks[0])]),
         jnp.concatenate([jnp.concatenate(gate_grads), jnp.concatenate(up_grads)], axis=1),
     ).astype(BF)
     gate_up_sum = ctx_scatter(gate_up_part)
     first_hop = shift(attn_grad_b, nf, 1)
     proj_slots = [attn_grad_b] + ring_gather(first_hop, nf - 1, around=nf)
+    proj_slots[-1] = gate(proj_slots[-1], *marks[1])
     mixture_grad_b = jnp.concatenate(
         [contract_cols(x, output_weight).astype(BF) for x in proj_slots]
     )
@@ -615,7 +629,9 @@
     q_part = contract_rows(x_rows, jnp.concatenate(query_grads)).astype(BF)
     o_part = contract_rows(jnp.concatenate(proj_slots), mixture_b).astype(BF)
     qo_part = jnp.concatenate([q_part, o_part], axis=1)
-    qo_part, down_sum, own_a, own_b = lax.optimization_barrier((qo_part, down_sum, own_a, own_b))
+    qo_part, gate_up_sum, own_a, own_b = lax.optimization_barrier(
+        (qo_part, gate_up_sum, own_a, own_b)
+    )
     qo_grad = ctx_scatter(qo_part).astype(F32)
     query_grad, output_grad = qo_grad[:, :units], qo_grad[:, units:].T
 
@@ -641,10 +657,9 @@
     k_part = contract_rows(x_rows, k_rows).astype(BF)
     v_part = contract_rows(x_rows, v_rows).astype(BF)
     key_grad = halving(k_part, me_c, nc, orders[0])
-    value_grad = halving(v_part, me_c, nc, orders[1], (gate_up_sum,))
+    value_grad = halving(v_part, me_c, nc, orders[1])
     gains = jnp.concatenate([gathered(early_gains, 3), gathered(key_gain_sum, 1)])
     gains_own = halving(gains.T, me_c, nc, orders[0]).T
-    down_grad = down_sum.astype(F32).T
     ff = gate_weight.shape[1]
     gate_up = gate_up_sum.astype(F32)
     gate_grad, up_grad = gate_up[:, :ff], gate_up[:, ff:]

time: 668 us -> 672 us (level)
  waiting for transfers between devices: 289 us -> 279 us
  other arithmetic: 42.1 us -> 51.4 us
    ppermute x36, waiting for transfers between devices: 219 us -> 204 us  [shift(): return lax.ppermute(x, 'fsdp', [(i, (i + by) % n) for i in range(n)])]
    ppermute x40 -> x46, starting transfers between devices: 25.2 us -> 31.4 us  [swap(): return lax.ppermute(x, 'ctx', [(i, i ^ bit) for i in range(n)])]
    dot_general x6 -> x7, matrix products: 31.3 us -> 27.9 us  [contract_rows(): lax.dot_general(left, right, (((0,), (0,)), ((), ())), preferred_element_...]
    ppermute x40 -> x46, waiting for transfers between devices: 70.7 us -> 73 us  [swap(): return lax.ppermute(x, 'ctx', [(i, i ^ bit) for i in range(n)])]
    unnamed x199 -> x205, local copies, waits for them, and re-layouts: 14.8 us -> 17.1 us
  transfers between devices with their start and end apart: 79 -> 84, of which waited for: 42 -> 38; matrix products, arithmetic and copies ran while one was open for 29% -> 26% of each run, Pallas kernels for 11% -> 10%
where the time goes in v1:
time: 672 us; the launch traced here: 666 us
  waiting for transfers between devices  279 us (42%)
  matrix products  142 us (21%)
  Pallas kernels  86.2 us (13%)
  starting transfers between devices  56.7 us (8%)
  other arithmetic  51.4 us (8%)
  local copies, waits for them, and re-layouts  34.6 us (5%)
  between operations  16.4 us (2%)
    ppermute x36, waiting for transfers between devices, shift(): return lax.ppermute(x, 'fsdp', [(i, (i + by) % n) for i in range(n)])  204 us
    ppermute x46, waiting for transfers between devices, swap(): return lax.ppermute(x, 'ctx', [(i, i ^ bit) for i in range(n)])  73 us
    dot_general x28, matrix products, contract_cols(): lax.dot_general(left, right, (((1,), (1,)), ((), ())), preferred_element_...  69.9 us
    dot_general x28, matrix products, mm(): return jnp.dot(left, right, preferred_element_type=F32)  44.4 us
    pallas_call x4, Pallas kernels, attend_back(): pl.pallas_call(functools.partial(bwd_kernel, np_, slots, heads, first), g...  41.8 us
    ppermute x46, starting transfers between devices, swap(): return lax.ppermute(x, 'ctx', [(i, i ^ bit) for i in range(n)])  31.4 us
    pallas_call x4, Pallas kernels, attend(): pl.pallas_call(functools.partial(fwd_kernel, np_, slots, first, last), gr...  28.9 us
    dot_general x7, matrix products, contract_rows(): lax.dot_general(left, right, (((0,), (0,)), ((), ())), preferred_element_...  27.9 us
  transfers between devices with their start and end apart: 84, of which 38 were waited for; matrix products, arithmetic and copies ran while one was open for 26% of the time, Pallas kernels for 10%

profile of v1, /device:TPU:0, one launch (start us, length us, event | category | flops | bytes accessed | tf_op | source)
XLA Modules:
  0.0 666.4 jit_solution(16805350959187046560)
XLA Ops:
  18.5 6.0 collective-permute-done
  48.0 8.8 %collective-permute-done.2 = bf16[128,2048]{1,0:T(8,128)(2,1)S(1)} collective-permute-done((bf16[128,2048]{1,0:T(8,128)(2,1)S(1)}, bf16[128,2048]{1,0:T(8,128)(2,1)S(1)}, u32[]{:S(2)}, u32[]{:S(2)}) %collective-permute-start.2) | collective-permute-done | bytes 524320 | tf_op jit(solution)/shard_map/ppermute | solution.py:38
  69.9 5.9 shard_map.237
  80.7 10.4 %collective-permute-done.12.refs_3_.refs_7_.refs_6_.refs_10_ = bf16[256,1024]{1,0:T(8,128)(2,1)} collective-permute-done((bf16[256,1024]{1,0:T(8,128)(2,1)}, bf16[256,1024]{1,0:T(8,128)(2,1)}, u32[]{:S(2)}, u32[]{:S(2)}) %collective-permute-start.12) | collective-permute-done | bytes 524320 | tf_op jit(solution)/shard_map/ppermute | solution.py:72
  91.1 10.7 %collective-permute-done.17.refs_5_.refs_9_.refs_8_.refs_12_ = bf16[256,1024]{1,0:T(8,128)(2,1)} collective-permute-done((bf16[256,1024]{1,0:T(8,128)(2,1)}, bf16[256,1024]{1,0:T(8,128)(2,1)}, u32[]{:S(2)}, u32[]{:S(2)}) %collective-permute-start.17) | collective-permute-done | bytes 524320 | tf_op jit(solution)/shard_map/ppermute | solution.py:72
  101.8 6.9 %shard_map.238 = (f32[4,1,512]{2,1,0:T(1,128)}, f32[4,1,512]{2,1,0:T(1,128)}, f32[512,512]{1,0:T(8,128)}) custom-call(s32[8]{0:T(128)} %pad_add_fusion.4.refs_0_, bf16[512,512]{1,0:T(8,128)(2,1)} %get-tuple-element.87.refs_1_, s32[1,512]{1,0:T(1,128)} %bitcast.295, bf16[256,1024]{1,0:T(8,128)(2,1)} %get-tuple-element.88.refs_3_.refs_7_.refs_6_.refs_10_, ...), custom_call_target="tpu_custom_call" | custom-call | flops 2147483648 | bytes 2097152 | tf_op jit(solution)/shard_map/pallas_call | solution.py:234
  112.6 7.2 %shard_map.239 = (f32[4,1,512]{2,1,0:T(1,128)}, f32[4,1,512]{2,1,0:T(1,128)}, f32[512,512]{1,0:T(8,128)}) custom-call(s32[8]{0:T(128)} %pad_add_fusion.5.refs_0_, bf16[512,512]{1,0:T(8,128)(2,1)} %get-tuple-element.87.refs_1_, s32[1,512]{1,0:T(1,128)} %bitcast.296, bf16[256,1024]{1,0:T(8,128)(2,1)} %collective-permute-done.12.refs_3_.refs_7_.refs_6_.refs_10_, ...), custom_call_target="tpu_custom_call" | custom-call | flops 2147483648 | bytes 2097152 | tf_op jit(solution)/shard_map/pallas_call | solution.py:234
  119.9 3.5 collective-permute-done.21.refs_5_.refs_9_.refs_8_.refs_12_
  126.3 7.2 %shard_map.240 = (f32[4,1,512]{2,1,0:T(1,128)}, f32[4,1,512]{2,1,0:T(1,128)}, f32[512,512]{1,0:T(8,128)}) custom-call(s32[8]{0:T(128)} %pad_add_fusion.6.refs_0_, bf16[512,512]{1,0:T(8,128)(2,1)} %get-tuple-element.87.refs_1_, s32[1,512]{1,0:T(1,128)} %bitcast.297, bf16[256,1024]{1,0:T(8,128)(2,1)} %collective-permute-done.23.refs_3_.refs_7_.refs_6_.refs_10_, ...), custom_call_target="tpu_custom_call" | custom-call | flops 2147483648 | bytes 2097152 | tf_op jit(solution)/shard_map/pallas_call | solution.py:234
  133.6 7.5 %shard_map.241 = (f32[512,512]{1,0:T(8,128)}, bf16[512,512]{1,0:T(8,128)(2,1)}, f32[4,1,512]{2,1,0:T(1,128)}) custom-call(s32[8]{0:T(128)} %pad_add_fusion.3.refs_0_, bf16[512,512]{1,0:T(8,128)(2,1)} %get-tuple-element.87.refs_1_, s32[1,512]{1,0:T(1,128)} %bitcast.298, bf16[256,1024]{1,0:T(8,128)(2,1)} %collective-permute-done.15.refs_3_.refs_7_.refs_6_.refs_10_, ...), custom_call_target="tpu_custom_call" | custom-call | flops 2147483648 | bytes 2097152 | tf_op jit(solution)/shard_map/pallas_call | solution.py:234
  143.4 16.1 %collective-permute-done.26 = bf16[128,2048]{1,0:T(8,128)(2,1)S(1)} collective-permute-done((bf16[128,2048]{1,0:T(8,128)(2,1)S(1)}, bf16[128,2048]{1,0:T(8,128)(2,1)S(1)}, u32[]{:S(2)}, u32[]{:S(2)}) %collective-permute-start.26) | collective-permute-done | bytes 524320 | tf_op jit(solution)/shard_map/ppermute | solution.py:38
  160.1 15.3 %collective-permute-done.27 = bf16[128,2048]{1,0:T(8,128)(2,1)S(1)} collective-permute-done((bf16[128,2048]{1,0:T(8,128)(2,1)S(1)}, bf16[128,2048]{1,0:T(8,128)(2,1)S(1)}, u32[]{:S(2)}, u32[]{:S(2)}) %collective-permute-start.27) | collective-permute-done | bytes 524320 | tf_op jit(solution)/shard_map/ppermute | solution.py:38
  175.9 14.5 %collective-permute-done.28 = bf16[128,2048]{1,0:T(8,128)(2,1)} collective-permute-done((bf16[128,2048]{1,0:T(8,128)(2,1)S(1)}, bf16[128,2048]{1,0:T(8,128)(2,1)}, u32[]{:S(2)}, u32[]{:S(2)}) %collective-permute-start.28) | collective-permute-done | bytes 524320 | tf_op jit(solution)/shard_map/ppermute | solution.py:38
  194.4 5.4 fusion.125
  199.8 8.1 %collective-permute-done.29 = bf16[128,2048]{1,0:T(8,128)(2,1)S(1)} collective-permute-done((bf16[128,2048]{1,0:T(8,128)(2,1)S(1)}, bf16[128,2048]{1,0:T(8,128)(2,1)S(1)}, u32[]{:S(2)}, u32[]{:S(2)}) %collective-permute-start.29) | collective-permute-done | bytes 524320 | tf_op jit(solution)/shard_map/ppermute | solution.py:38
  213.9 10.6 %collective-permute-done.31 = bf16[128,2048]{1,0:T(8,128)(2,1)S(1)} collective-permute-done((bf16[128,2048]{1,0:T(8,128)(2,1)S(1)}, bf16[128,2048]{1,0:T(8,128)(2,1)S(1)}, u32[]{:S(2)}, u32[]{:S(2)}) %collective-permute-start.31) | collective-permute-done | bytes 524320 | tf_op jit(solution)/shard_map/ppermute | solution.py:38
  228.3 7.4 %collective-permute-done.30 = bf16[128,2048]{1,0:T(8,128)(2,1)S(1)} collective-permute-done((bf16[128,2048]{1,0:T(8,128)(2,1)S(1)}, bf16[128,2048]{1,0:T(8,128)(2,1)S(1)}, u32[]{:S(2)}, u32[]{:S(2)}) %collective-permute-start.30) | collective-permute-done | bytes 524320 | tf_op jit(solution)/shard_map/ppermute | solution.py:38
  237.3 9.7 %collective-permute-done.33 = bf16[128,2048]{1,0:T(8,128)(2,1)S(1)} collective-permute-done((bf16[128,2048]{1,0:T(8,128)(2,1)S(1)}, bf16[128,2048]{1,0:T(8,128)(2,1)S(1)}, u32[]{:S(2)}, u32[]{:S(2)}) %collective-permute-start.33) | collective-permute-done | bytes 524320 | tf_op jit(solution)/shard_map/ppermute | solution.py:38
  257.2 9.2 %collective-permute-done.34 = bf16[128,2048]{1,0:T(8,128)(2,1)S(1)} collective-permute-done((bf16[128,2048]{1,0:T(8,128)(2,1)S(1)}, bf16[128,2048]{1,0:T(8,128)(2,1)S(1)}, u32[]{:S(2)}, u32[]{:S(2)}) %collective-permute-start.34) | collective-permute-done | bytes 524320 | tf_op jit(solution)/shard_map/ppermute | solution.py:38
  270.3 4.0 multiply_convert_fusion.6
  274.4 8.0 %collective-permute-done.35 = bf16[128,2048]{1,0:T(8,128)(2,1)S(1)} collective-permute-done((bf16[128,2048]{1,0:T(8,128)(2,1)S(1)}, bf16[128,2048]{1,0:T(8,128)(2,1)S(1)}, u32[]{:S(2)}, u32[]{:S(2)}) %collective-permute-start.35) | collective-permute-done | bytes 524320 | tf_op jit(solution)/shard_map/ppermute | solution.py:38
  282.4 4.0 multiply_convert_fusion.4
  286.4 8.8 %collective-permute-done.37 = bf16[128,2048]{1,0:T(8,128)(2,1)S(1)} collective-permute-done((bf16[128,2048]{1,0:T(8,128)(2,1)S(1)}, bf16[128,2048]{1,0:T(8,128)(2,1)S(1)}, u32[]{:S(2)}, u32[]{:S(2)}) %collective-permute-start.37) | collective-permute-done | bytes 524320 | tf_op jit(solution)/shard_map/ppermute | solution.py:38
  295.6 4.0 multiply_convert_fusion.2
  299.6 6.9 %collective-permute-done.39 = bf16[128,2048]{1,0:T(8,128)(2,1)S(1)} collective-permute-done((bf16[128,2048]{1,0:T(8,128)(2,1)S(1)}, bf16[128,2048]{1,0:T(8,128)(2,1)S(1)}, u32[]{:S(2)}, u32[]{:S(2)}) %collective-permute-start.39) | collective-permute-done | bytes 524320 | tf_op jit(solution)/shard_map/ppermute | solution.py:38
  314.0 4.0 multiply_convert_fusion
  322.8 14.9 %convolution_convert_fusion = bf16[2048,4096]{1,0:T(8,128)(2,1)} fusion(bf16[128,2048]{1,0:T(8,128)(2,1)} %get-tuple-element.222, bf16[128,2048]{1,0:T(8,128)(2,1)} %get-tuple-element.135, bf16[128,2048]{1,0:T(8,128)(2,1)} %get-tuple-element.134, bf16[128,2048]{1,0:T(8,128)(2,1)} %get-tuple-element.108, bf16[128,2048]{1,0:T(8,128)(2,1)} %get-tuple-element.223, ...), kind=kOutput, calls=%fused_computation | convolution fusion | flops 8640266240 | bytes 23068672 | tf_op jit(solution)/shard_map/dot_general | solution.py:26
  341.6 7.8 %fusion.126 = f32[128,2048]{1,0:T(8,128)S(1)} fusion(bf16[128,2048]{1,0:T(8,128)(2,1)S(1)} %copy-done.54, bf16[2048,2048]{1,0:T(8,128)(2,1)} %param.24), kind=kOutput, calls=%fused_computation.365 | convolution fusion | flops 1073741824 | bytes 9961472 | tf_op jit(solution)/shard_map/dot_general | solution.py:30
  349.5 8.0 %fusion.15 = bf16[128,2048]{1,0:T(8,128)(2,1)S(1)} fusion(f32[128,2048]{1,0:T(8,128)S(1)} %fusion.126, bf16[128,2048]{1,0:T(8,128)(2,1)S(1)} %copy-done.53, bf16[2048,2048]{1,0:T(8,128)(2,1)} %param.25), kind=kOutput, calls=%fused_computation.38 | convolution fusion | flops 1074266112 | bytes 10485760 | tf_op jit(solution)/shard_map/dot_general | solution.py:30
  360.7 13.2 %collective-permute-done.36 = bf16[128,2048]{1,0:T(8,128)(2,1)S(1)} collective-permute-done((bf16[128,2048]{1,0:T(8,128)(2,1)S(1)}, bf16[128,2048]{1,0:T(8,128)(2,1)S(1)}, u32[]{:S(2)}, u32[]{:S(2)}) %collective-permute-start.36) | collective-permute-done | bytes 524320 | tf_op jit(solution)/shard_map/ppermute | solution.py:38
  382.8 9.5 %collective-permute-done.38 = bf16[128,2048]{1,0:T(8,128)(2,1)S(1)} collective-permute-done((bf16[128,2048]{1,0:T(8,128)(2,1)S(1)}, bf16[128,2048]{1,0:T(8,128)(2,1)S(1)}, u32[]{:S(2)}, u32[]{:S(2)}) %collective-permute-start.38) | collective-permute-done | bytes 524320 | tf_op jit(solution)/shard_map/ppermute | solution.py:38
  395.8 11.5 %collective-permute-done.40 = bf16[128,2048]{1,0:T(8,128)(2,1)S(1)} collective-permute-done((bf16[128,2048]{1,0:T(8,128)(2,1)S(1)}, bf16[128,2048]{1,0:T(8,128)(2,1)S(1)}, u32[]{:S(2)}, u32[]{:S(2)}) %collective-permute-start.40) | collective-permute-done | bytes 524320 | tf_op jit(solution)/shard_map/ppermute | solution.py:38
  413.4 12.3 %collective-permute-done.41 = bf16[128,2048]{1,0:T(8,128)(2,1)} collective-permute-done((bf16[128,2048]{1,0:T(8,128)(2,1)}, bf16[128,2048]{1,0:T(8,128)(2,1)}, u32[]{:S(2)}, u32[]{:S(2)}) %collective-permute-start.41) | collective-permute-done | bytes 524320 | tf_op jit(solution)/shard_map/ppermute | solution.py:38
  432.7 5.9 collective-permute-done.42
  439.4 9.2 %collective-permute-done.47 = bf16[512,1024]{1,0:T(8,128)(2,1)} collective-permute-done((bf16[512,1024]{1,0:T(8,128)(2,1)S(1)}, bf16[512,1024]{1,0:T(8,128)(2,1)}, u32[]{:S(2)}, u32[]{:S(2)}) %collective-permute-start.47) | collective-permute-done | bytes 1048608 | tf_op jit(solution)/shard_map/ppermute | solution.py:72
  452.6 19.6 %collective-permute-done.45 = bf16[512,1024]{1,0:T(8,128)(2,1)S(1)} collective-permute-done((bf16[512,1024]{1,0:T(8,128)(2,1)S(1)}, bf16[512,1024]{1,0:T(8,128)(2,1)S(1)}, u32[]{:S(2)}, u32[]{:S(2)}) %collective-permute-start.45) | collective-permute-done | bytes 1048608 | tf_op jit(solution)/shard_map/ppermute | solution.py:72
  475.2 10.4 %shard_map.242 = (f32[512,512]{1,0:T(8,128)}, bf16[256,1024]{1,0:T(8,128)(2,1)}, bf16[256,1024]{1,0:T(8,128)(2,1)}, bf16[256,1024]{1,0:T(8,128)(2,1)}, bf16[256,1024]{1,0:T(8,128)(2,1)}) custom-call(s32[8]{0:T(128)} %pad_add_fusion.3.refs_0_, bf16[512,512]{1,0:T(8,128)(2,1)} %get-tuple-element.87.refs_1_, bf16[512,512]{1,0:T(8,128)(2,1)} %pad_maximum_fusion.7.refs_2_, ...), custom_call_target="tpu_custom_call" | custom-call | flops 5368709120 | bytes 4194304 | tf_op jit(solution)/shard_map/pallas_call | solution.py:306
  486.1 4.3 convolution_convert_fusion.5
  497.4 10.4 %shard_map.243 = (f32[512,512]{1,0:T(8,128)}, bf16[256,1024]{1,0:T(8,128)(2,1)}, bf16[256,1024]{1,0:T(8,128)(2,1)}, bf16[256,1024]{1,0:T(8,128)(2,1)}, bf16[256,1024]{1,0:T(8,128)(2,1)}) custom-call(s32[8]{0:T(128)} %pad_add_fusion.6.refs_0_, bf16[512,512]{1,0:T(8,128)(2,1)} %get-tuple-element.87.refs_1_, bf16[512,512]{1,0:T(8,128)(2,1)} %pad_maximum_fusion.7.refs_2_, ...), custom_call_target="tpu_custom_call" | custom-call | flops 5368709120 | bytes 4194304 | tf_op jit(solution)/shard_map/pallas_call | solution.py:306
  518.7 10.5 %shard_map.244 = (f32[512,512]{1,0:T(8,128)}, bf16[256,1024]{1,0:T(8,128)(2,1)}, bf16[256,1024]{1,0:T(8,128)(2,1)}, bf16[256,1024]{1,0:T(8,128)(2,1)}, bf16[256,1024]{1,0:T(8,128)(2,1)}) custom-call(s32[8]{0:T(128)} %pad_add_fusion.5.refs_0_, bf16[512,512]{1,0:T(8,128)(2,1)} %get-tuple-element.87.refs_1_, bf16[512,512]{1,0:T(8,128)(2,1)} %pad_maximum_fusion.7.refs_2_, ...), custom_call_target="tpu_custom_call" | custom-call | flops 5368709120 | bytes 4194304 | tf_op jit(solution)/shard_map/pallas_call | solution.py:306
  535.9 10.6 %shard_map.245 = (f32[512,512]{1,0:T(8,128)}, bf16[256,1024]{1,0:T(8,128)(2,1)}, bf16[256,1024]{1,0:T(8,128)(2,1)}, bf16[256,1024]{1,0:T(8,128)(2,1)}, bf16[256,1024]{1,0:T(8,128)(2,1)}) custom-call(s32[8]{0:T(128)} %pad_add_fusion.4.refs_0_, bf16[512,512]{1,0:T(8,128)(2,1)} %get-tuple-element.87.refs_1_, bf16[512,512]{1,0:T(8,128)(2,1)} %pad_maximum_fusion.7.refs_2_, ...), custom_call_target="tpu_custom_call" | custom-call | flops 5368709120 | bytes 4194304 | tf_op jit(solution)/shard_map/pallas_call | solution.py:306
  551.3 4.9 shard_map.246
  558.3 4.6 collective-permute-start.57
  580.1 4.6 shard_map.247
  591.2 4.1 fusion.111
  620.4 12.4 %collective-permute-done.69 = bf16[128,2048]{1,0:T(8,128)(2,1)S(1)} collective-permute-done((bf16[128,2048]{1,0:T(8,128)(2,1)S(1)}, bf16[128,2048]{1,0:T(8,128)(2,1)S(1)}, u32[]{:S(2)}, u32[]{:S(2)}) %collective-permute-start.69) | collective-permute-done | bytes 524320 | tf_op jit(solution)/shard_map/ppermute | solution.py:38
  633.7 6.0 collective-permute-done.75
  642.2 5.7 collective-permute-done.70
  (540 shorter events, 239.3 us)
Async XLA Ops:
  7.2 572.9 %reduce-scatter.3.cloned.1.call-start = ((), (), s32[]{:S(2)}) async-start(), calls=%async_computation.2 | async-start | bytes 18874368 | tf_op jit(solution)/shard_map/reduce_scatter | solution.py:509
  7.3 17.3 %collective-permute-start = (bf16[128,2048]{1,0:T(8,128)(2,1)}, bf16[128,2048]{1,0:T(8,128)(2,1)S(1)}, u32[]{:S(2)}, u32[]{:S(2)}) collective-permute-start(bf16[128,2048]{1,0:T(8,128)(2,1)} %param.14), channel_id=1, source_target_pairs={{0,1},{1,2},{2,3},{3,0},{4,5},{5,6},{6,7},{7,4},{8,9},{9,10},{10,1... | collective-permute-start | bytes 1572872 | tf_op jit(solution)/shard_map/ppermute | solution.py:38
  29.0 14.4 %collective-permute-start.1 = (bf16[128,2048]{1,0:T(8,128)(2,1)S(1)}, bf16[128,2048]{1,0:T(8,128)(2,1)S(1)}, u32[]{:S(2)}, u32[]{:S(2)}) collective-permute-start(bf16[128,2048]{1,0:T(8,128)(2,1)S(1)} %collective-permute-done), channel_id=1, source_target_pairs={{0,1},{1,2},{2,3},{3,0},{4,5},{5,6},{6,7},{7,4},{8,9},{9,10},{10,1... | collective-permute-start | bytes 1572872 | tf_op jit(solution)/shard_map/ppermute | solution.py:38
  43.4 13.5 %collective-permute-start.2 = (bf16[128,2048]{1,0:T(8,128)(2,1)S(1)}, bf16[128,2048]{1,0:T(8,128)(2,1)S(1)}, u32[]{:S(2)}, u32[]{:S(2)}) collective-permute-start(bf16[128,2048]{1,0:T(8,128)(2,1)S(1)} %collective-permute-done.1), channel_id=1, source_target_pairs={{0,1},{1,2},{2,3},{3,0},{4,5},{5,6},{6,7},{7,4},{8,9},{9,10},{10,1... | collective-permute-start | bytes 1572872 | tf_op jit(solution)/shard_map/ppermute | solution.py:38
  75.9 15.2 %collective-permute-start.12 = (bf16[256,1024]{1,0:T(8,128)(2,1)}, bf16[256,1024]{1,0:T(8,128)(2,1)}, u32[]{:S(2)}, u32[]{:S(2)}) collective-permute-start(bf16[256,1024]{1,0:T(8,128)(2,1)} %get-tuple-element.88.refs_3_.refs_7_.refs_6_.refs_10_), channel_id=1, source_target_pairs={{0,8},{4,12},{8,0},{12,4},{16,24},{20,28},{24,16},{28,20},{1,9},{5... | collective-permute-start | bytes 1572872 | tf_op jit(solution)/shard_map/ppermute | solution.py:72
  77.2 24.6 %collective-permute-start.17 = (bf16[256,1024]{1,0:T(8,128)(2,1)}, bf16[256,1024]{1,0:T(8,128)(2,1)}, u32[]{:S(2)}, u32[]{:S(2)}) collective-permute-start(bf16[256,1024]{1,0:T(8,128)(2,1)} %get-tuple-element.89.refs_5_.refs_9_.refs_8_.refs_12_), channel_id=1, source_target_pairs={{0,8},{4,12},{8,0},{12,4},{16,24},{20,28},{24,16},{28,20},{1,9},{5... | collective-permute-start | bytes 1572872 | tf_op jit(solution)/shard_map/ppermute | solution.py:72
  78.0 23.8 %collective-permute-start.14 = (bf16[256,1024]{1,0:T(8,128)(2,1)}, bf16[256,1024]{1,0:T(8,128)(2,1)}, u32[]{:S(2)}, u32[]{:S(2)}) collective-permute-start(bf16[256,1024]{1,0:T(8,128)(2,1)} %get-tuple-element.89.refs_5_.refs_9_.refs_8_.refs_12_), channel_id=1, source_target_pairs={{0,4},{4,0},{8,12},{12,8},{16,20},{20,16},{24,28},{28,24},{1,5},{5... | collective-permute-start | bytes 1572872 | tf_op jit(solution)/shard_map/ppermute | solution.py:72
  78.0 30.7 %collective-permute-start.20 = (bf16[256,1024]{1,0:T(8,128)(2,1)}, bf16[256,1024]{1,0:T(8,128)(2,1)}, u32[]{:S(2)}, u32[]{:S(2)}) collective-permute-start(bf16[256,1024]{1,0:T(8,128)(2,1)} %get-tuple-element.89.refs_5_.refs_9_.refs_8_.refs_12_), channel_id=1, source_target_pairs={{0,16},{4,20},{8,24},{12,28},{16,0},{20,4},{24,8},{28,12},{1,17},{... | collective-permute-start | bytes 1572872 | tf_op jit(solution)/shard_map/ppermute | solution.py:72
  79.9 32.2 %collective-permute-start.23 = (bf16[256,1024]{1,0:T(8,128)(2,1)}, bf16[256,1024]{1,0:T(8,128)(2,1)}, u32[]{:S(2)}, u32[]{:S(2)}) collective-permute-start(bf16[256,1024]{1,0:T(8,128)(2,1)} %get-tuple-element.88.refs_3_.refs_7_.refs_6_.refs_10_), channel_id=1, source_target_pairs={{0,16},{4,20},{8,24},{12,28},{16,0},{20,4},{24,8},{28,12},{1,17},{... | collective-permute-start | bytes 1572872 | tf_op jit(solution)/shard_map/ppermute | solution.py:72
  91.1 21.0 %collective-permute-start.16 = (bf16[256,1024]{1,0:T(8,128)(2,1)}, bf16[256,1024]{1,0:T(8,128)(2,1)}, u32[]{:S(2)}, u32[]{:S(2)}) collective-permute-start(bf16[256,1024]{1,0:T(8,128)(2,1)} %collective-permute-done.12.refs_3_.refs_7_.refs_6_.refs_10_), channel_id=1, source_target_pairs={{0,4},{4,0},{8,12},{12,8},{16,20},{20,16},{24,28},{28,24},{1,5},{5... | collective-permute-start | bytes 1572872 | tf_op jit(solution)/shard_map/ppermute | solution.py:72
  108.7 14.7 %collective-permute-start.21 = (bf16[256,1024]{1,0:T(8,128)(2,1)}, bf16[256,1024]{1,0:T(8,128)(2,1)}, u32[]{:S(2)}, u32[]{:S(2)}) collective-permute-start(bf16[256,1024]{1,0:T(8,128)(2,1)} %collective-permute-done.20.refs_5_.refs_9_.refs_8_.refs_12_), channel_id=1, source_target_pairs={{0,8},{4,12},{8,0},{12,4},{16,24},{20,28},{24,16},{28,20},{1,9},{5... | collective-permute-start | bytes 1572872 | tf_op jit(solution)/shard_map/ppermute | solution.py:72
  110.0 14.3 %collective-permute-start.15 = (bf16[256,1024]{1,0:T(8,128)(2,1)}, bf16[256,1024]{1,0:T(8,128)(2,1)}, u32[]{:S(2)}, u32[]{:S(2)}) collective-permute-start(bf16[256,1024]{1,0:T(8,128)(2,1)} %collective-permute-done.12.refs_3_.refs_7_.refs_6_.refs_10_), channel_id=1, source_target_pairs={{0,16},{4,20},{8,24},{12,28},{16,0},{20,4},{24,8},{28,12},{1,17},{... | collective-permute-start | bytes 1572872 | tf_op jit(solution)/shard_map/ppermute | solution.py:72
  112.1 13.4 %collective-permute-start.25 = (bf16[256,1024]{1,0:T(8,128)(2,1)}, bf16[256,1024]{1,0:T(8,128)(2,1)S(1)}, u32[]{:S(2)}, u32[]{:S(2)}) collective-permute-start(bf16[256,1024]{1,0:T(8,128)(2,1)} %collective-permute-done.20.refs_5_.refs_9_.refs_8_.refs_12_), channel_id=1, source_target_pairs={{0,4},{4,0},{8,12},{12,8},{16,20},{20,16},{24,28},{28,24},{1,5},{5... | collective-permute-start | bytes 1572872 | tf_op jit(solution)/shard_map/ppermute | solution.py:72
  112.1 13.4 %collective-permute-start.24 = (bf16[256,1024]{1,0:T(8,128)(2,1)}, bf16[256,1024]{1,0:T(8,128)(2,1)}, u32[]{:S(2)}, u32[]{:S(2)}) collective-permute-start(bf16[256,1024]{1,0:T(8,128)(2,1)} %collective-permute-done.23.refs_3_.refs_7_.refs_6_.refs_10_), channel_id=1, source_target_pairs={{0,4},{4,0},{8,12},{12,8},{16,20},{20,16},{24,28},{28,24},{1,5},{5... | collective-permute-start | bytes 1572872 | tf_op jit(solution)/shard_map/ppermute | solution.py:72
  143.4 16.2 %collective-permute-start.26 = (bf16[128,2048]{1,0:T(8,128)(2,1)S(1)}, bf16[128,2048]{1,0:T(8,128)(2,1)S(1)}, u32[]{:S(2)}, u32[]{:S(2)}) collective-permute-start(bf16[128,2048]{1,0:T(8,128)(2,1)S(1)} %convolution_convert_fusion.8), channel_id=1, source_target_pairs={{0,1},{1,2},{2,3},{3,0},{4,5},{5,6},{6,7},{7,4},{8,9},{9,10},{10,1... | collective-permute-start | bytes 1572872 | tf_op jit(solution)/shard_map/ppermute | solution.py:38
  160.0 15.3 %collective-permute-start.27 = (bf16[128,2048]{1,0:T(8,128)(2,1)S(1)}, bf16[128,2048]{1,0:T(8,128)(2,1)S(1)}, u32[]{:S(2)}, u32[]{:S(2)}) collective-permute-start(bf16[128,2048]{1,0:T(8,128)(2,1)S(1)} %add_convert_fusion.30), channel_id=1, source_target_pairs={{0,1},{1,2},{2,3},{3,0},{4,5},{5,6},{6,7},{7,4},{8,9},{9,10},{10,1... | collective-permute-start | bytes 1572872 | tf_op jit(solution)/shard_map/ppermute | solution.py:38
  175.8 14.6 %collective-permute-start.28 = (bf16[128,2048]{1,0:T(8,128)(2,1)S(1)}, bf16[128,2048]{1,0:T(8,128)(2,1)}, u32[]{:S(2)}, u32[]{:S(2)}) collective-permute-start(bf16[128,2048]{1,0:T(8,128)(2,1)S(1)} %add_convert_fusion.29), channel_id=1, source_target_pairs={{0,1},{1,2},{2,3},{3,0},{4,5},{5,6},{6,7},{7,4},{8,9},{9,10},{10,1... | collective-permute-start | bytes 1572872 | tf_op jit(solution)/shard_map/ppermute | solution.py:38
  194.1 13.8 %collective-permute-start.29 = (bf16[128,2048]{1,0:T(8,128)(2,1)S(1)}, bf16[128,2048]{1,0:T(8,128)(2,1)S(1)}, u32[]{:S(2)}, u32[]{:S(2)}) collective-permute-start(bf16[128,2048]{1,0:T(8,128)(2,1)S(1)} %fusion.40), channel_id=1, source_target_pairs={{0,1},{1,2},{2,3},{3,0},{4,5},{5,6},{6,7},{7,4},{8,9},{9,10},{10,1... | collective-permute-start | bytes 1572872 | tf_op jit(solution)/shard_map/ppermute | solution.py:38
  207.9 16.6 %collective-permute-start.31 = (bf16[128,2048]{1,0:T(8,128)(2,1)S(1)}, bf16[128,2048]{1,0:T(8,128)(2,1)S(1)}, u32[]{:S(2)}, u32[]{:S(2)}) collective-permute-start(bf16[128,2048]{1,0:T(8,128)(2,1)S(1)} %collective-permute-done.29), channel_id=1, source_target_pairs={{0,1},{1,2},{2,3},{3,0},{4,5},{5,6},{6,7},{7,4},{8,9},{9,10},{10,1... | collective-permute-start | bytes 1572872 | tf_op jit(solution)/shard_map/ppermute | solution.py:38
  213.9 21.9 %collective-permute-start.30 = (bf16[128,2048]{1,0:T(8,128)(2,1)S(1)}, bf16[128,2048]{1,0:T(8,128)(2,1)S(1)}, u32[]{:S(2)}, u32[]{:S(2)}) collective-permute-start(bf16[128,2048]{1,0:T(8,128)(2,1)S(1)} %convolution_convert_fusion.7), channel_id=1, source_target_pairs={{0,1},{1,2},{2,3},{3,0},{4,5},{5,6},{6,7},{7,4},{8,9},{9,10},{10,1... | collective-permute-start | bytes 1572872 | tf_op jit(solution)/shard_map/ppermute | solution.py:38
  225.8 21.1 %collective-permute-start.33 = (bf16[128,2048]{1,0:T(8,128)(2,1)S(1)}, bf16[128,2048]{1,0:T(8,128)(2,1)S(1)}, u32[]{:S(2)}, u32[]{:S(2)}) collective-permute-start(bf16[128,2048]{1,0:T(8,128)(2,1)S(1)} %collective-permute-done.31), channel_id=1, source_target_pairs={{0,1},{1,2},{2,3},{3,0},{4,5},{5,6},{6,7},{7,4},{8,9},{9,10},{10,1... | collective-permute-start | bytes 1572872 | tf_op jit(solution)/shard_map/ppermute | solution.py:38
  237.0 17.3 %collective-permute-start.32 = (bf16[128,2048]{1,0:T(8,128)(2,1)S(1)}, bf16[128,2048]{1,0:T(8,128)(2,1)S(1)}, u32[]{:S(2)}, u32[]{:S(2)}) collective-permute-start(bf16[128,2048]{1,0:T(8,128)(2,1)S(1)} %add_convert_fusion.28), channel_id=1, source_target_pairs={{0,1},{1,2},{2,3},{3,0},{4,5},{5,6},{6,7},{7,4},{8,9},{9,10},{10,1... | collective-permute-start | bytes 1572872 | tf_op jit(solution)/shard_map/ppermute | solution.py:38
  337.7 318.5 %reduce-scatter.5.cloned.1.call-start = ((), (), s32[]{:S(2)}) async-start(), calls=%async_computation.3 | async-start | bytes 4718592 | tf_op jit(solution)/shard_map/reduce_scatter | solution.py:509
  357.5 16.4 %collective-permute-start.36 = (bf16[128,2048]{1,0:T(8,128)(2,1)S(1)}, bf16[128,2048]{1,0:T(8,128)(2,1)S(1)}, u32[]{:S(2)}, u32[]{:S(2)}) collective-permute-start(bf16[128,2048]{1,0:T(8,128)(2,1)S(1)} %fusion.15), channel_id=1, source_target_pairs={{0,1},{1,2},{2,3},{3,0},{4,5},{5,6},{6,7},{7,4},{8,9},{9,10},{10,1... | collective-permute-start | bytes 1572872 | tf_op jit(solution)/shard_map/ppermute | solution.py:38
  376.9 15.4 %collective-permute-start.38 = (bf16[128,2048]{1,0:T(8,128)(2,1)S(1)}, bf16[128,2048]{1,0:T(8,128)(2,1)S(1)}, u32[]{:S(2)}, u32[]{:S(2)}) collective-permute-start(bf16[128,2048]{1,0:T(8,128)(2,1)S(1)} %add_convert_fusion.25), channel_id=1, source_target_pairs={{0,1},{1,2},{2,3},{3,0},{4,5},{5,6},{6,7},{7,4},{8,9},{9,10},{10,1... | collective-permute-start | bytes 1572872 | tf_op jit(solution)/shard_map/ppermute | solution.py:38
  392.4 14.9 %collective-permute-start.40 = (bf16[128,2048]{1,0:T(8,128)(2,1)S(1)}, bf16[128,2048]{1,0:T(8,128)(2,1)S(1)}, u32[]{:S(2)}, u32[]{:S(2)}) collective-permute-start(bf16[128,2048]{1,0:T(8,128)(2,1)S(1)} %add_convert_fusion.24), channel_id=1, source_target_pairs={{0,1},{1,2},{2,3},{3,0},{4,5},{5,6},{6,7},{7,4},{8,9},{9,10},{10,1... | collective-permute-start | bytes 1572872 | tf_op jit(solution)/shard_map/ppermute | solution.py:38
  411.7 13.9 %collective-permute-start.41 = (bf16[128,2048]{1,0:T(8,128)(2,1)}, bf16[128,2048]{1,0:T(8,128)(2,1)}, u32[]{:S(2)}, u32[]{:S(2)}) collective-permute-start(bf16[128,2048]{1,0:T(8,128)(2,1)} %subtract_convert_fusion), channel_id=1, source_target_pairs={{0,1},{1,2},{2,3},{3,0},{4,5},{5,6},{6,7},{7,4},{8,9},{9,10},{10,1... | collective-permute-start | bytes 1572872 | tf_op jit(solution)/shard_map/ppermute | solution.py:38
  412.9 35.8 %collective-permute-start.47 = (bf16[512,1024]{1,0:T(8,128)(2,1)S(1)}, bf16[512,1024]{1,0:T(8,128)(2,1)}, u32[]{:S(2)}, u32[]{:S(2)}) collective-permute-start(bf16[512,1024]{1,0:T(8,128)(2,1)S(1)} %slice.536), channel_id=1, source_target_pairs={{0,8},{4,12},{8,0},{12,4},{16,24},{20,28},{24,16},{28,20},{1,9},{5... | collective-permute-start | bytes 3145736 | tf_op jit(solution)/shard_map/ppermute | solution.py:72
  425.6 13.0 %collective-permute-start.42 = (bf16[128,2048]{1,0:T(8,128)(2,1)}, bf16[128,2048]{1,0:T(8,128)(2,1)S(1)}, u32[]{:S(2)}, u32[]{:S(2)}) collective-permute-start(bf16[128,2048]{1,0:T(8,128)(2,1)} %collective-permute-done.41), channel_id=1, source_target_pairs={{0,1},{1,2},{2,3},{3,0},{4,5},{5,6},{6,7},{7,4},{8,9},{9,10},{10,1... | collective-permute-start | bytes 1572872 | tf_op jit(solution)/shard_map/ppermute | solution.py:38
  426.9 45.3 %collective-permute-start.45 = (bf16[512,1024]{1,0:T(8,128)(2,1)S(1)}, bf16[512,1024]{1,0:T(8,128)(2,1)S(1)}, u32[]{:S(2)}, u32[]{:S(2)}) collective-permute-start(bf16[512,1024]{1,0:T(8,128)(2,1)S(1)} %slice.533), channel_id=1, source_target_pairs={{0,16},{4,20},{8,24},{12,28},{16,0},{20,4},{24,8},{28,12},{1,17},{... | collective-permute-start | bytes 3145736 | tf_op jit(solution)/shard_map/ppermute | solution.py:72
  438.6 34.9 %collective-permute-start.43 = (bf16[128,2048]{1,0:T(8,128)(2,1)S(1)}, bf16[128,2048]{1,0:T(8,128)(2,1)S(1)}, u32[]{:S(2)}, u32[]{:S(2)}) collective-permute-start(bf16[128,2048]{1,0:T(8,128)(2,1)S(1)} %collective-permute-done.42), channel_id=1, source_target_pairs={{0,1},{1,2},{2,3},{3,0},{4,5},{5,6},{6,7},{7,4},{8,9},{9,10},{10,1... | collective-permute-start | bytes 1572872 | tf_op jit(solution)/shard_map/ppermute | solution.py:38
  451.1 39.3 %collective-permute-start.81 = (bf16[256,1024]{1,0:T(8,128)(2,1)}, bf16[256,1024]{1,0:T(8,128)(2,1)}, u32[]{:S(2)}, u32[]{:S(2)}) collective-permute-start(bf16[256,1024]{1,0:T(8,128)(2,1)} %slice.593), channel_id=1, source_target_pairs={{0,16},{4,20},{8,24},{12,28},{16,0},{20,4},{24,8},{28,12},{1,17},{... | collective-permute-start | bytes 1572872 | tf_op jit(solution)/shard_map/ppermute | solution.py:72
  473.5 18.2 %collective-permute-start.80 = (bf16[256,1024]{1,0:T(8,128)(2,1)}, bf16[256,1024]{1,0:T(8,128)(2,1)}, u32[]{:S(2)}, u32[]{:S(2)}) collective-permute-start(bf16[256,1024]{1,0:T(8,128)(2,1)} %slice.591), channel_id=1, source_target_pairs={{0,8},{4,12},{8,0},{12,4},{16,24},{20,28},{24,16},{28,20},{1,9},{5... | collective-permute-start | bytes 1572872 | tf_op jit(solution)/shard_map/ppermute | solution.py:72
  510.5 20.3 %collective-permute-start.63 = (bf16[256,1024]{1,0:T(8,128)(2,1)}, bf16[256,1024]{1,0:T(8,128)(2,1)}, u32[]{:S(2)}, u32[]{:S(2)}) collective-permute-start(bf16[256,1024]{1,0:T(8,128)(2,1)} %add_convert_fusion.13), channel_id=1, source_target_pairs={{0,8},{4,12},{8,0},{12,4},{16,24},{20,28},{24,16},{28,20},{1,9},{5... | collective-permute-start | bytes 1572872 | tf_op jit(solution)/shard_map/ppermute | solution.py:72
  514.5 32.1 %collective-permute-start.60 = (bf16[256,1024]{1,0:T(8,128)(2,1)}, bf16[256,1024]{1,0:T(8,128)(2,1)}, u32[]{:S(2)}, u32[]{:S(2)}) collective-permute-start(bf16[256,1024]{1,0:T(8,128)(2,1)} %add_convert_fusion.18), channel_id=1, source_target_pairs={{0,16},{4,20},{8,24},{12,28},{16,0},{20,4},{24,8},{28,12},{1,17},{... | collective-permute-start | bytes 1572872 | tf_op jit(solution)/shard_map/ppermute | solution.py:72
  530.2 20.8 %collective-permute-start.54 = (bf16[256,1024]{1,0:T(8,128)(2,1)}, bf16[256,1024]{1,0:T(8,128)(2,1)S(1)}, u32[]{:S(2)}, u32[]{:S(2)}) collective-permute-start(bf16[256,1024]{1,0:T(8,128)(2,1)} %add_convert_fusion.23), channel_id=1, source_target_pairs={{0,16},{4,20},{8,24},{12,28},{16,0},{20,4},{24,8},{28,12},{1,17},{... | collective-permute-start | bytes 1572872 | tf_op jit(solution)/shard_map/ppermute | solution.py:72
  533.2 25.1 %collective-permute-start.64 = (bf16[256,1024]{1,0:T(8,128)(2,1)}, bf16[256,1024]{1,0:T(8,128)(2,1)S(1)}, u32[]{:S(2)}, u32[]{:S(2)}) collective-permute-start(bf16[256,1024]{1,0:T(8,128)(2,1)} %add_convert_fusion.12), channel_id=1, source_target_pairs={{0,16},{4,20},{8,24},{12,28},{16,0},{20,4},{24,8},{28,12},{1,17},{... | collective-permute-start | bytes 1572872 | tf_op jit(solution)/shard_map/ppermute | solution.py:72
  535.9 15.4 %collective-permute-start.55 = (bf16[256,1024]{1,0:T(8,128)(2,1)}, bf16[256,1024]{1,0:T(8,128)(2,1)}, u32[]{:S(2)}, u32[]{:S(2)}) collective-permute-start(bf16[256,1024]{1,0:T(8,128)(2,1)} %add_convert_fusion.22), channel_id=1, source_target_pairs={{0,8},{4,12},{8,0},{12,4},{16,24},{20,28},{24,16},{28,20},{1,9},{5... | collective-permute-start | bytes 1572872 | tf_op jit(solution)/shard_map/ppermute | solution.py:72
  546.5 16.3 %collective-permute-start.62 = (bf16[256,1024]{1,0:T(8,128)(2,1)}, bf16[256,1024]{1,0:T(8,128)(2,1)}, u32[]{:S(2)}, u32[]{:S(2)}) collective-permute-start(bf16[256,1024]{1,0:T(8,128)(2,1)} %get-tuple-element.141), channel_id=1, source_target_pairs={{0,4},{4,0},{8,12},{12,8},{16,20},{20,16},{24,28},{28,24},{1,5},{5... | collective-permute-start | bytes 1572872 | tf_op jit(solution)/shard_map/ppermute | solution.py:72
  549.1 16.5 %collective-permute-start.61 = (bf16[256,1024]{1,0:T(8,128)(2,1)}, bf16[256,1024]{1,0:T(8,128)(2,1)}, u32[]{:S(2)}, u32[]{:S(2)}) collective-permute-start(bf16[256,1024]{1,0:T(8,128)(2,1)} %add_convert_fusion.17), channel_id=1, source_target_pairs={{0,8},{4,12},{8,0},{12,4},{16,24},{20,28},{24,16},{28,20},{1,9},{5... | collective-permute-start | bytes 1572872 | tf_op jit(solution)/shard_map/ppermute | solution.py:72
  551.1 14.4 %collective-permute-start.59 = (bf16[256,1024]{1,0:T(8,128)(2,1)}, bf16[256,1024]{1,0:T(8,128)(2,1)}, u32[]{:S(2)}, u32[]{:S(2)}) collective-permute-start(bf16[256,1024]{1,0:T(8,128)(2,1)} %get-tuple-element.137), channel_id=1, source_target_pairs={{0,4},{4,0},{8,12},{12,8},{16,20},{20,16},{24,28},{28,24},{1,5},{5... | collective-permute-start | bytes 1572872 | tf_op jit(solution)/shard_map/ppermute | solution.py:72
  600.5 16.3 %collective-permute-start.68 = (bf16[128,2048]{1,0:T(8,128)(2,1)S(1)}, bf16[128,2048]{1,0:T(8,128)(2,1)S(1)}, u32[]{:S(2)}, u32[]{:S(2)}) collective-permute-start(bf16[128,2048]{1,0:T(8,128)(2,1)S(1)} %fusion.16), channel_id=1, source_target_pairs={{0,1},{1,2},{2,3},{3,0},{4,5},{5,6},{6,7},{7,4},{8,9},{9,10},{10,1... | collective-permute-start | bytes 1572872 | tf_op jit(solution)/shard_map/ppermute | solution.py:38
  604.0 13.7 %collective-permute-start.74 = (bf16[1024,512]{1,0:T(8,128)(2,1)S(1)}, bf16[1024,512]{1,0:T(8,128)(2,1)S(1)}, u32[]{:S(2)}, u32[]{:S(2)}) collective-permute-start(bf16[1024,512]{1,0:T(8,128)(2,1)S(1)} %pad_maximum_fusion.6), channel_id=1, source_target_pairs={{0,4},{4,0},{8,12},{12,8},{16,20},{20,16},{24,28},{28,24},{1,5},{5... | collective-permute-start | bytes 3145736 | tf_op jit(solution)/shard_map/ppermute | solution.py:72
  606.1 13.9 %collective-permute-start.71 = (bf16[1024,512]{1,0:T(8,128)(2,1)S(1)}, bf16[1024,512]{1,0:T(8,128)(2,1)S(1)}, u32[]{:S(2)}, u32[]{:S(2)}) collective-permute-start(bf16[1024,512]{1,0:T(8,128)(2,1)S(1)} %pad_maximum_fusion.5), channel_id=1, source_target_pairs={{0,4},{4,0},{8,12},{12,8},{16,20},{20,16},{24,28},{28,24},{1,5},{5... | collective-permute-start | bytes 3145736 | tf_op jit(solution)/shard_map/ppermute | solution.py:72
  617.6 15.2 %collective-permute-start.69 = (bf16[128,2048]{1,0:T(8,128)(2,1)S(1)}, bf16[128,2048]{1,0:T(8,128)(2,1)S(1)}, u32[]{:S(2)}, u32[]{:S(2)}) collective-permute-start(bf16[128,2048]{1,0:T(8,128)(2,1)S(1)} %add_convert_fusion.9), channel_id=1, source_target_pairs={{0,1},{1,2},{2,3},{3,0},{4,5},{5,6},{6,7},{7,4},{8,9},{9,10},{10,1... | collective-permute-start | bytes 1572872 | tf_op jit(solution)/shard_map/ppermute | solution.py:38
  618.0 21.7 %collective-permute-start.75 = (bf16[512,512]{1,0:T(8,128)(2,1)S(1)}, bf16[512,512]{1,0:T(8,128)(2,1)S(1)}, u32[]{:S(2)}, u32[]{:S(2)}) collective-permute-start(bf16[512,512]{1,0:T(8,128)(2,1)S(1)} %slice.570), channel_id=1, source_target_pairs={{0,8},{4,12},{8,0},{12,4},{16,24},{20,28},{24,16},{28,20},{1,9},{5... | collective-permute-start | bytes 1572872 | tf_op jit(solution)/shard_map/ppermute | solution.py:72
  620.3 21.2 %collective-permute-start.72 = (bf16[512,512]{1,0:T(8,128)(2,1)S(1)}, bf16[512,512]{1,0:T(8,128)(2,1)S(1)}, u32[]{:S(2)}, u32[]{:S(2)}) collective-permute-start(bf16[512,512]{1,0:T(8,128)(2,1)S(1)} %slice.566), channel_id=1, source_target_pairs={{0,16},{4,20},{8,24},{12,28},{16,0},{20,4},{24,8},{28,12},{1,17},{... | collective-permute-start | bytes 1572872 | tf_op jit(solution)/shard_map/ppermute | solution.py:72
  633.6 14.3 %collective-permute-start.70 = (bf16[128,2048]{1,0:T(8,128)(2,1)S(1)}, bf16[128,2048]{1,0:T(8,128)(2,1)S(1)}, u32[]{:S(2)}, u32[]{:S(2)}) collective-permute-start(bf16[128,2048]{1,0:T(8,128)(2,1)S(1)} %add_convert_fusion.8), channel_id=1, source_target_pairs={{0,1},{1,2},{2,3},{3,0},{4,5},{5,6},{6,7},{7,4},{8,9},{9,10},{10,1... | collective-permute-start | bytes 1572872 | tf_op jit(solution)/shard_map/ppermute | solution.py:38
  (137 other events, 1115.6 us)
Sparse Core Ops, SparseCore 0:
  337.8 143.0 reduce-scatter.2
  595.4 60.7 reduce-scatter.4

commit v2 on v1

--- a/solution.py
+++ b/solution.py
@@ -38,10 +38,10 @@
     return lax.ppermute(x, "fsdp", [(i, (i + by) % n) for i in range(n)])
 
 
-def ring_gather(x, n, around=None):
+def ring_gather(x, n):
     slots = [x]
     for _ in range(n - 1):
-        slots.append(shift(slots[-1], around or n, 1))
+        slots.append(shift(slots[-1], n, 1))
     return slots
 
 
@@ -555,13 +555,15 @@
     attn_gain_part = jnp.sum(state_grad * attn_out * attn_rms[:, None], axis=0)
     attn_grad_b = norm_back(attn_out, attn_rms, attn_gain[None, :], state_grad).astype(BF)
     gate_up_part = contract_rows(
-        jnp.concatenate(state_slots[:-1] + [gate(state_slots[-1], *marks[0])]),
+        jnp.concatenate(state_slots),
         jnp.concatenate([jnp.concatenate(gate_grads), jnp.concatenate(up_grads)], axis=1),
     ).astype(BF)
     gate_up_sum = ctx_scatter(gate_up_part)
     first_hop = shift(attn_grad_b, nf, 1)
-    proj_slots = [attn_grad_b] + ring_gather(first_hop, nf - 1, around=nf)
-    proj_slots[-1] = gate(proj_slots[-1], *marks[1])
+    proj_slots = [attn_grad_b, first_hop]
+    for s in range(2, nf):
+        got = shift(proj_slots[-1], nf, 1)
+        proj_slots.append(gate(got, *marks[0]) if s == 2 else got)
     mixture_grad_b = jnp.concatenate(
         [contract_cols(x, output_weight).astype(BF) for x in proj_slots]
     )
@@ -579,21 +581,17 @@
     for gi, group in enumerate(groups[::-1]):
         starts, kv = group_inputs(group)
         if gi:
-            dq = gate(dq, *waits[gi - 1])
+            dq = gate(dq, *waits[gi - 1], *(marks[1] if gi == 1 else []))
         dq, *out = attend_back(
             starts, query_rot, mixture_grad_b, mixture, log_total, qpos, kv, dq, heads, half
         )
         for m, a, b in zip(group, out[: len(group)], out[len(group) :]):
             sums[0][m], sums[1][m] = a, b
         waits.append([send(i, m) for i in range(2) for m in group if m & 1])
-    hops = []
     for far in range(max(distance(m) for m in range(nc)), 0, -1):
         for i in range(2):
             for m in [m for m in sums[i] if distance(m) == far]:
-                got = send(i, m)
-                if m == orders[i][-1]:
-                    hops.append(got)
-    dq = gate(dq, *hops)
+                send(i, m)
     own_a, own_b = sums[0][0], sums[1][0]
 
     def unit_full(x):
@@ -629,9 +627,8 @@
     q_part = contract_rows(x_rows, jnp.concatenate(query_grads)).astype(BF)
     o_part = contract_rows(jnp.concatenate(proj_slots), mixture_b).astype(BF)
     qo_part = jnp.concatenate([q_part, o_part], axis=1)
-    qo_part, gate_up_sum, own_a, own_b = lax.optimization_barrier(
-        (qo_part, gate_up_sum, own_a, own_b)
-    )
+    gate_up_sum, own_a, own_b = lax.optimization_barrier((gate_up_sum, own_a, own_b))
+    qo_part, gate_up_sum = lax.optimization_barrier((qo_part, gate_up_sum))
     qo_grad = ctx_scatter(qo_part).astype(F32)
     query_grad, output_grad = qo_grad[:, :units], qo_grad[:, units:].T
 

time: 672 us -> 653 us (0.972)
  waiting for transfers between devices: 279 us -> 256 us
    ppermute x46, waiting for transfers between devices: 73 us -> 50.2 us  [swap(): return lax.ppermute(x, 'ctx', [(i, i ^ bit) for i in range(n)])]
    unnamed x205 -> x259, local copies, waits for them, and re-layouts: 17.1 us -> 14.3 us
  transfers between devices with their start and end apart: 84 -> 84, of which waited for: 38 -> 38; matrix products, arithmetic and copies ran while one was open for 26% -> 29% of each run, Pallas kernels for 10% -> 11%
where the time goes in v2:
time: 653 us; the launch traced here: 647 us
  waiting for transfers between devices  256 us (39%)
  matrix products  139 us (21%)
  Pallas kernels  86.2 us (13%)
  other arithmetic  57.7 us (9%)
  starting transfers between devices  55.1 us (8%)
  local copies, waits for them, and re-layouts  36.3 us (6%)
  between operations  16.8 us (3%)
    ppermute x36, waiting for transfers between devices, shift(): return lax.ppermute(x, 'fsdp', [(i, (i + by) % n) for i in range(n)])  204 us
    dot_general x28, matrix products, contract_cols(): lax.dot_general(left, right, (((1,), (1,)), ((), ())), preferred_element_...  72.6 us
    ppermute x46, waiting for transfers between devices, swap(): return lax.ppermute(x, 'ctx', [(i, i ^ bit) for i in range(n)])  50.2 us
    pallas_call x4, Pallas kernels, attend_back(): pl.pallas_call(functools.partial(bwd_kernel, np_, slots, heads, first), g...  41.8 us
    dot_general x28, matrix products, mm(): return jnp.dot(left, right, preferred_element_type=F32)  38.7 us
    ppermute x46, starting transfers between devices, swap(): return lax.ppermute(x, 'ctx', [(i, i ^ bit) for i in range(n)])  29.7 us
    pallas_call x4, Pallas kernels, attend(): pl.pallas_call(functools.partial(fwd_kernel, np_, slots, first, last), gr...  28.9 us
    dot_general x7, matrix products, contract_rows(): lax.dot_general(left, right, (((0,), (0,)), ((), ())), preferred_element_...  28 us
  transfers between devices with their start and end apart: 84, of which 38 were waited for; matrix products, arithmetic and copies ran while one was open for 29% of the time, Pallas kernels for 11%

profile of v2, /device:TPU:0, one launch (start us, length us, event | category | flops | bytes accessed | tf_op | source)
XLA Modules:
  0.0 647.4 jit_solution(14583720284047875821)
XLA Ops:
  18.4 6.1 collective-permute-done
  48.0 8.9 %collective-permute-done.2 = bf16[128,2048]{1,0:T(8,128)(2,1)S(1)} collective-permute-done((bf16[128,2048]{1,0:T(8,128)(2,1)S(1)}, bf16[128,2048]{1,0:T(8,128)(2,1)S(1)}, u32[]{:S(2)}, u32[]{:S(2)}) %collective-permute-start.2) | collective-permute-done | bytes 524320 | tf_op jit(solution)/shard_map/ppermute | solution.py:38
  69.6 5.9 shard_map.237
  80.4 10.4 %collective-permute-done.12.refs_3_.refs_7_.refs_6_.refs_10_ = bf16[256,1024]{1,0:T(8,128)(2,1)} collective-permute-done((bf16[256,1024]{1,0:T(8,128)(2,1)}, bf16[256,1024]{1,0:T(8,128)(2,1)}, u32[]{:S(2)}, u32[]{:S(2)}) %collective-permute-start.12) | collective-permute-done | bytes 524320 | tf_op jit(solution)/shard_map/ppermute | solution.py:72
  90.8 10.7 %collective-permute-done.17.refs_5_.refs_9_.refs_8_.refs_12_ = bf16[256,1024]{1,0:T(8,128)(2,1)} collective-permute-done((bf16[256,1024]{1,0:T(8,128)(2,1)}, bf16[256,1024]{1,0:T(8,128)(2,1)}, u32[]{:S(2)}, u32[]{:S(2)}) %collective-permute-start.17) | collective-permute-done | bytes 524320 | tf_op jit(solution)/shard_map/ppermute | solution.py:72
  101.5 6.9 %shard_map.238 = (f32[4,1,512]{2,1,0:T(1,128)}, f32[4,1,512]{2,1,0:T(1,128)}, f32[512,512]{1,0:T(8,128)}) custom-call(s32[8]{0:T(128)} %pad_add_fusion.4.refs_0_, bf16[512,512]{1,0:T(8,128)(2,1)} %get-tuple-element.86.refs_1_, s32[1,512]{1,0:T(1,128)} %bitcast.295, bf16[256,1024]{1,0:T(8,128)(2,1)} %get-tuple-element.87.refs_3_.refs_7_.refs_6_.refs_10_, ...), custom_call_target="tpu_custom_call" | custom-call | flops 2147483648 | bytes 2097152 | tf_op jit(solution)/shard_map/pallas_call | solution.py:234
  112.2 7.2 %shard_map.239 = (f32[4,1,512]{2,1,0:T(1,128)}, f32[4,1,512]{2,1,0:T(1,128)}, f32[512,512]{1,0:T(8,128)}) custom-call(s32[8]{0:T(128)} %pad_add_fusion.5.refs_0_, bf16[512,512]{1,0:T(8,128)(2,1)} %get-tuple-element.86.refs_1_, s32[1,512]{1,0:T(1,128)} %bitcast.296, bf16[256,1024]{1,0:T(8,128)(2,1)} %collective-permute-done.12.refs_3_.refs_7_.refs_6_.refs_10_, ...), custom_call_target="tpu_custom_call" | custom-call | flops 2147483648 | bytes 2097152 | tf_op jit(solution)/shard_map/pallas_call | solution.py:234
  119.4 3.6 collective-permute-done.21.refs_5_.refs_9_.refs_8_.refs_12_
  125.9 7.2 %shard_map.240 = (f32[4,1,512]{2,1,0:T(1,128)}, f32[4,1,512]{2,1,0:T(1,128)}, f32[512,512]{1,0:T(8,128)}) custom-call(s32[8]{0:T(128)} %pad_add_fusion.6.refs_0_, bf16[512,512]{1,0:T(8,128)(2,1)} %get-tuple-element.86.refs_1_, s32[1,512]{1,0:T(1,128)} %bitcast.297, bf16[256,1024]{1,0:T(8,128)(2,1)} %collective-permute-done.23.refs_3_.refs_7_.refs_6_.refs_10_, ...), custom_call_target="tpu_custom_call" | custom-call | flops 2147483648 | bytes 2097152 | tf_op jit(solution)/shard_map/pallas_call | solution.py:234
  133.2 7.5 %shard_map.241 = (f32[512,512]{1,0:T(8,128)}, bf16[512,512]{1,0:T(8,128)(2,1)}, f32[4,1,512]{2,1,0:T(1,128)}) custom-call(s32[8]{0:T(128)} %pad_add_fusion.3.refs_0_, bf16[512,512]{1,0:T(8,128)(2,1)} %get-tuple-element.86.refs_1_, s32[1,512]{1,0:T(1,128)} %bitcast.298, bf16[256,1024]{1,0:T(8,128)(2,1)} %collective-permute-done.15.refs_3_.refs_7_.refs_6_.refs_10_, ...), custom_call_target="tpu_custom_call" | custom-call | flops 2147483648 | bytes 2097152 | tf_op jit(solution)/shard_map/pallas_call | solution.py:234
  143.0 16.1 %collective-permute-done.26 = bf16[128,2048]{1,0:T(8,128)(2,1)S(1)} collective-permute-done((bf16[128,2048]{1,0:T(8,128)(2,1)S(1)}, bf16[128,2048]{1,0:T(8,128)(2,1)S(1)}, u32[]{:S(2)}, u32[]{:S(2)}) %collective-permute-start.26) | collective-permute-done | bytes 524320 | tf_op jit(solution)/shard_map/ppermute | solution.py:38
  159.7 15.3 %collective-permute-done.27 = bf16[128,2048]{1,0:T(8,128)(2,1)S(1)} collective-permute-done((bf16[128,2048]{1,0:T(8,128)(2,1)S(1)}, bf16[128,2048]{1,0:T(8,128)(2,1)S(1)}, u32[]{:S(2)}, u32[]{:S(2)}) %collective-permute-start.27) | collective-permute-done | bytes 524320 | tf_op jit(solution)/shard_map/ppermute | solution.py:38
  175.5 14.4 %collective-permute-done.28 = bf16[128,2048]{1,0:T(8,128)(2,1)S(1)} collective-permute-done((bf16[128,2048]{1,0:T(8,128)(2,1)S(1)}, bf16[128,2048]{1,0:T(8,128)(2,1)S(1)}, u32[]{:S(2)}, u32[]{:S(2)}) %collective-permute-start.28) | collective-permute-done | bytes 524320 | tf_op jit(solution)/shard_map/ppermute | solution.py:38
  192.6 12.2 %collective-permute-done.29 = bf16[128,2048]{1,0:T(8,128)(2,1)S(1)} collective-permute-done((bf16[128,2048]{1,0:T(8,128)(2,1)S(1)}, bf16[128,2048]{1,0:T(8,128)(2,1)S(1)}, u32[]{:S(2)}, u32[]{:S(2)}) %collective-permute-start.29) | collective-permute-done | bytes 524320 | tf_op jit(solution)/shard_map/ppermute | solution.py:38
  210.0 11.4 %collective-permute-done.31 = bf16[128,2048]{1,0:T(8,128)(2,1)S(1)} collective-permute-done((bf16[128,2048]{1,0:T(8,128)(2,1)S(1)}, bf16[128,2048]{1,0:T(8,128)(2,1)S(1)}, u32[]{:S(2)}, u32[]{:S(2)}) %collective-permute-start.31) | collective-permute-done | bytes 524320 | tf_op jit(solution)/shard_map/ppermute | solution.py:38
  225.1 7.5 %collective-permute-done.30 = bf16[128,2048]{1,0:T(8,128)(2,1)S(1)} collective-permute-done((bf16[128,2048]{1,0:T(8,128)(2,1)S(1)}, bf16[128,2048]{1,0:T(8,128)(2,1)S(1)}, u32[]{:S(2)}, u32[]{:S(2)}) %collective-permute-start.30) | collective-permute-done | bytes 524320 | tf_op jit(solution)/shard_map/ppermute | solution.py:38
  234.1 9.7 %collective-permute-done.33 = bf16[128,2048]{1,0:T(8,128)(2,1)S(1)} collective-permute-done((bf16[128,2048]{1,0:T(8,128)(2,1)S(1)}, bf16[128,2048]{1,0:T(8,128)(2,1)S(1)}, u32[]{:S(2)}, u32[]{:S(2)}) %collective-permute-start.33) | collective-permute-done | bytes 524320 | tf_op jit(solution)/shard_map/ppermute | solution.py:38
  253.7 9.4 %collective-permute-done.34 = bf16[128,2048]{1,0:T(8,128)(2,1)S(1)} collective-permute-done((bf16[128,2048]{1,0:T(8,128)(2,1)S(1)}, bf16[128,2048]{1,0:T(8,128)(2,1)S(1)}, u32[]{:S(2)}, u32[]{:S(2)}) %collective-permute-start.34) | collective-permute-done | bytes 524320 | tf_op jit(solution)/shard_map/ppermute | solution.py:38
  266.4 4.0 multiply_convert_fusion.6
  270.5 8.0 %collective-permute-done.35 = bf16[128,2048]{1,0:T(8,128)(2,1)S(1)} collective-permute-done((bf16[128,2048]{1,0:T(8,128)(2,1)S(1)}, bf16[128,2048]{1,0:T(8,128)(2,1)S(1)}, u32[]{:S(2)}, u32[]{:S(2)}) %collective-permute-start.35) | collective-permute-done | bytes 524320 | tf_op jit(solution)/shard_map/ppermute | solution.py:38
  278.8 4.0 multiply_convert_fusion.4
  282.9 9.4 %collective-permute-done.37 = bf16[128,2048]{1,0:T(8,128)(2,1)S(1)} collective-permute-done((bf16[128,2048]{1,0:T(8,128)(2,1)S(1)}, bf16[128,2048]{1,0:T(8,128)(2,1)S(1)}, u32[]{:S(2)}, u32[]{:S(2)}) %collective-permute-start.37) | collective-permute-done | bytes 524320 | tf_op jit(solution)/shard_map/ppermute | solution.py:38
  292.4 4.0 multiply_convert_fusion.2
  296.3 7.0 %collective-permute-done.39 = bf16[128,2048]{1,0:T(8,128)(2,1)S(1)} collective-permute-done((bf16[128,2048]{1,0:T(8,128)(2,1)S(1)}, bf16[128,2048]{1,0:T(8,128)(2,1)S(1)}, u32[]{:S(2)}, u32[]{:S(2)}) %collective-permute-start.39) | collective-permute-done | bytes 524320 | tf_op jit(solution)/shard_map/ppermute | solution.py:38
  303.3 4.0 multiply_convert_fusion
  307.3 14.9 %convolution_convert_fusion = bf16[2048,4096]{1,0:T(8,128)(2,1)} fusion(bf16[128,2048]{1,0:T(8,128)(2,1)} %get-tuple-element.220, bf16[128,2048]{1,0:T(8,128)(2,1)} %get-tuple-element.130, bf16[128,2048]{1,0:T(8,128)(2,1)} %get-tuple-element.129, bf16[128,2048]{1,0:T(8,128)(2,1)} %get-tuple-element.107, bf16[128,2048]{1,0:T(8,128)(2,1)} %get-tuple-element.221, ...), kind=kOutput, calls=%fused_computation | convolution fusion | flops 8640266240 | bytes 23068672 | tf_op jit(solution)/shard_map/dot_general | solution.py:26
  328.4 7.9 %fusion.126 = f32[128,2048]{1,0:T(8,128)S(1)} fusion(bf16[128,2048]{1,0:T(8,128)(2,1)S(1)} %copy-done.73, bf16[2048,2048]{1,0:T(8,128)(2,1)} %param.24), kind=kOutput, calls=%fused_computation.365 | convolution fusion | flops 1073741824 | bytes 9961472 | tf_op jit(solution)/shard_map/dot_general | solution.py:30
  336.4 8.1 %fusion.15 = bf16[128,2048]{1,0:T(8,128)(2,1)S(1)} fusion(f32[128,2048]{1,0:T(8,128)S(1)} %fusion.126, bf16[128,2048]{1,0:T(8,128)(2,1)S(1)} %copy-done.71, bf16[2048,2048]{1,0:T(8,128)(2,1)} %param.25), kind=kOutput, calls=%fused_computation.38 | convolution fusion | flops 1074266112 | bytes 10485760 | tf_op jit(solution)/shard_map/dot_general | solution.py:30
  350.5 9.2 %collective-permute-done.36 = bf16[128,2048]{1,0:T(8,128)(2,1)S(1)} collective-permute-done((bf16[128,2048]{1,0:T(8,128)(2,1)S(1)}, bf16[128,2048]{1,0:T(8,128)(2,1)S(1)}, u32[]{:S(2)}, u32[]{:S(2)}) %collective-permute-start.36) | collective-permute-done | bytes 524320 | tf_op jit(solution)/shard_map/ppermute | solution.py:38
  368.5 8.7 %collective-permute-done.38 = bf16[128,2048]{1,0:T(8,128)(2,1)S(1)} collective-permute-done((bf16[128,2048]{1,0:T(8,128)(2,1)S(1)}, bf16[128,2048]{1,0:T(8,128)(2,1)S(1)}, u32[]{:S(2)}, u32[]{:S(2)}) %collective-permute-start.38) | collective-permute-done | bytes 524320 | tf_op jit(solution)/shard_map/ppermute | solution.py:38
  389.5 3.2 multiply_reduce_fusion
  397.8 12.3 %collective-permute-done.41 = bf16[128,2048]{1,0:T(8,128)(2,1)} collective-permute-done((bf16[128,2048]{1,0:T(8,128)(2,1)}, bf16[128,2048]{1,0:T(8,128)(2,1)}, u32[]{:S(2)}, u32[]{:S(2)}) %collective-permute-start.41) | collective-permute-done | bytes 524320 | tf_op jit(solution)/shard_map/ppermute | solution.py:38
  413.0 3.4 add_convert_fusion.1
  416.4 8.9 %collective-permute-done.42 = bf16[128,2048]{1,0:T(8,128)(2,1)S(1)} collective-permute-done((bf16[128,2048]{1,0:T(8,128)(2,1)}, bf16[128,2048]{1,0:T(8,128)(2,1)S(1)}, u32[]{:S(2)}, u32[]{:S(2)}) %collective-permute-start.42) | collective-permute-done | bytes 524320 | tf_op jit(solution)/shard_map/ppermute | solution.py:38
  431.2 8.3 %collective-permute-done.45 = bf16[128,2048]{1,0:T(8,128)(2,1)S(1)} collective-permute-done((bf16[128,2048]{1,0:T(8,128)(2,1)S(1)}, bf16[128,2048]{1,0:T(8,128)(2,1)S(1)}, u32[]{:S(2)}, u32[]{:S(2)}) %collective-permute-start.45) | collective-permute-done | bytes 524320 | tf_op jit(solution)/shard_map/ppermute | solution.py:38
  441.2 10.4 %shard_map.242 = (f32[512,512]{1,0:T(8,128)}, bf16[256,1024]{1,0:T(8,128)(2,1)}, bf16[256,1024]{1,0:T(8,128)(2,1)}, bf16[256,1024]{1,0:T(8,128)(2,1)}, bf16[256,1024]{1,0:T(8,128)(2,1)}) custom-call(s32[8]{0:T(128)} %pad_add_fusion.3.refs_0_, bf16[512,512]{1,0:T(8,128)(2,1)} %get-tuple-element.86.refs_1_, bf16[512,512]{1,0:T(8,128)(2,1)} %pad_maximum_fusion.7.refs_2_, ...), custom_call_target="tpu_custom_call" | custom-call | flops 5368709120 | bytes 4194304 | tf_op jit(solution)/shard_map/pallas_call | solution.py:306
  452.1 4.4 convolution_convert_fusion.5
  464.9 10.4 %shard_map.243 = (f32[512,512]{1,0:T(8,128)}, bf16[256,1024]{1,0:T(8,128)(2,1)}, bf16[256,1024]{1,0:T(8,128)(2,1)}, bf16[256,1024]{1,0:T(8,128)(2,1)}, bf16[256,1024]{1,0:T(8,128)(2,1)}) custom-call(s32[8]{0:T(128)} %pad_add_fusion.6.refs_0_, bf16[512,512]{1,0:T(8,128)(2,1)} %get-tuple-element.86.refs_1_, bf16[512,512]{1,0:T(8,128)(2,1)} %pad_maximum_fusion.7.refs_2_, ...), custom_call_target="tpu_custom_call" | custom-call | flops 5368709120 | bytes 4194304 | tf_op jit(solution)/shard_map/pallas_call | solution.py:306
  489.3 10.5 %shard_map.244 = (f32[512,512]{1,0:T(8,128)}, bf16[256,1024]{1,0:T(8,128)(2,1)}, bf16[256,1024]{1,0:T(8,128)(2,1)}, bf16[256,1024]{1,0:T(8,128)(2,1)}, bf16[256,1024]{1,0:T(8,128)(2,1)}) custom-call(s32[8]{0:T(128)} %pad_add_fusion.5.refs_0_, bf16[512,512]{1,0:T(8,128)(2,1)} %get-tuple-element.86.refs_1_, bf16[512,512]{1,0:T(8,128)(2,1)} %pad_maximum_fusion.7.refs_2_, ...), custom_call_target="tpu_custom_call" | custom-call | flops 5368709120 | bytes 4194304 | tf_op jit(solution)/shard_map/pallas_call | solution.py:306
  506.7 10.6 %shard_map.245 = (f32[512,512]{1,0:T(8,128)}, bf16[256,1024]{1,0:T(8,128)(2,1)}, bf16[256,1024]{1,0:T(8,128)(2,1)}, bf16[256,1024]{1,0:T(8,128)(2,1)}, bf16[256,1024]{1,0:T(8,128)(2,1)}) custom-call(s32[8]{0:T(128)} %pad_add_fusion.4.refs_0_, bf16[512,512]{1,0:T(8,128)(2,1)} %get-tuple-element.86.refs_1_, bf16[512,512]{1,0:T(8,128)(2,1)} %pad_maximum_fusion.7.refs_2_, ...), custom_call_target="tpu_custom_call" | custom-call | flops 5368709120 | bytes 4194304 | tf_op jit(solution)/shard_map/pallas_call | solution.py:306
  517.3 4.9 shard_map.246
  543.5 3.5 fusion.133
  553.4 4.8 collective-permute-done.60
  560.7 4.6 shard_map.247
  571.1 4.1 fusion.111
  600.8 12.2 %collective-permute-done.69 = bf16[128,2048]{1,0:T(8,128)(2,1)S(1)} collective-permute-done((bf16[128,2048]{1,0:T(8,128)(2,1)S(1)}, bf16[128,2048]{1,0:T(8,128)(2,1)S(1)}, u32[]{:S(2)}, u32[]{:S(2)}) %collective-permute-start.69) | collective-permute-done | bytes 524320 | tf_op jit(solution)/shard_map/ppermute | solution.py:38
  613.9 6.8 %collective-permute-done.75 = bf16[512,512]{1,0:T(8,128)(2,1)S(1)} collective-permute-done((bf16[512,512]{1,0:T(8,128)(2,1)S(1)}, bf16[512,512]{1,0:T(8,128)(2,1)S(1)}, u32[]{:S(2)}, u32[]{:S(2)}) %collective-permute-start.75) | collective-permute-done | bytes 524320 | tf_op jit(solution)/shard_map/ppermute | solution.py:72
  623.2 5.1 collective-permute-done.70
  (594 shorter events, 242.5 us)
Async XLA Ops:
  7.2 553.4 %reduce-scatter.3.cloned.1.call-start = ((), (), s32[]{:S(2)}) async-start(), calls=%async_computation.2 | async-start | bytes 18874368 | tf_op jit(solution)/shard_map/reduce_scatter | solution.py:509
  7.3 17.3 %collective-permute-start = (bf16[128,2048]{1,0:T(8,128)(2,1)}, bf16[128,2048]{1,0:T(8,128)(2,1)S(1)}, u32[]{:S(2)}, u32[]{:S(2)}) collective-permute-start(bf16[128,2048]{1,0:T(8,128)(2,1)} %param.14), channel_id=1, source_target_pairs={{0,1},{1,2},{2,3},{3,0},{4,5},{5,6},{6,7},{7,4},{8,9},{9,10},{10,1... | collective-permute-start | bytes 1572872 | tf_op jit(solution)/shard_map/ppermute | solution.py:38
  29.0 14.4 %collective-permute-start.1 = (bf16[128,2048]{1,0:T(8,128)(2,1)S(1)}, bf16[128,2048]{1,0:T(8,128)(2,1)S(1)}, u32[]{:S(2)}, u32[]{:S(2)}) collective-permute-start(bf16[128,2048]{1,0:T(8,128)(2,1)S(1)} %collective-permute-done), channel_id=1, source_target_pairs={{0,1},{1,2},{2,3},{3,0},{4,5},{5,6},{6,7},{7,4},{8,9},{9,10},{10,1... | collective-permute-start | bytes 1572872 | tf_op jit(solution)/shard_map/ppermute | solution.py:38
  43.4 13.5 %collective-permute-start.2 = (bf16[128,2048]{1,0:T(8,128)(2,1)S(1)}, bf16[128,2048]{1,0:T(8,128)(2,1)S(1)}, u32[]{:S(2)}, u32[]{:S(2)}) collective-permute-start(bf16[128,2048]{1,0:T(8,128)(2,1)S(1)} %collective-permute-done.1), channel_id=1, source_target_pairs={{0,1},{1,2},{2,3},{3,0},{4,5},{5,6},{6,7},{7,4},{8,9},{9,10},{10,1... | collective-permute-start | bytes 1572872 | tf_op jit(solution)/shard_map/ppermute | solution.py:38
  75.6 15.2 %collective-permute-start.12 = (bf16[256,1024]{1,0:T(8,128)(2,1)}, bf16[256,1024]{1,0:T(8,128)(2,1)}, u32[]{:S(2)}, u32[]{:S(2)}) collective-permute-start(bf16[256,1024]{1,0:T(8,128)(2,1)} %get-tuple-element.87.refs_3_.refs_7_.refs_6_.refs_10_), channel_id=1, source_target_pairs={{0,8},{4,12},{8,0},{12,4},{16,24},{20,28},{24,16},{28,20},{1,9},{5... | collective-permute-start | bytes 1572872 | tf_op jit(solution)/shard_map/ppermute | solution.py:72
  76.8 24.7 %collective-permute-start.17 = (bf16[256,1024]{1,0:T(8,128)(2,1)}, bf16[256,1024]{1,0:T(8,128)(2,1)}, u32[]{:S(2)}, u32[]{:S(2)}) collective-permute-start(bf16[256,1024]{1,0:T(8,128)(2,1)} %get-tuple-element.88.refs_5_.refs_9_.refs_8_.refs_12_), channel_id=1, source_target_pairs={{0,8},{4,12},{8,0},{12,4},{16,24},{20,28},{24,16},{28,20},{1,9},{5... | collective-permute-start | bytes 1572872 | tf_op jit(solution)/shard_map/ppermute | solution.py:72
  77.7 23.8 %collective-permute-start.14 = (bf16[256,1024]{1,0:T(8,128)(2,1)}, bf16[256,1024]{1,0:T(8,128)(2,1)}, u32[]{:S(2)}, u32[]{:S(2)}) collective-permute-start(bf16[256,1024]{1,0:T(8,128)(2,1)} %get-tuple-element.88.refs_5_.refs_9_.refs_8_.refs_12_), channel_id=1, source_target_pairs={{0,4},{4,0},{8,12},{12,8},{16,20},{20,16},{24,28},{28,24},{1,5},{5... | collective-permute-start | bytes 1572872 | tf_op jit(solution)/shard_map/ppermute | solution.py:72
  77.7 30.7 %collective-permute-start.20 = (bf16[256,1024]{1,0:T(8,128)(2,1)}, bf16[256,1024]{1,0:T(8,128)(2,1)}, u32[]{:S(2)}, u32[]{:S(2)}) collective-permute-start(bf16[256,1024]{1,0:T(8,128)(2,1)} %get-tuple-element.88.refs_5_.refs_9_.refs_8_.refs_12_), channel_id=1, source_target_pairs={{0,16},{4,20},{8,24},{12,28},{16,0},{20,4},{24,8},{28,12},{1,17},{... | collective-permute-start | bytes 1572872 | tf_op jit(solution)/shard_map/ppermute | solution.py:72
  79.5 32.1 %collective-permute-start.23 = (bf16[256,1024]{1,0:T(8,128)(2,1)}, bf16[256,1024]{1,0:T(8,128)(2,1)}, u32[]{:S(2)}, u32[]{:S(2)}) collective-permute-start(bf16[256,1024]{1,0:T(8,128)(2,1)} %get-tuple-element.87.refs_3_.refs_7_.refs_6_.refs_10_), channel_id=1, source_target_pairs={{0,16},{4,20},{8,24},{12,28},{16,0},{20,4},{24,8},{28,12},{1,17},{... | collective-permute-start | bytes 1572872 | tf_op jit(solution)/shard_map/ppermute | solution.py:72
  90.8 20.9 %collective-permute-start.16 = (bf16[256,1024]{1,0:T(8,128)(2,1)}, bf16[256,1024]{1,0:T(8,128)(2,1)}, u32[]{:S(2)}, u32[]{:S(2)}) collective-permute-start(bf16[256,1024]{1,0:T(8,128)(2,1)} %collective-permute-done.12.refs_3_.refs_7_.refs_6_.refs_10_), channel_id=1, source_target_pairs={{0,4},{4,0},{8,12},{12,8},{16,20},{20,16},{24,28},{28,24},{1,5},{5... | collective-permute-start | bytes 1572872 | tf_op jit(solution)/shard_map/ppermute | solution.py:72
  108.4 14.7 %collective-permute-start.21 = (bf16[256,1024]{1,0:T(8,128)(2,1)}, bf16[256,1024]{1,0:T(8,128)(2,1)}, u32[]{:S(2)}, u32[]{:S(2)}) collective-permute-start(bf16[256,1024]{1,0:T(8,128)(2,1)} %collective-permute-done.20.refs_5_.refs_9_.refs_8_.refs_12_), channel_id=1, source_target_pairs={{0,8},{4,12},{8,0},{12,4},{16,24},{20,28},{24,16},{28,20},{1,9},{5... | collective-permute-start | bytes 1572872 | tf_op jit(solution)/shard_map/ppermute | solution.py:72
  109.6 14.4 %collective-permute-start.15 = (bf16[256,1024]{1,0:T(8,128)(2,1)}, bf16[256,1024]{1,0:T(8,128)(2,1)}, u32[]{:S(2)}, u32[]{:S(2)}) collective-permute-start(bf16[256,1024]{1,0:T(8,128)(2,1)} %collective-permute-done.12.refs_3_.refs_7_.refs_6_.refs_10_), channel_id=1, source_target_pairs={{0,16},{4,20},{8,24},{12,28},{16,0},{20,4},{24,8},{28,12},{1,17},{... | collective-permute-start | bytes 1572872 | tf_op jit(solution)/shard_map/ppermute | solution.py:72
  143.0 16.2 %collective-permute-start.26 = (bf16[128,2048]{1,0:T(8,128)(2,1)S(1)}, bf16[128,2048]{1,0:T(8,128)(2,1)S(1)}, u32[]{:S(2)}, u32[]{:S(2)}) collective-permute-start(bf16[128,2048]{1,0:T(8,128)(2,1)S(1)} %convolution_convert_fusion.8), channel_id=1, source_target_pairs={{0,1},{1,2},{2,3},{3,0},{4,5},{5,6},{6,7},{7,4},{8,9},{9,10},{10,1... | collective-permute-start | bytes 1572872 | tf_op jit(solution)/shard_map/ppermute | solution.py:38
  159.6 15.3 %collective-permute-start.27 = (bf16[128,2048]{1,0:T(8,128)(2,1)S(1)}, bf16[128,2048]{1,0:T(8,128)(2,1)S(1)}, u32[]{:S(2)}, u32[]{:S(2)}) collective-permute-start(bf16[128,2048]{1,0:T(8,128)(2,1)S(1)} %add_convert_fusion.30), channel_id=1, source_target_pairs={{0,1},{1,2},{2,3},{3,0},{4,5},{5,6},{6,7},{7,4},{8,9},{9,10},{10,1... | collective-permute-start | bytes 1572872 | tf_op jit(solution)/shard_map/ppermute | solution.py:38
  175.4 14.5 %collective-permute-start.28 = (bf16[128,2048]{1,0:T(8,128)(2,1)S(1)}, bf16[128,2048]{1,0:T(8,128)(2,1)S(1)}, u32[]{:S(2)}, u32[]{:S(2)}) collective-permute-start(bf16[128,2048]{1,0:T(8,128)(2,1)S(1)} %add_convert_fusion.29), channel_id=1, source_target_pairs={{0,1},{1,2},{2,3},{3,0},{4,5},{5,6},{6,7},{7,4},{8,9},{9,10},{10,1... | collective-permute-start | bytes 1572872 | tf_op jit(solution)/shard_map/ppermute | solution.py:38
  190.7 14.0 %collective-permute-start.29 = (bf16[128,2048]{1,0:T(8,128)(2,1)S(1)}, bf16[128,2048]{1,0:T(8,128)(2,1)S(1)}, u32[]{:S(2)}, u32[]{:S(2)}) collective-permute-start(bf16[128,2048]{1,0:T(8,128)(2,1)S(1)} %fusion.40), channel_id=1, source_target_pairs={{0,1},{1,2},{2,3},{3,0},{4,5},{5,6},{6,7},{7,4},{8,9},{9,10},{10,1... | collective-permute-start | bytes 1572872 | tf_op jit(solution)/shard_map/ppermute | solution.py:38
  204.8 16.6 %collective-permute-start.31 = (bf16[128,2048]{1,0:T(8,128)(2,1)S(1)}, bf16[128,2048]{1,0:T(8,128)(2,1)S(1)}, u32[]{:S(2)}, u32[]{:S(2)}) collective-permute-start(bf16[128,2048]{1,0:T(8,128)(2,1)S(1)} %collective-permute-done.29), channel_id=1, source_target_pairs={{0,1},{1,2},{2,3},{3,0},{4,5},{5,6},{6,7},{7,4},{8,9},{9,10},{10,1... | collective-permute-start | bytes 1572872 | tf_op jit(solution)/shard_map/ppermute | solution.py:38
  209.9 22.7 %collective-permute-start.30 = (bf16[128,2048]{1,0:T(8,128)(2,1)S(1)}, bf16[128,2048]{1,0:T(8,128)(2,1)S(1)}, u32[]{:S(2)}, u32[]{:S(2)}) collective-permute-start(bf16[128,2048]{1,0:T(8,128)(2,1)S(1)} %convolution_convert_fusion.7), channel_id=1, source_target_pairs={{0,1},{1,2},{2,3},{3,0},{4,5},{5,6},{6,7},{7,4},{8,9},{9,10},{10,1... | collective-permute-start | bytes 1572872 | tf_op jit(solution)/shard_map/ppermute | solution.py:38
  222.7 21.2 %collective-permute-start.33 = (bf16[128,2048]{1,0:T(8,128)(2,1)S(1)}, bf16[128,2048]{1,0:T(8,128)(2,1)S(1)}, u32[]{:S(2)}, u32[]{:S(2)}) collective-permute-start(bf16[128,2048]{1,0:T(8,128)(2,1)S(1)} %collective-permute-done.31), channel_id=1, source_target_pairs={{0,1},{1,2},{2,3},{3,0},{4,5},{5,6},{6,7},{7,4},{8,9},{9,10},{10,1... | collective-permute-start | bytes 1572872 | tf_op jit(solution)/shard_map/ppermute | solution.py:38
  233.9 17.3 %collective-permute-start.32 = (bf16[128,2048]{1,0:T(8,128)(2,1)S(1)}, bf16[128,2048]{1,0:T(8,128)(2,1)S(1)}, u32[]{:S(2)}, u32[]{:S(2)}) collective-permute-start(bf16[128,2048]{1,0:T(8,128)(2,1)S(1)} %add_convert_fusion.28), channel_id=1, source_target_pairs={{0,1},{1,2},{2,3},{3,0},{4,5},{5,6},{6,7},{7,4},{8,9},{9,10},{10,1... | collective-permute-start | bytes 1572872 | tf_op jit(solution)/shard_map/ppermute | solution.py:38
  278.4 13.9 %collective-permute-start.37 = (bf16[128,2048]{1,0:T(8,128)(2,1)S(1)}, bf16[128,2048]{1,0:T(8,128)(2,1)S(1)}, u32[]{:S(2)}, u32[]{:S(2)}) collective-permute-start(bf16[128,2048]{1,0:T(8,128)(2,1)S(1)} %collective-permute-done.35), channel_id=1, source_target_pairs={{0,1},{1,2},{2,3},{3,0},{4,5},{5,6},{6,7},{7,4},{8,9},{9,10},{10,1... | collective-permute-start | bytes 1572872 | tf_op jit(solution)/shard_map/ppermute | solution.py:38
  322.3 314.8 %reduce-scatter.5.cloned.1.call-start = ((), (), s32[]{:S(2)}) async-start(), calls=%async_computation.3 | async-start | bytes 4718592 | tf_op jit(solution)/shard_map/reduce_scatter | solution.py:509
  344.5 15.1 %collective-permute-start.36 = (bf16[128,2048]{1,0:T(8,128)(2,1)S(1)}, bf16[128,2048]{1,0:T(8,128)(2,1)S(1)}, u32[]{:S(2)}, u32[]{:S(2)}) collective-permute-start(bf16[128,2048]{1,0:T(8,128)(2,1)S(1)} %fusion.15), channel_id=1, source_target_pairs={{0,1},{1,2},{2,3},{3,0},{4,5},{5,6},{6,7},{7,4},{8,9},{9,10},{10,1... | collective-permute-start | bytes 1572872 | tf_op jit(solution)/shard_map/ppermute | solution.py:38
  362.6 14.6 %collective-permute-start.38 = (bf16[128,2048]{1,0:T(8,128)(2,1)S(1)}, bf16[128,2048]{1,0:T(8,128)(2,1)S(1)}, u32[]{:S(2)}, u32[]{:S(2)}) collective-permute-start(bf16[128,2048]{1,0:T(8,128)(2,1)S(1)} %add_convert_fusion.25), channel_id=1, source_target_pairs={{0,1},{1,2},{2,3},{3,0},{4,5},{5,6},{6,7},{7,4},{8,9},{9,10},{10,1... | collective-permute-start | bytes 1572872 | tf_op jit(solution)/shard_map/ppermute | solution.py:38
  385.8 24.3 %collective-permute-start.44 = (bf16[1024,1024]{1,0:T(8,128)(2,1)}, bf16[1024,1024]{1,0:T(8,128)(2,1)}, u32[]{:S(2)}, u32[]{:S(2)}) collective-permute-start(bf16[1024,1024]{1,0:T(8,128)(2,1)} %pad_maximum_fusion.4), channel_id=1, source_target_pairs={{0,4},{4,0},{8,12},{12,8},{16,20},{20,16},{24,28},{28,24},{1,5},{5... | collective-permute-start | bytes 6291464 | tf_op jit(solution)/shard_map/ppermute | solution.py:72
  389.0 24.0 %collective-permute-start.43 = (bf16[1024,1024]{1,0:T(8,128)(2,1)}, bf16[1024,1024]{1,0:T(8,128)(2,1)}, u32[]{:S(2)}, u32[]{:S(2)}) collective-permute-start(bf16[1024,1024]{1,0:T(8,128)(2,1)} %pad_maximum_fusion.3), channel_id=1, source_target_pairs={{0,4},{4,0},{8,12},{12,8},{16,20},{20,16},{24,28},{28,24},{1,5},{5... | collective-permute-start | bytes 6291464 | tf_op jit(solution)/shard_map/ppermute | solution.py:72
  393.9 16.2 %collective-permute-start.41 = (bf16[128,2048]{1,0:T(8,128)(2,1)}, bf16[128,2048]{1,0:T(8,128)(2,1)}, u32[]{:S(2)}, u32[]{:S(2)}) collective-permute-start(bf16[128,2048]{1,0:T(8,128)(2,1)} %subtract_convert_fusion), channel_id=1, source_target_pairs={{0,1},{1,2},{2,3},{3,0},{4,5},{5,6},{6,7},{7,4},{8,9},{9,10},{10,1... | collective-permute-start | bytes 1572872 | tf_op jit(solution)/shard_map/ppermute | solution.py:38
  410.1 15.2 %collective-permute-start.42 = (bf16[128,2048]{1,0:T(8,128)(2,1)}, bf16[128,2048]{1,0:T(8,128)(2,1)S(1)}, u32[]{:S(2)}, u32[]{:S(2)}) collective-permute-start(bf16[128,2048]{1,0:T(8,128)(2,1)} %collective-permute-done.41), channel_id=1, source_target_pairs={{0,1},{1,2},{2,3},{3,0},{4,5},{5,6},{6,7},{7,4},{8,9},{9,10},{10,1... | collective-permute-start | bytes 1572872 | tf_op jit(solution)/shard_map/ppermute | solution.py:38
  425.3 14.2 %collective-permute-start.45 = (bf16[128,2048]{1,0:T(8,128)(2,1)S(1)}, bf16[128,2048]{1,0:T(8,128)(2,1)S(1)}, u32[]{:S(2)}, u32[]{:S(2)}) collective-permute-start(bf16[128,2048]{1,0:T(8,128)(2,1)S(1)} %collective-permute-done.42), channel_id=1, source_target_pairs={{0,1},{1,2},{2,3},{3,0},{4,5},{5,6},{6,7},{7,4},{8,9},{9,10},{10,1... | collective-permute-start | bytes 1572872 | tf_op jit(solution)/shard_map/ppermute | solution.py:38
  428.6 28.3 %collective-permute-start.49 = (bf16[512,1024]{1,0:T(8,128)(2,1)S(1)}, bf16[512,1024]{1,0:T(8,128)(2,1)}, u32[]{:S(2)}, u32[]{:S(2)}) collective-permute-start(bf16[512,1024]{1,0:T(8,128)(2,1)S(1)} %slice.536), channel_id=1, source_target_pairs={{0,8},{4,12},{8,0},{12,4},{16,24},{20,28},{24,16},{28,20},{1,9},{5... | collective-permute-start | bytes 3145736 | tf_op jit(solution)/shard_map/ppermute | solution.py:72
  429.1 31.9 %collective-permute-start.48 = (bf16[512,1024]{1,0:T(8,128)(2,1)}, bf16[512,1024]{1,0:T(8,128)(2,1)}, u32[]{:S(2)}, u32[]{:S(2)}) collective-permute-start(bf16[512,1024]{1,0:T(8,128)(2,1)} %slice.534), channel_id=1, source_target_pairs={{0,16},{4,20},{8,24},{12,28},{16,0},{20,4},{24,8},{28,12},{1,17},{... | collective-permute-start | bytes 3145736 | tf_op jit(solution)/shard_map/ppermute | solution.py:72
  459.6 22.3 %collective-permute-start.81 = (bf16[256,1024]{1,0:T(8,128)(2,1)}, bf16[256,1024]{1,0:T(8,128)(2,1)}, u32[]{:S(2)}, u32[]{:S(2)}) collective-permute-start(bf16[256,1024]{1,0:T(8,128)(2,1)} %slice.593), channel_id=1, source_target_pairs={{0,16},{4,20},{8,24},{12,28},{16,0},{20,4},{24,8},{28,12},{1,17},{... | collective-permute-start | bytes 1572872 | tf_op jit(solution)/shard_map/ppermute | solution.py:72
  464.5 19.2 %collective-permute-start.80 = (bf16[256,1024]{1,0:T(8,128)(2,1)}, bf16[256,1024]{1,0:T(8,128)(2,1)}, u32[]{:S(2)}, u32[]{:S(2)}) collective-permute-start(bf16[256,1024]{1,0:T(8,128)(2,1)} %slice.591), channel_id=1, source_target_pairs={{0,8},{4,12},{8,0},{12,4},{16,24},{20,28},{24,16},{28,20},{1,9},{5... | collective-permute-start | bytes 1572872 | tf_op jit(solution)/shard_map/ppermute | solution.py:72
  475.3 14.0 %collective-permute-start.50 = (bf16[256,1024]{1,0:T(8,128)(2,1)}, bf16[256,1024]{1,0:T(8,128)(2,1)}, u32[]{:S(2)}, u32[]{:S(2)}) collective-permute-start(bf16[256,1024]{1,0:T(8,128)(2,1)} %get-tuple-element.116), channel_id=1, source_target_pairs={{0,4},{4,0},{8,12},{12,8},{16,20},{20,16},{24,28},{28,24},{1,5},{5... | collective-permute-start | bytes 1572872 | tf_op jit(solution)/shard_map/ppermute | solution.py:72
  475.4 13.9 %collective-permute-start.51 = (bf16[256,1024]{1,0:T(8,128)(2,1)}, bf16[256,1024]{1,0:T(8,128)(2,1)}, u32[]{:S(2)}, u32[]{:S(2)}) collective-permute-start(bf16[256,1024]{1,0:T(8,128)(2,1)} %get-tuple-element.117), channel_id=1, source_target_pairs={{0,4},{4,0},{8,12},{12,8},{16,20},{20,16},{24,28},{28,24},{1,5},{5... | collective-permute-start | bytes 1572872 | tf_op jit(solution)/shard_map/ppermute | solution.py:72
  478.1 22.3 %collective-permute-start.62 = (bf16[256,1024]{1,0:T(8,128)(2,1)}, bf16[256,1024]{1,0:T(8,128)(2,1)}, u32[]{:S(2)}, u32[]{:S(2)}) collective-permute-start(bf16[256,1024]{1,0:T(8,128)(2,1)} %add_convert_fusion.14), channel_id=1, source_target_pairs={{0,8},{4,12},{8,0},{12,4},{16,24},{20,28},{24,16},{28,20},{1,9},{5... | collective-permute-start | bytes 1572872 | tf_op jit(solution)/shard_map/ppermute | solution.py:72
  481.9 46.2 %collective-permute-start.59 = (bf16[256,1024]{1,0:T(8,128)(2,1)}, bf16[256,1024]{1,0:T(8,128)(2,1)}, u32[]{:S(2)}, u32[]{:S(2)}) collective-permute-start(bf16[256,1024]{1,0:T(8,128)(2,1)} %add_convert_fusion.19), channel_id=1, source_target_pairs={{0,16},{4,20},{8,24},{12,28},{16,0},{20,4},{24,8},{28,12},{1,17},{... | collective-permute-start | bytes 1572872 | tf_op jit(solution)/shard_map/ppermute | solution.py:72
  502.6 46.2 %collective-permute-start.63 = (bf16[256,1024]{1,0:T(8,128)(2,1)}, bf16[256,1024]{1,0:T(8,128)(2,1)}, u32[]{:S(2)}, u32[]{:S(2)}) collective-permute-start(bf16[256,1024]{1,0:T(8,128)(2,1)} %add_convert_fusion.13), channel_id=1, source_target_pairs={{0,16},{4,20},{8,24},{12,28},{16,0},{20,4},{24,8},{28,12},{1,17},{... | collective-permute-start | bytes 1572872 | tf_op jit(solution)/shard_map/ppermute | solution.py:72
  506.1 47.4 %collective-permute-start.58 = (bf16[256,1024]{1,0:T(8,128)(2,1)}, bf16[256,1024]{1,0:T(8,128)(2,1)}, u32[]{:S(2)}, u32[]{:S(2)}) collective-permute-start(bf16[256,1024]{1,0:T(8,128)(2,1)} %add_convert_fusion.22), channel_id=1, source_target_pairs={{0,16},{4,20},{8,24},{12,28},{16,0},{20,4},{24,8},{28,12},{1,17},{... | collective-permute-start | bytes 1572872 | tf_op jit(solution)/shard_map/ppermute | solution.py:72
  534.2 16.6 %collective-permute-start.64 = (bf16[256,1024]{1,0:T(8,128)(2,1)}, bf16[256,1024]{1,0:T(8,128)(2,1)}, u32[]{:S(2)}, u32[]{:S(2)}) collective-permute-start(bf16[256,1024]{1,0:T(8,128)(2,1)} %add_convert_fusion.11), channel_id=1, source_target_pairs={{0,8},{4,12},{8,0},{12,4},{16,24},{20,28},{24,16},{28,20},{1,9},{5... | collective-permute-start | bytes 1572872 | tf_op jit(solution)/shard_map/ppermute | solution.py:72
  534.8 16.1 %collective-permute-start.61 = (bf16[256,1024]{1,0:T(8,128)(2,1)}, bf16[256,1024]{1,0:T(8,128)(2,1)}, u32[]{:S(2)}, u32[]{:S(2)}) collective-permute-start(bf16[256,1024]{1,0:T(8,128)(2,1)} %get-tuple-element.137), channel_id=1, source_target_pairs={{0,4},{4,0},{8,12},{12,8},{16,20},{20,16},{24,28},{28,24},{1,5},{5... | collective-permute-start | bytes 1572872 | tf_op jit(solution)/shard_map/ppermute | solution.py:72
  534.8 23.5 %collective-permute-start.60 = (bf16[256,1024]{1,0:T(8,128)(2,1)}, bf16[256,1024]{1,0:T(8,128)(2,1)}, u32[]{:S(2)}, u32[]{:S(2)}) collective-permute-start(bf16[256,1024]{1,0:T(8,128)(2,1)} %add_convert_fusion.18), channel_id=1, source_target_pairs={{0,8},{4,12},{8,0},{12,4},{16,24},{20,28},{24,16},{28,20},{1,9},{5... | collective-permute-start | bytes 1572872 | tf_op jit(solution)/shard_map/ppermute | solution.py:72
  580.3 16.5 %collective-permute-start.68 = (bf16[128,2048]{1,0:T(8,128)(2,1)S(1)}, bf16[128,2048]{1,0:T(8,128)(2,1)S(1)}, u32[]{:S(2)}, u32[]{:S(2)}) collective-permute-start(bf16[128,2048]{1,0:T(8,128)(2,1)S(1)} %fusion.16), channel_id=1, source_target_pairs={{0,1},{1,2},{2,3},{3,0},{4,5},{5,6},{6,7},{7,4},{8,9},{9,10},{10,1... | collective-permute-start | bytes 1572872 | tf_op jit(solution)/shard_map/ppermute | solution.py:38
  583.9 14.1 %collective-permute-start.74 = (bf16[1024,512]{1,0:T(8,128)(2,1)S(1)}, bf16[1024,512]{1,0:T(8,128)(2,1)S(1)}, u32[]{:S(2)}, u32[]{:S(2)}) collective-permute-start(bf16[1024,512]{1,0:T(8,128)(2,1)S(1)} %pad_maximum_fusion.6), channel_id=1, source_target_pairs={{0,4},{4,0},{8,12},{12,8},{16,20},{20,16},{24,28},{28,24},{1,5},{5... | collective-permute-start | bytes 3145736 | tf_op jit(solution)/shard_map/ppermute | solution.py:72
  597.6 15.4 %collective-permute-start.69 = (bf16[128,2048]{1,0:T(8,128)(2,1)S(1)}, bf16[128,2048]{1,0:T(8,128)(2,1)S(1)}, u32[]{:S(2)}, u32[]{:S(2)}) collective-permute-start(bf16[128,2048]{1,0:T(8,128)(2,1)S(1)} %add_convert_fusion.9), channel_id=1, source_target_pairs={{0,1},{1,2},{2,3},{3,0},{4,5},{5,6},{6,7},{7,4},{8,9},{9,10},{10,1... | collective-permute-start | bytes 1572872 | tf_op jit(solution)/shard_map/ppermute | solution.py:38
  598.3 22.5 %collective-permute-start.75 = (bf16[512,512]{1,0:T(8,128)(2,1)S(1)}, bf16[512,512]{1,0:T(8,128)(2,1)S(1)}, u32[]{:S(2)}, u32[]{:S(2)}) collective-permute-start(bf16[512,512]{1,0:T(8,128)(2,1)S(1)} %slice.570), channel_id=1, source_target_pairs={{0,8},{4,12},{8,0},{12,4},{16,24},{20,28},{24,16},{28,20},{1,9},{5... | collective-permute-start | bytes 1572872 | tf_op jit(solution)/shard_map/ppermute | solution.py:72
  599.3 23.2 %collective-permute-start.72 = (bf16[512,512]{1,0:T(8,128)(2,1)S(1)}, bf16[512,512]{1,0:T(8,128)(2,1)S(1)}, u32[]{:S(2)}, u32[]{:S(2)}) collective-permute-start(bf16[512,512]{1,0:T(8,128)(2,1)S(1)} %slice.566), channel_id=1, source_target_pairs={{0,16},{4,20},{8,24},{12,28},{16,0},{20,4},{24,8},{28,12},{1,17},{... | collective-permute-start | bytes 1572872 | tf_op jit(solution)/shard_map/ppermute | solution.py:72
  613.8 14.5 %collective-permute-start.70 = (bf16[128,2048]{1,0:T(8,128)(2,1)S(1)}, bf16[128,2048]{1,0:T(8,128)(2,1)S(1)}, u32[]{:S(2)}, u32[]{:S(2)}) collective-permute-start(bf16[128,2048]{1,0:T(8,128)(2,1)S(1)} %add_convert_fusion.8), channel_id=1, source_target_pairs={{0,1},{1,2},{2,3},{3,0},{4,5},{5,6},{6,7},{7,4},{8,9},{9,10},{10,1... | collective-permute-start | bytes 1572872 | tf_op jit(solution)/shard_map/ppermute | solution.py:38
  (164 other events, 1253.0 us)
Sparse Core Ops, SparseCore 0:
  322.4 117.4 reduce-scatter.2
  575.4 61.6 reduce-scatter.4

commit v3 on v2

--- a/solution.py
+++ b/solution.py
@@ -499,6 +499,20 @@
     up_pre = [mm(x, up_weight) for x in state_slots]
     activated = [(jax.nn.silu(g) * u).astype(BF) for g, u in zip(gate_pre, up_pre)]
     mlp_out = ring_scatter(lambda s: mm(activated[s], down_weight), nf)
+
+    activ = [{0: jnp.concatenate(activated[:half])}, {0: jnp.concatenate(activated[half:])}]
+
+    def fetch_activ(i, m):
+        if m not in activ[i]:
+            src, bit = came_from(m, orders[i])
+            have = fetch_activ(i, src)
+            activ[i][m] = swap(have, nc, bit)
+        return activ[i][m]
+
+    for i in range(2):
+        for m in range(nc):
+            fetch_activ(i, m)
+
     mlp_rms = lax.rsqrt(jnp.mean(mlp_out * mlp_out, axis=1) + norm_eps)
     block_output = (hidden_state + mlp_out * mlp_rms[:, None] * mlp_gain[None, :]).astype(BF)
     upstream = cotangent.astype(F32)
@@ -531,42 +545,44 @@
             grad_slots.append(got)
         gate_grads.append(g)
         up_grads.append(u)
-    grad_rows = jnp.concatenate(grad_slots)
-    activ_rows = jnp.concatenate(activated)
-    wide = activ_rows.shape[1] // 2
-    down_parts = [
-        contract_rows(grad_rows, activ_rows[:, i * wide : (i + 1) * wide]).astype(BF)
-        for i in range(2)
-    ]
+    gate_up_part = contract_rows(
+        jnp.concatenate(state_slots),
+        jnp.concatenate([jnp.concatenate(gate_grads), jnp.concatenate(up_grads)], axis=1),
+    ).astype(BF)
+    gate_up_sum = ctx_scatter(gate_up_part)
     state_grad = state_part(gate_grads[0], up_grads[0])
     if nf > 1:
         got = shift(acc, nf, 1)
         state_grad = got.astype(F32) + state_grad
     state_grad = upstream + state_grad
-    marks = [[] for _ in range(nc)]
-    down_grad = jnp.concatenate(
-        [
-            halving(p, me_c, nc, order, marks)
-            for p, order in zip(down_parts, bit_orders(nc))
-        ],
-        axis=1,
-    ).T
+    grad_rows = jnp.concatenate(grad_slots)
+    block = width // nc
+
+    def columns(m):
+        cut = lax.dynamic_slice_in_dim(grad_rows, (me_c ^ m) * block, block, axis=1)
+        if m == 0:
+            return cut
+        return swap(cut, nc, m)
+
+    down_grad = None
+    for masks in (range(nc // 2), range(nc // 2, nc)):
+        part = contract_rows(
+            jnp.concatenate([activ[i][m] for m in masks for i in range(2)]),
+            jnp.concatenate([columns(m) for m in masks]),
+        )
+        down_grad = part if down_grad is None else down_grad + part
 
     attn_gain_part = jnp.sum(state_grad * attn_out * attn_rms[:, None], axis=0)
     attn_grad_b = norm_back(attn_out, attn_rms, attn_gain[None, :], state_grad).astype(BF)
-    gate_up_part = contract_rows(
-        jnp.concatenate(state_slots),
-        jnp.concatenate([jnp.concatenate(gate_grads), jnp.concatenate(up_grads)], axis=1),
-    ).astype(BF)
-    gate_up_sum = ctx_scatter(gate_up_part)
     first_hop = shift(attn_grad_b, nf, 1)
     proj_slots = [attn_grad_b, first_hop]
-    for s in range(2, nf):
+    for _ in range(2, nf):
         got = shift(proj_slots[-1], nf, 1)
-        proj_slots.append(gate(got, *marks[0]) if s == 2 else got)
-    mixture_grad_b = jnp.concatenate(
-        [contract_cols(x, output_weight).astype(BF) for x in proj_slots]
-    )
+        proj_slots.append(got)
+    mixture_grads = []
+    for s in range(nf):
+        mixture_grads.append(contract_cols(proj_slots[s], output_weight).astype(BF))
+    mixture_grad_b = jnp.concatenate(mixture_grads)
 
     dq = None
     sums = [{}, {}]
@@ -581,7 +597,7 @@
     for gi, group in enumerate(groups[::-1]):
         starts, kv = group_inputs(group)
         if gi:
-            dq = gate(dq, *waits[gi - 1], *(marks[1] if gi == 1 else []))
+            dq = gate(dq, *waits[gi - 1])
         dq, *out = attend_back(
             starts, query_rot, mixture_grad_b, mixture, log_total, qpos, kv, dq, heads, half
         )

time: 653 us -> 738 us (1.13)
  waiting for transfers between devices: 256 us -> 317 us
  local copies, waits for them, and re-layouts: 36.3 us -> 62.6 us
  other arithmetic: 57.7 us -> 37.9 us
  matrix products: 139 us -> 151 us
    ppermute x46 -> x61, waiting for transfers between devices: 50.2 us -> 111 us  [swap(): return lax.ppermute(x, 'ctx', [(i, i ^ bit) for i in range(n)])]
    unnamed x259 -> x242, local copies, waits for them, and re-layouts: 14.3 us -> 41.4 us
    dot_general x7, matrix products: 28 us -> 42.9 us  [contract_rows(): lax.dot_general(left, right, (((0,), (0,)), ((), ())), preferred_element_...]
    convert_element_type x10 -> x6, other arithmetic: 10.4 us -> 0.86 us  [halving(): total = total.astype(BF)]
    ppermute x46 -> x61, starting transfers between devices: 29.7 us -> 37.1 us  [swap(): return lax.ppermute(x, 'ctx', [(i, i ^ bit) for i in range(n)])]
  transfers between devices with their start and end apart: 84 -> 99, of which waited for: 38 -> 37; matrix products, arithmetic and copies ran while one was open for 29% -> 28% of each run, Pallas kernels for 11% -> 9%
where the time goes in v3:
time: 738 us; the launch traced here: 731 us
  waiting for transfers between devices  317 us (43%)
  matrix products  151 us (20%)
  Pallas kernels  86.2 us (12%)
  local copies, waits for them, and re-layouts  62.6 us (8%)
  starting transfers between devices  59.6 us (8%)
  other arithmetic  37.9 us (5%)
  between operations  16.5 us (2%)
    ppermute x36, waiting for transfers between devices, shift(): return lax.ppermute(x, 'fsdp', [(i, (i + by) % n) for i in range(n)])  206 us
    ppermute x61, waiting for transfers between devices, swap(): return lax.ppermute(x, 'ctx', [(i, i ^ bit) for i in range(n)])  111 us
    dot_general x28, matrix products, contract_cols(): lax.dot_general(left, right, (((1,), (1,)), ((), ())), preferred_element_...  69.5 us
    dot_general x7, matrix products, contract_rows(): lax.dot_general(left, right, (((0,), (0,)), ((), ())), preferred_element_...  42.9 us
    pallas_call x4, Pallas kernels, attend_back(): pl.pallas_call(functools.partial(bwd_kernel, np_, slots, heads, first), g...  41.9 us
    unnamed x242, local copies, waits for them, and re-layouts  41.4 us
    dot_general x28, matrix products, mm(): return jnp.dot(left, right, preferred_element_type=F32)  38.8 us
    ppermute x61, starting transfers between devices, swap(): return lax.ppermute(x, 'ctx', [(i, i ^ bit) for i in range(n)])  37.1 us
  transfers between devices with their start and end apart: 99, of which 37 were waited for; matrix products, arithmetic and copies ran while one was open for 28% of the time, Pallas kernels for 9%

profile of v3, /device:TPU:0, one launch (start us, length us, event | category | flops | bytes accessed | tf_op | source)
XLA Modules:
  0.0 731.5 jit_solution(11605254706119180637)
XLA Ops:
  18.5 6.1 collective-permute-done
  48.2 10.2 %collective-permute-done.2 = bf16[128,2048]{1,0:T(8,128)(2,1)S(1)} collective-permute-done((bf16[128,2048]{1,0:T(8,128)(2,1)S(1)}, bf16[128,2048]{1,0:T(8,128)(2,1)S(1)}, u32[]{:S(2)}, u32[]{:S(2)}) %collective-permute-start.2) | collective-permute-done | bytes 524320 | tf_op jit(solution)/shard_map/ppermute | solution.py:38
  70.2 5.9 shard_map.237
  81.0 10.4 %collective-permute-done.12.refs_3_.refs_7_.refs_6_.refs_10_ = bf16[256,1024]{1,0:T(8,128)(2,1)} collective-permute-done((bf16[256,1024]{1,0:T(8,128)(2,1)}, bf16[256,1024]{1,0:T(8,128)(2,1)}, u32[]{:S(2)}, u32[]{:S(2)}) %collective-permute-start.12) | collective-permute-done | bytes 524320 | tf_op jit(solution)/shard_map/ppermute | solution.py:72
  91.4 10.7 %collective-permute-done.17.refs_5_.refs_9_.refs_8_.refs_12_ = bf16[256,1024]{1,0:T(8,128)(2,1)} collective-permute-done((bf16[256,1024]{1,0:T(8,128)(2,1)}, bf16[256,1024]{1,0:T(8,128)(2,1)}, u32[]{:S(2)}, u32[]{:S(2)}) %collective-permute-start.17) | collective-permute-done | bytes 524320 | tf_op jit(solution)/shard_map/ppermute | solution.py:72
  102.1 6.9 shard_map.238
  113.1 7.3 shard_map.239
  126.9 7.2 shard_map.240
  134.1 7.5 %shard_map.241 = (f32[512,512]{1,0:T(8,128)}, bf16[512,512]{1,0:T(8,128)(2,1)}, f32[4,1,512]{2,1,0:T(1,128)}) custom-call(s32[8]{0:T(128)} %pad_add_fusion.3.refs_0_, bf16[512,512]{1,0:T(8,128)(2,1)} %get-tuple-element.85.refs_1_, s32[1,512]{1,0:T(1,128)} %bitcast.298, bf16[256,1024]{1,0:T(8,128)(2,1)} %collective-permute-done.15.refs_3_.refs_7_.refs_6_.refs_10_, ...), custom_call_target="tpu_custom_call" | custom-call | flops 2147483648 | bytes 2097152 | tf_op jit(solution)/shard_map/pallas_call | solution.py:234
  144.0 16.1 %collective-permute-done.26 = bf16[128,2048]{1,0:T(8,128)(2,1)S(1)} collective-permute-done((bf16[128,2048]{1,0:T(8,128)(2,1)S(1)}, bf16[128,2048]{1,0:T(8,128)(2,1)S(1)}, u32[]{:S(2)}, u32[]{:S(2)}) %collective-permute-start.26) | collective-permute-done | bytes 524320 | tf_op jit(solution)/shard_map/ppermute | solution.py:38
  160.6 15.3 %collective-permute-done.27 = bf16[128,2048]{1,0:T(8,128)(2,1)S(1)} collective-permute-done((bf16[128,2048]{1,0:T(8,128)(2,1)S(1)}, bf16[128,2048]{1,0:T(8,128)(2,1)S(1)}, u32[]{:S(2)}, u32[]{:S(2)}) %collective-permute-start.27) | collective-permute-done | bytes 524320 | tf_op jit(solution)/shard_map/ppermute | solution.py:38
  176.4 14.4 %collective-permute-done.28 = bf16[128,2048]{1,0:T(8,128)(2,1)S(1)} collective-permute-done((bf16[128,2048]{1,0:T(8,128)(2,1)S(1)}, bf16[128,2048]{1,0:T(8,128)(2,1)S(1)}, u32[]{:S(2)}, u32[]{:S(2)}) %collective-permute-start.28) | collective-permute-done | bytes 524320 | tf_op jit(solution)/shard_map/ppermute | solution.py:38
  197.7 7.8 %collective-permute-done.29 = bf16[128,2048]{1,0:T(8,128)(2,1)S(1)} collective-permute-done((bf16[128,2048]{1,0:T(8,128)(2,1)S(1)}, bf16[128,2048]{1,0:T(8,128)(2,1)S(1)}, u32[]{:S(2)}, u32[]{:S(2)}) %collective-permute-start.29) | collective-permute-done | bytes 524320 | tf_op jit(solution)/shard_map/ppermute | solution.py:38
  210.8 11.3 %collective-permute-done.31 = bf16[128,2048]{1,0:T(8,128)(2,1)S(1)} collective-permute-done((bf16[128,2048]{1,0:T(8,128)(2,1)S(1)}, bf16[128,2048]{1,0:T(8,128)(2,1)S(1)}, u32[]{:S(2)}, u32[]{:S(2)}) %collective-permute-start.31) | collective-permute-done | bytes 524320 | tf_op jit(solution)/shard_map/ppermute | solution.py:38
  225.7 7.7 %collective-permute-done.30 = bf16[128,2048]{1,0:T(8,128)(2,1)S(1)} collective-permute-done((bf16[128,2048]{1,0:T(8,128)(2,1)S(1)}, bf16[128,2048]{1,0:T(8,128)(2,1)S(1)}, u32[]{:S(2)}, u32[]{:S(2)}) %collective-permute-start.30) | collective-permute-done | bytes 524320 | tf_op jit(solution)/shard_map/ppermute | solution.py:38
  235.2 9.4 %collective-permute-done.33 = bf16[128,2048]{1,0:T(8,128)(2,1)S(1)} collective-permute-done((bf16[128,2048]{1,0:T(8,128)(2,1)S(1)}, bf16[128,2048]{1,0:T(8,128)(2,1)S(1)}, u32[]{:S(2)}, u32[]{:S(2)}) %collective-permute-start.33) | collective-permute-done | bytes 524320 | tf_op jit(solution)/shard_map/ppermute | solution.py:38
  252.1 11.8 %collective-permute-done.34 = bf16[128,2048]{1,0:T(8,128)(2,1)S(1)} collective-permute-done((bf16[128,2048]{1,0:T(8,128)(2,1)S(1)}, bf16[128,2048]{1,0:T(8,128)(2,1)S(1)}, u32[]{:S(2)}, u32[]{:S(2)}) %collective-permute-start.34) | collective-permute-done | bytes 524320 | tf_op jit(solution)/shard_map/ppermute | solution.py:38
  267.3 4.0 multiply_convert_fusion.6
  271.3 8.1 %collective-permute-done.35 = bf16[128,2048]{1,0:T(8,128)(2,1)S(1)} collective-permute-done((bf16[128,2048]{1,0:T(8,128)(2,1)S(1)}, bf16[128,2048]{1,0:T(8,128)(2,1)S(1)}, u32[]{:S(2)}, u32[]{:S(2)}) %collective-permute-start.35) | collective-permute-done | bytes 524320 | tf_op jit(solution)/shard_map/ppermute | solution.py:38
  279.4 4.0 multiply_convert_fusion.4
  283.4 9.0 %collective-permute-done.37 = bf16[128,2048]{1,0:T(8,128)(2,1)S(1)} collective-permute-done((bf16[128,2048]{1,0:T(8,128)(2,1)S(1)}, bf16[128,2048]{1,0:T(8,128)(2,1)S(1)}, u32[]{:S(2)}, u32[]{:S(2)}) %collective-permute-start.37) | collective-permute-done | bytes 524320 | tf_op jit(solution)/shard_map/ppermute | solution.py:38
  292.6 4.0 multiply_convert_fusion.2
  296.7 6.9 collective-permute-done.39
  303.6 4.0 multiply_convert_fusion
  307.6 14.9 %convolution_convert_fusion = bf16[2048,4096]{1,0:T(8,128)(2,1)} fusion(bf16[128,2048]{1,0:T(8,128)(2,1)} %get-tuple-element.218, bf16[128,2048]{1,0:T(8,128)(2,1)} %get-tuple-element.128, bf16[128,2048]{1,0:T(8,128)(2,1)} %get-tuple-element.127, bf16[128,2048]{1,0:T(8,128)(2,1)} %get-tuple-element.106, bf16[128,2048]{1,0:T(8,128)(2,1)} %get-tuple-element.219, ...), kind=kOutput, calls=%fused_computation | convolution fusion | flops 8640266240 | bytes 23068672 | tf_op jit(solution)/shard_map/dot_general | solution.py:26
  336.1 18.4 %collective-permute-done.85 = bf16[256,2048]{1,0:T(8,128)(2,1)} collective-permute-done((bf16[256,2048]{1,0:T(8,128)(2,1)S(1)}, bf16[256,2048]{1,0:T(8,128)(2,1)}, u32[]{:S(2)}, u32[]{:S(2)}) %collective-permute-start.85) | collective-permute-done | bytes 1048608 | tf_op jit(solution)/shard_map/ppermute | solution.py:72
  358.5 6.5 fusion.139
  365.0 6.5 fusion.15
  377.2 13.4 %collective-permute-done.86 = bf16[256,2048]{1,0:T(8,128)(2,1)} collective-permute-done((bf16[256,2048]{1,0:T(8,128)(2,1)}, bf16[256,2048]{1,0:T(8,128)(2,1)}, u32[]{:S(2)}, u32[]{:S(2)}) %collective-permute-start.86) | collective-permute-done | bytes 1048608 | tf_op jit(solution)/shard_map/ppermute | solution.py:72
  400.2 31.4 %collective-permute-done.89 = bf16[256,2048]{1,0:T(8,128)(2,1)S(1)} collective-permute-done((bf16[256,2048]{1,0:T(8,128)(2,1)}, bf16[256,2048]{1,0:T(8,128)(2,1)S(1)}, u32[]{:S(2)}, u32[]{:S(2)}) %collective-permute-start.89) | collective-permute-done | bytes 1048608 | tf_op jit(solution)/shard_map/ppermute | solution.py:72
  439.8 4.1 add_convert_fusion.21
  456.2 4.1 collective-permute-done.38
  466.0 11.3 %collective-permute-done.40 = bf16[128,2048]{1,0:T(8,128)(2,1)S(1)} collective-permute-done((bf16[128,2048]{1,0:T(8,128)(2,1)S(1)}, bf16[128,2048]{1,0:T(8,128)(2,1)S(1)}, u32[]{:S(2)}, u32[]{:S(2)}) %collective-permute-start.40) | collective-permute-done | bytes 524320 | tf_op jit(solution)/shard_map/ppermute | solution.py:38
  484.7 7.2 fusion.38
  491.9 8.4 %collective-permute-done.41 = bf16[128,2048]{1,0:T(8,128)(2,1)S(1)} collective-permute-done((bf16[128,2048]{1,0:T(8,128)(2,1)}, bf16[128,2048]{1,0:T(8,128)(2,1)S(1)}, u32[]{:S(2)}, u32[]{:S(2)}) %collective-permute-start.41) | collective-permute-done | bytes 524320 | tf_op jit(solution)/shard_map/ppermute | solution.py:38
  505.3 9.5 %collective-permute-done.42 = bf16[128,2048]{1,0:T(8,128)(2,1)S(1)} collective-permute-done((bf16[128,2048]{1,0:T(8,128)(2,1)S(1)}, bf16[128,2048]{1,0:T(8,128)(2,1)S(1)}, u32[]{:S(2)}, u32[]{:S(2)}) %collective-permute-start.42) | collective-permute-done | bytes 524320 | tf_op jit(solution)/shard_map/ppermute | solution.py:38
  516.5 11.9 %collective-permute-done.43 = bf16[128,2048]{1,0:T(8,128)(2,1)S(1)} collective-permute-done((bf16[128,2048]{1,0:T(8,128)(2,1)S(1)}, bf16[128,2048]{1,0:T(8,128)(2,1)S(1)}, u32[]{:S(2)}, u32[]{:S(2)}) %collective-permute-start.43) | collective-permute-done | bytes 524320 | tf_op jit(solution)/shard_map/ppermute | solution.py:38
  530.1 10.4 %shard_map.242 = (f32[512,512]{1,0:T(8,128)}, bf16[256,1024]{1,0:T(8,128)(2,1)}, bf16[256,1024]{1,0:T(8,128)(2,1)}, bf16[256,1024]{1,0:T(8,128)(2,1)}, bf16[256,1024]{1,0:T(8,128)(2,1)}) custom-call(s32[8]{0:T(128)} %pad_add_fusion.3.refs_0_, bf16[512,512]{1,0:T(8,128)(2,1)} %get-tuple-element.85.refs_1_, bf16[512,512]{1,0:T(8,128)(2,1)} %pad_maximum_fusion.6.refs_2_, ...), custom_call_target="tpu_custom_call" | custom-call | flops 5368709120 | bytes 4194304 | tf_op jit(solution)/shard_map/pallas_call | solution.py:306
  541.1 8.2 %convolution_add_fusion = f32[2048,256]{1,0:T(8,128)} fusion(f32[2048,256]{1,0:T(8,128)} %fusion.38, bf16[2048,2048]{1,0:T(8,128)(2,1)} %constant_dynamic-update-slice_fusion.14, bf16[512,256]{1,0:T(8,128)(2,1)} %collective-permute-done.96, bf16[512,256]{1,0:T(8,128)(2,1)} %collective-permute-done.95, bf16[512,256]{1,0:T(8,128)(2,1)} %collective-permute-done.94, ...), kind=kOutput, calls=%fused_computation.21 | convolution fusion | flops 2152202240 | bytes 13631488 | tf_op jit(solution)/shard_map/dot_general | solution.py:26
  554.5 10.4 %shard_map.243 = (f32[512,512]{1,0:T(8,128)}, bf16[256,1024]{1,0:T(8,128)(2,1)}, bf16[256,1024]{1,0:T(8,128)(2,1)}, bf16[256,1024]{1,0:T(8,128)(2,1)}, bf16[256,1024]{1,0:T(8,128)(2,1)}) custom-call(s32[8]{0:T(128)} %pad_add_fusion.6.refs_0_, bf16[512,512]{1,0:T(8,128)(2,1)} %get-tuple-element.85.refs_1_, bf16[512,512]{1,0:T(8,128)(2,1)} %pad_maximum_fusion.6.refs_2_, ...), custom_call_target="tpu_custom_call" | custom-call | flops 5368709120 | bytes 4194304 | tf_op jit(solution)/shard_map/pallas_call | solution.py:306
  573.1 10.4 %shard_map.244 = (f32[512,512]{1,0:T(8,128)}, bf16[256,1024]{1,0:T(8,128)(2,1)}, bf16[256,1024]{1,0:T(8,128)(2,1)}, bf16[256,1024]{1,0:T(8,128)(2,1)}, bf16[256,1024]{1,0:T(8,128)(2,1)}) custom-call(s32[8]{0:T(128)} %pad_add_fusion.5.refs_0_, bf16[512,512]{1,0:T(8,128)(2,1)} %get-tuple-element.85.refs_1_, bf16[512,512]{1,0:T(8,128)(2,1)} %pad_maximum_fusion.6.refs_2_, ...), custom_call_target="tpu_custom_call" | custom-call | flops 5368709120 | bytes 4194304 | tf_op jit(solution)/shard_map/pallas_call | solution.py:306
  589.6 10.6 %shard_map.245 = (f32[512,512]{1,0:T(8,128)}, bf16[256,1024]{1,0:T(8,128)(2,1)}, bf16[256,1024]{1,0:T(8,128)(2,1)}, bf16[256,1024]{1,0:T(8,128)(2,1)}, bf16[256,1024]{1,0:T(8,128)(2,1)}) custom-call(s32[8]{0:T(128)} %pad_add_fusion.4.refs_0_, bf16[512,512]{1,0:T(8,128)(2,1)} %get-tuple-element.85.refs_1_, bf16[512,512]{1,0:T(8,128)(2,1)} %pad_maximum_fusion.6.refs_2_, ...), custom_call_target="tpu_custom_call" | custom-call | flops 5368709120 | bytes 4194304 | tf_op jit(solution)/shard_map/pallas_call | solution.py:306
  600.2 4.9 shard_map.246
  634.3 10.1 %collective-permute-done.60 = bf16[256,1024]{1,0:T(8,128)(2,1)S(1)} collective-permute-done((bf16[256,1024]{1,0:T(8,128)(2,1)S(1)}, bf16[256,1024]{1,0:T(8,128)(2,1)S(1)}, u32[]{:S(2)}, u32[]{:S(2)}) %collective-permute-start.60) | collective-permute-done | bytes 524320 | tf_op jit(solution)/shard_map/ppermute | solution.py:72
  646.8 4.6 shard_map.247
  658.7 4.2 fusion.124
  691.6 11.4 %collective-permute-done.65 = bf16[128,2048]{1,0:T(8,128)(2,1)S(1)} collective-permute-done((bf16[128,2048]{1,0:T(8,128)(2,1)S(1)}, bf16[128,2048]{1,0:T(8,128)(2,1)S(1)}, u32[]{:S(2)}, u32[]{:S(2)}) %collective-permute-start.65) | collective-permute-done | bytes 524320 | tf_op jit(solution)/shard_map/ppermute | solution.py:38
  706.7 11.0 %collective-permute-done.66 = bf16[128,2048]{1,0:T(8,128)(2,1)S(1)} collective-permute-done((bf16[128,2048]{1,0:T(8,128)(2,1)S(1)}, bf16[128,2048]{1,0:T(8,128)(2,1)S(1)}, u32[]{:S(2)}, u32[]{:S(2)}) %collective-permute-start.66) | collective-permute-done | bytes 524320 | tf_op jit(solution)/shard_map/ppermute | solution.py:38
  (597 shorter events, 265.1 us)
Async XLA Ops:
  7.2 638.8 %reduce-scatter.3.cloned.1.call-start = ((), (), s32[]{:S(2)}) async-start(), calls=%async_computation.2 | async-start | bytes 18874368 | tf_op jit(solution)/shard_map/reduce_scatter | solution.py:523
  7.3 17.3 %collective-permute-start = (bf16[128,2048]{1,0:T(8,128)(2,1)}, bf16[128,2048]{1,0:T(8,128)(2,1)S(1)}, u32[]{:S(2)}, u32[]{:S(2)}) collective-permute-start(bf16[128,2048]{1,0:T(8,128)(2,1)} %param.14), channel_id=1, source_target_pairs={{0,1},{1,2},{2,3},{3,0},{4,5},{5,6},{6,7},{7,4},{8,9},{9,10},{10,1... | collective-permute-start | bytes 1572872 | tf_op jit(solution)/shard_map/ppermute | solution.py:38
  76.2 15.2 %collective-permute-start.12 = (bf16[256,1024]{1,0:T(8,128)(2,1)}, bf16[256,1024]{1,0:T(8,128)(2,1)}, u32[]{:S(2)}, u32[]{:S(2)}) collective-permute-start(bf16[256,1024]{1,0:T(8,128)(2,1)} %get-tuple-element.86.refs_3_.refs_7_.refs_6_.refs_10_), channel_id=1, source_target_pairs={{0,8},{4,12},{8,0},{12,4},{16,24},{20,28},{24,16},{28,20},{1,9},{5... | collective-permute-start | bytes 1572872 | tf_op jit(solution)/shard_map/ppermute | solution.py:72
  77.7 24.3 %collective-permute-start.17 = (bf16[256,1024]{1,0:T(8,128)(2,1)}, bf16[256,1024]{1,0:T(8,128)(2,1)}, u32[]{:S(2)}, u32[]{:S(2)}) collective-permute-start(bf16[256,1024]{1,0:T(8,128)(2,1)} %get-tuple-element.87.refs_5_.refs_9_.refs_8_.refs_12_), channel_id=1, source_target_pairs={{0,8},{4,12},{8,0},{12,4},{16,24},{20,28},{24,16},{28,20},{1,9},{5... | collective-permute-start | bytes 1572872 | tf_op jit(solution)/shard_map/ppermute | solution.py:72
  78.3 23.8 %collective-permute-start.14 = (bf16[256,1024]{1,0:T(8,128)(2,1)}, bf16[256,1024]{1,0:T(8,128)(2,1)}, u32[]{:S(2)}, u32[]{:S(2)}) collective-permute-start(bf16[256,1024]{1,0:T(8,128)(2,1)} %get-tuple-element.87.refs_5_.refs_9_.refs_8_.refs_12_), channel_id=1, source_target_pairs={{0,4},{4,0},{8,12},{12,8},{16,20},{20,16},{24,28},{28,24},{1,5},{5... | collective-permute-start | bytes 1572872 | tf_op jit(solution)/shard_map/ppermute | solution.py:72
  78.3 32.3 %collective-permute-start.20 = (bf16[256,1024]{1,0:T(8,128)(2,1)}, bf16[256,1024]{1,0:T(8,128)(2,1)}, u32[]{:S(2)}, u32[]{:S(2)}) collective-permute-start(bf16[256,1024]{1,0:T(8,128)(2,1)} %get-tuple-element.87.refs_5_.refs_9_.refs_8_.refs_12_), channel_id=1, source_target_pairs={{0,16},{4,20},{8,24},{12,28},{16,0},{20,4},{24,8},{28,12},{1,17},{... | collective-permute-start | bytes 1572872 | tf_op jit(solution)/shard_map/ppermute | solution.py:72
  80.5 32.2 %collective-permute-start.23 = (bf16[256,1024]{1,0:T(8,128)(2,1)}, bf16[256,1024]{1,0:T(8,128)(2,1)}, u32[]{:S(2)}, u32[]{:S(2)}) collective-permute-start(bf16[256,1024]{1,0:T(8,128)(2,1)} %get-tuple-element.86.refs_3_.refs_7_.refs_6_.refs_10_), channel_id=1, source_target_pairs={{0,16},{4,20},{8,24},{12,28},{16,0},{20,4},{24,8},{28,12},{1,17},{... | collective-permute-start | bytes 1572872 | tf_op jit(solution)/shard_map/ppermute | solution.py:72
  91.3 21.3 %collective-permute-start.16 = (bf16[256,1024]{1,0:T(8,128)(2,1)}, bf16[256,1024]{1,0:T(8,128)(2,1)}, u32[]{:S(2)}, u32[]{:S(2)}) collective-permute-start(bf16[256,1024]{1,0:T(8,128)(2,1)} %collective-permute-done.12.refs_3_.refs_7_.refs_6_.refs_10_), channel_id=1, source_target_pairs={{0,4},{4,0},{8,12},{12,8},{16,20},{20,16},{24,28},{28,24},{1,5},{5... | collective-permute-start | bytes 1572872 | tf_op jit(solution)/shard_map/ppermute | solution.py:72
  143.9 16.2 %collective-permute-start.26 = (bf16[128,2048]{1,0:T(8,128)(2,1)S(1)}, bf16[128,2048]{1,0:T(8,128)(2,1)S(1)}, u32[]{:S(2)}, u32[]{:S(2)}) collective-permute-start(bf16[128,2048]{1,0:T(8,128)(2,1)S(1)} %convolution_convert_fusion.6), channel_id=1, source_target_pairs={{0,1},{1,2},{2,3},{3,0},{4,5},{5,6},{6,7},{7,4},{8,9},{9,10},{10,1... | collective-permute-start | bytes 1572872 | tf_op jit(solution)/shard_map/ppermute | solution.py:38
  160.6 15.3 %collective-permute-start.27 = (bf16[128,2048]{1,0:T(8,128)(2,1)S(1)}, bf16[128,2048]{1,0:T(8,128)(2,1)S(1)}, u32[]{:S(2)}, u32[]{:S(2)}) collective-permute-start(bf16[128,2048]{1,0:T(8,128)(2,1)S(1)} %add_convert_fusion.26), channel_id=1, source_target_pairs={{0,1},{1,2},{2,3},{3,0},{4,5},{5,6},{6,7},{7,4},{8,9},{9,10},{10,1... | collective-permute-start | bytes 1572872 | tf_op jit(solution)/shard_map/ppermute | solution.py:38
  205.6 16.6 %collective-permute-start.31 = (bf16[128,2048]{1,0:T(8,128)(2,1)S(1)}, bf16[128,2048]{1,0:T(8,128)(2,1)S(1)}, u32[]{:S(2)}, u32[]{:S(2)}) collective-permute-start(bf16[128,2048]{1,0:T(8,128)(2,1)S(1)} %collective-permute-done.29), channel_id=1, source_target_pairs={{0,1},{1,2},{2,3},{3,0},{4,5},{5,6},{6,7},{7,4},{8,9},{9,10},{10,1... | collective-permute-start | bytes 1572872 | tf_op jit(solution)/shard_map/ppermute | solution.py:38
  210.7 22.6 %collective-permute-start.30 = (bf16[128,2048]{1,0:T(8,128)(2,1)S(1)}, bf16[128,2048]{1,0:T(8,128)(2,1)S(1)}, u32[]{:S(2)}, u32[]{:S(2)}) collective-permute-start(bf16[128,2048]{1,0:T(8,128)(2,1)S(1)} %convolution_convert_fusion.5), channel_id=1, source_target_pairs={{0,1},{1,2},{2,3},{3,0},{4,5},{5,6},{6,7},{7,4},{8,9},{9,10},{10,1... | collective-permute-start | bytes 1572872 | tf_op jit(solution)/shard_map/ppermute | solution.py:38
  222.1 22.5 %collective-permute-start.33 = (bf16[128,2048]{1,0:T(8,128)(2,1)S(1)}, bf16[128,2048]{1,0:T(8,128)(2,1)S(1)}, u32[]{:S(2)}, u32[]{:S(2)}) collective-permute-start(bf16[128,2048]{1,0:T(8,128)(2,1)S(1)} %collective-permute-done.31), channel_id=1, source_target_pairs={{0,1},{1,2},{2,3},{3,0},{4,5},{5,6},{6,7},{7,4},{8,9},{9,10},{10,1... | collective-permute-start | bytes 1572872 | tf_op jit(solution)/shard_map/ppermute | solution.py:38
  234.7 17.3 %collective-permute-start.32 = (bf16[128,2048]{1,0:T(8,128)(2,1)S(1)}, bf16[128,2048]{1,0:T(8,128)(2,1)S(1)}, u32[]{:S(2)}, u32[]{:S(2)}) collective-permute-start(bf16[128,2048]{1,0:T(8,128)(2,1)S(1)} %add_convert_fusion.24), channel_id=1, source_target_pairs={{0,1},{1,2},{2,3},{3,0},{4,5},{5,6},{6,7},{7,4},{8,9},{9,10},{10,1... | collective-permute-start | bytes 1572872 | tf_op jit(solution)/shard_map/ppermute | solution.py:38
  322.5 398.7 %reduce-scatter.5.cloned.1.call-start = ((), (), s32[]{:S(2)}) async-start(), calls=%async_computation.3 | async-start | bytes 4718592 | tf_op jit(solution)/shard_map/reduce_scatter | solution.py:523
  328.5 25.9 %collective-permute-start.85 = (bf16[256,2048]{1,0:T(8,128)(2,1)S(1)}, bf16[256,2048]{1,0:T(8,128)(2,1)}, u32[]{:S(2)}, u32[]{:S(2)}) collective-permute-start(bf16[256,2048]{1,0:T(8,128)(2,1)S(1)} %pad_maximum_fusion.4), channel_id=1, source_target_pairs={{0,16},{4,20},{8,24},{12,28},{16,0},{20,4},{24,8},{28,12},{1,17},{... | collective-permute-start | bytes 3145736 | tf_op jit(solution)/shard_map/ppermute | solution.py:72
  329.2 27.6 %collective-permute-start.78 = (bf16[256,2048]{1,0:T(8,128)(2,1)S(1)}, bf16[256,2048]{1,0:T(8,128)(2,1)}, u32[]{:S(2)}, u32[]{:S(2)}) collective-permute-start(bf16[256,2048]{1,0:T(8,128)(2,1)S(1)} %pad_maximum_fusion.4), channel_id=1, source_target_pairs={{0,8},{4,12},{8,0},{12,4},{16,24},{20,28},{24,16},{28,20},{1,9},{5... | collective-permute-start | bytes 3145736 | tf_op jit(solution)/shard_map/ppermute | solution.py:72
  330.6 26.7 %collective-permute-start.76 = (bf16[256,2048]{1,0:T(8,128)(2,1)S(1)}, bf16[256,2048]{1,0:T(8,128)(2,1)S(1)}, u32[]{:S(2)}, u32[]{:S(2)}) collective-permute-start(bf16[256,2048]{1,0:T(8,128)(2,1)S(1)} %pad_maximum_fusion.4), channel_id=1, source_target_pairs={{0,4},{4,0},{8,12},{12,8},{16,20},{20,16},{24,28},{28,24},{1,5},{5... | collective-permute-start | bytes 3145736 | tf_op jit(solution)/shard_map/ppermute | solution.py:72
  333.5 57.2 %collective-permute-start.86 = (bf16[256,2048]{1,0:T(8,128)(2,1)}, bf16[256,2048]{1,0:T(8,128)(2,1)}, u32[]{:S(2)}, u32[]{:S(2)}) collective-permute-start(bf16[256,2048]{1,0:T(8,128)(2,1)} %pad_maximum_fusion.5), channel_id=1, source_target_pairs={{0,16},{4,20},{8,24},{12,28},{16,0},{20,4},{24,8},{28,12},{1,17},{... | collective-permute-start | bytes 3145736 | tf_op jit(solution)/shard_map/ppermute | solution.py:72
  335.5 57.7 %collective-permute-start.79 = (bf16[256,2048]{1,0:T(8,128)(2,1)}, bf16[256,2048]{1,0:T(8,128)(2,1)}, u32[]{:S(2)}, u32[]{:S(2)}) collective-permute-start(bf16[256,2048]{1,0:T(8,128)(2,1)} %pad_maximum_fusion.5), channel_id=1, source_target_pairs={{0,8},{4,12},{8,0},{12,4},{16,24},{20,28},{24,16},{28,20},{1,9},{5... | collective-permute-start | bytes 3145736 | tf_op jit(solution)/shard_map/ppermute | solution.py:72
  354.5 17.1 %collective-permute-start.77 = (bf16[256,2048]{1,0:T(8,128)(2,1)}, bf16[256,2048]{1,0:T(8,128)(2,1)}, u32[]{:S(2)}, u32[]{:S(2)}) collective-permute-start(bf16[256,2048]{1,0:T(8,128)(2,1)} %pad_maximum_fusion.5), channel_id=1, source_target_pairs={{0,4},{4,0},{8,12},{12,8},{16,20},{20,16},{24,28},{28,24},{1,5},{5... | collective-permute-start | bytes 3145736 | tf_op jit(solution)/shard_map/ppermute | solution.py:72
  356.8 42.9 %collective-permute-start.87 = (bf16[256,2048]{1,0:T(8,128)(2,1)}, bf16[256,2048]{1,0:T(8,128)(2,1)}, u32[]{:S(2)}, u32[]{:S(2)}) collective-permute-start(bf16[256,2048]{1,0:T(8,128)(2,1)} %collective-permute-done.85), channel_id=1, source_target_pairs={{0,4},{4,0},{8,12},{12,8},{16,20},{20,16},{24,28},{28,24},{1,5},{5... | collective-permute-start | bytes 3145736 | tf_op jit(solution)/shard_map/ppermute | solution.py:72
  357.3 40.0 %collective-permute-start.80 = (bf16[256,2048]{1,0:T(8,128)(2,1)}, bf16[256,2048]{1,0:T(8,128)(2,1)}, u32[]{:S(2)}, u32[]{:S(2)}) collective-permute-start(bf16[256,2048]{1,0:T(8,128)(2,1)} %collective-permute-done.78), channel_id=1, source_target_pairs={{0,4},{4,0},{8,12},{12,8},{16,20},{20,16},{24,28},{28,24},{1,5},{5... | collective-permute-start | bytes 3145736 | tf_op jit(solution)/shard_map/ppermute | solution.py:72
  371.6 60.0 %collective-permute-start.89 = (bf16[256,2048]{1,0:T(8,128)(2,1)}, bf16[256,2048]{1,0:T(8,128)(2,1)S(1)}, u32[]{:S(2)}, u32[]{:S(2)}) collective-permute-start(bf16[256,2048]{1,0:T(8,128)(2,1)} %collective-permute-done.78), channel_id=1, source_target_pairs={{0,16},{4,20},{8,24},{12,28},{16,0},{20,4},{24,8},{28,12},{1,17},{... | collective-permute-start | bytes 3145736 | tf_op jit(solution)/shard_map/ppermute | solution.py:72
  390.7 49.1 %collective-permute-start.36 = (bf16[128,2048]{1,0:T(8,128)(2,1)S(1)}, bf16[128,2048]{1,0:T(8,128)(2,1)}, u32[]{:S(2)}, u32[]{:S(2)}) collective-permute-start(bf16[128,2048]{1,0:T(8,128)(2,1)S(1)} %fusion.15), channel_id=1, source_target_pairs={{0,1},{1,2},{2,3},{3,0},{4,5},{5,6},{6,7},{7,4},{8,9},{9,10},{10,1... | collective-permute-start | bytes 1572872 | tf_op jit(solution)/shard_map/ppermute | solution.py:38
  393.2 50.7 %collective-permute-start.90 = (bf16[256,2048]{1,0:T(8,128)(2,1)}, bf16[256,2048]{1,0:T(8,128)(2,1)}, u32[]{:S(2)}, u32[]{:S(2)}) collective-permute-start(bf16[256,2048]{1,0:T(8,128)(2,1)} %collective-permute-done.86), channel_id=1, source_target_pairs={{0,8},{4,12},{8,0},{12,4},{16,24},{20,28},{24,16},{28,20},{1,9},{5... | collective-permute-start | bytes 3145736 | tf_op jit(solution)/shard_map/ppermute | solution.py:72
  397.4 47.3 %collective-permute-start.88 = (bf16[256,2048]{1,0:T(8,128)(2,1)}, bf16[256,2048]{1,0:T(8,128)(2,1)S(1)}, u32[]{:S(2)}, u32[]{:S(2)}) collective-permute-start(bf16[256,2048]{1,0:T(8,128)(2,1)} %collective-permute-done.86), channel_id=1, source_target_pairs={{0,4},{4,0},{8,12},{12,8},{16,20},{20,16},{24,28},{28,24},{1,5},{5... | collective-permute-start | bytes 3145736 | tf_op jit(solution)/shard_map/ppermute | solution.py:72
  399.7 49.6 %collective-permute-start.81 = (bf16[256,2048]{1,0:T(8,128)(2,1)}, bf16[256,2048]{1,0:T(8,128)(2,1)S(1)}, u32[]{:S(2)}, u32[]{:S(2)}) collective-permute-start(bf16[256,2048]{1,0:T(8,128)(2,1)} %collective-permute-done.79), channel_id=1, source_target_pairs={{0,4},{4,0},{8,12},{12,8},{16,20},{20,16},{24,28},{28,24},{1,5},{5... | collective-permute-start | bytes 3145736 | tf_op jit(solution)/shard_map/ppermute | solution.py:72
  431.6 30.4 %collective-permute-start.91 = (bf16[256,2048]{1,0:T(8,128)(2,1)S(1)}, bf16[256,2048]{1,0:T(8,128)(2,1)S(1)}, u32[]{:S(2)}, u32[]{:S(2)}) collective-permute-start(bf16[256,2048]{1,0:T(8,128)(2,1)S(1)} %collective-permute-done.89), channel_id=1, source_target_pairs={{0,4},{4,0},{8,12},{12,8},{16,20},{20,16},{24,28},{28,24},{1,5},{5... | collective-permute-start | bytes 3145736 | tf_op jit(solution)/shard_map/ppermute | solution.py:72
  443.9 16.4 %collective-permute-start.38 = (bf16[128,2048]{1,0:T(8,128)(2,1)S(1)}, bf16[128,2048]{1,0:T(8,128)(2,1)}, u32[]{:S(2)}, u32[]{:S(2)}) collective-permute-start(bf16[128,2048]{1,0:T(8,128)(2,1)S(1)} %add_convert_fusion.21), channel_id=1, source_target_pairs={{0,1},{1,2},{2,3},{3,0},{4,5},{5,6},{6,7},{7,4},{8,9},{9,10},{10,1... | collective-permute-start | bytes 1572872 | tf_op jit(solution)/shard_map/ppermute | solution.py:38
  443.9 58.9 %collective-permute-start.92 = (bf16[256,2048]{1,0:T(8,128)(2,1)}, bf16[256,2048]{1,0:T(8,128)(2,1)}, u32[]{:S(2)}, u32[]{:S(2)}) collective-permute-start(bf16[256,2048]{1,0:T(8,128)(2,1)} %collective-permute-done.90), channel_id=1, source_target_pairs={{0,4},{4,0},{8,12},{12,8},{16,20},{20,16},{24,28},{28,24},{1,5},{5... | collective-permute-start | bytes 3145736 | tf_op jit(solution)/shard_map/ppermute | solution.py:72
  461.4 15.9 %collective-permute-start.40 = (bf16[128,2048]{1,0:T(8,128)(2,1)S(1)}, bf16[128,2048]{1,0:T(8,128)(2,1)S(1)}, u32[]{:S(2)}, u32[]{:S(2)}) collective-permute-start(bf16[128,2048]{1,0:T(8,128)(2,1)S(1)} %add_convert_fusion.20), channel_id=1, source_target_pairs={{0,1},{1,2},{2,3},{3,0},{4,5},{5,6},{6,7},{7,4},{8,9},{9,10},{10,1... | collective-permute-start | bytes 1572872 | tf_op jit(solution)/shard_map/ppermute | solution.py:38
  464.2 76.3 %collective-permute-start.93 = (bf16[512,256]{1,0:T(8,128)(2,1)}, bf16[512,256]{1,0:T(8,128)(2,1)}, u32[]{:S(2)}, u32[]{:S(2)}) collective-permute-start(bf16[512,256]{1,0:T(8,128)(2,1)} %get-tuple-element.192), channel_id=1, source_target_pairs={{0,16},{4,20},{8,24},{12,28},{16,0},{20,4},{24,8},{28,12},{1,17},{... | collective-permute-start | bytes 786440 | tf_op jit(solution)/shard_map/ppermute | solution.py:72
  464.2 17.4 %collective-permute-start.84 = (bf16[512,256]{1,0:T(8,128)(2,1)S(1)}, bf16[512,256]{1,0:T(8,128)(2,1)S(1)}, u32[]{:S(2)}, u32[]{:S(2)}) collective-permute-start(bf16[512,256]{1,0:T(8,128)(2,1)S(1)} %get-tuple-element.196), channel_id=1, source_target_pairs={{0,12},{4,8},{8,4},{12,0},{16,28},{20,24},{24,20},{28,16},{1,13},{... | collective-permute-start | bytes 786440 | tf_op jit(solution)/shard_map/ppermute | solution.py:72
  465.4 16.9 %collective-permute-start.83 = (bf16[512,256]{1,0:T(8,128)(2,1)S(1)}, bf16[512,256]{1,0:T(8,128)(2,1)S(1)}, u32[]{:S(2)}, u32[]{:S(2)}) collective-permute-start(bf16[512,256]{1,0:T(8,128)(2,1)S(1)} %get-tuple-element.197), channel_id=1, source_target_pairs={{0,8},{4,12},{8,0},{12,4},{16,24},{20,28},{24,16},{28,20},{1,9},{5... | collective-permute-start | bytes 786440 | tf_op jit(solution)/shard_map/ppermute | solution.py:72
  481.7 59.4 %collective-permute-start.96 = (bf16[512,256]{1,0:T(8,128)(2,1)}, bf16[512,256]{1,0:T(8,128)(2,1)}, u32[]{:S(2)}, u32[]{:S(2)}) collective-permute-start(bf16[512,256]{1,0:T(8,128)(2,1)} %get-tuple-element.193), channel_id=1, source_target_pairs={{0,28},{4,24},{8,20},{12,16},{16,12},{20,8},{24,4},{28,0},{1,29},{... | collective-permute-start | bytes 786440 | tf_op jit(solution)/shard_map/ppermute | solution.py:72
  482.3 58.8 %collective-permute-start.95 = (bf16[512,256]{1,0:T(8,128)(2,1)}, bf16[512,256]{1,0:T(8,128)(2,1)}, u32[]{:S(2)}, u32[]{:S(2)}) collective-permute-start(bf16[512,256]{1,0:T(8,128)(2,1)} %get-tuple-element.194), channel_id=1, source_target_pairs={{0,24},{4,28},{8,16},{12,20},{16,8},{20,12},{24,0},{28,4},{1,25},{... | collective-permute-start | bytes 786440 | tf_op jit(solution)/shard_map/ppermute | solution.py:72
  484.7 15.6 %collective-permute-start.41 = (bf16[128,2048]{1,0:T(8,128)(2,1)}, bf16[128,2048]{1,0:T(8,128)(2,1)S(1)}, u32[]{:S(2)}, u32[]{:S(2)}) collective-permute-start(bf16[128,2048]{1,0:T(8,128)(2,1)} %subtract_convert_fusion), channel_id=1, source_target_pairs={{0,1},{1,2},{2,3},{3,0},{4,5},{5,6},{6,7},{7,4},{8,9},{9,10},{10,1... | collective-permute-start | bytes 1572872 | tf_op jit(solution)/shard_map/ppermute | solution.py:38
  502.9 38.2 %collective-permute-start.94 = (bf16[512,256]{1,0:T(8,128)(2,1)S(1)}, bf16[512,256]{1,0:T(8,128)(2,1)}, u32[]{:S(2)}, u32[]{:S(2)}) collective-permute-start(bf16[512,256]{1,0:T(8,128)(2,1)S(1)} %get-tuple-element.195), channel_id=1, source_target_pairs={{0,20},{4,16},{8,28},{12,24},{16,4},{20,0},{24,12},{28,8},{1,21},{... | collective-permute-start | bytes 786440 | tf_op jit(solution)/shard_map/ppermute | solution.py:72
  567.6 39.8 %collective-permute-start.55 = (bf16[256,1024]{1,0:T(8,128)(2,1)}, bf16[256,1024]{1,0:T(8,128)(2,1)}, u32[]{:S(2)}, u32[]{:S(2)}) collective-permute-start(bf16[256,1024]{1,0:T(8,128)(2,1)} %add_convert_fusion.15), channel_id=1, source_target_pairs={{0,16},{4,20},{8,24},{12,28},{16,0},{20,4},{24,8},{28,12},{1,17},{... | collective-permute-start | bytes 1572872 | tf_op jit(solution)/shard_map/ppermute | solution.py:72
  571.2 15.9 %collective-permute-start.58 = (bf16[256,1024]{1,0:T(8,128)(2,1)}, bf16[256,1024]{1,0:T(8,128)(2,1)}, u32[]{:S(2)}, u32[]{:S(2)}) collective-permute-start(bf16[256,1024]{1,0:T(8,128)(2,1)} %add_convert_fusion.10), channel_id=1, source_target_pairs={{0,8},{4,12},{8,0},{12,4},{16,24},{20,28},{24,16},{28,20},{1,9},{5... | collective-permute-start | bytes 1572872 | tf_op jit(solution)/shard_map/ppermute | solution.py:72
  585.1 45.3 %collective-permute-start.54 = (bf16[256,1024]{1,0:T(8,128)(2,1)}, bf16[256,1024]{1,0:T(8,128)(2,1)}, u32[]{:S(2)}, u32[]{:S(2)}) collective-permute-start(bf16[256,1024]{1,0:T(8,128)(2,1)} %add_convert_fusion.18), channel_id=1, source_target_pairs={{0,16},{4,20},{8,24},{12,28},{16,0},{20,4},{24,8},{28,12},{1,17},{... | collective-permute-start | bytes 1572872 | tf_op jit(solution)/shard_map/ppermute | solution.py:72
  589.6 44.8 %collective-permute-start.59 = (bf16[256,1024]{1,0:T(8,128)(2,1)}, bf16[256,1024]{1,0:T(8,128)(2,1)}, u32[]{:S(2)}, u32[]{:S(2)}) collective-permute-start(bf16[256,1024]{1,0:T(8,128)(2,1)} %add_convert_fusion.9), channel_id=1, source_target_pairs={{0,16},{4,20},{8,24},{12,28},{16,0},{20,4},{24,8},{28,12},{1,17},{... | collective-permute-start | bytes 1572872 | tf_op jit(solution)/shard_map/ppermute | solution.py:72
  614.1 18.4 %collective-permute-start.56 = (bf16[256,1024]{1,0:T(8,128)(2,1)}, bf16[256,1024]{1,0:T(8,128)(2,1)}, u32[]{:S(2)}, u32[]{:S(2)}) collective-permute-start(bf16[256,1024]{1,0:T(8,128)(2,1)} %add_convert_fusion.14), channel_id=1, source_target_pairs={{0,8},{4,12},{8,0},{12,4},{16,24},{20,28},{24,16},{28,20},{1,9},{5... | collective-permute-start | bytes 1572872 | tf_op jit(solution)/shard_map/ppermute | solution.py:72
  615.9 16.6 %collective-permute-start.53 = (bf16[256,1024]{1,0:T(8,128)(2,1)}, bf16[256,1024]{1,0:T(8,128)(2,1)}, u32[]{:S(2)}, u32[]{:S(2)}) collective-permute-start(bf16[256,1024]{1,0:T(8,128)(2,1)} %get-tuple-element.130), channel_id=1, source_target_pairs={{0,4},{4,0},{8,12},{12,8},{16,20},{20,16},{24,28},{28,24},{1,5},{5... | collective-permute-start | bytes 1572872 | tf_op jit(solution)/shard_map/ppermute | solution.py:72
  615.9 18.4 %collective-permute-start.57 = (bf16[256,1024]{1,0:T(8,128)(2,1)}, bf16[256,1024]{1,0:T(8,128)(2,1)}, u32[]{:S(2)}, u32[]{:S(2)}) collective-permute-start(bf16[256,1024]{1,0:T(8,128)(2,1)} %get-tuple-element.135), channel_id=1, source_target_pairs={{0,4},{4,0},{8,12},{12,8},{16,20},{20,16},{24,28},{28,24},{1,5},{5... | collective-permute-start | bytes 1572872 | tf_op jit(solution)/shard_map/ppermute | solution.py:72
  667.0 20.6 %collective-permute-start.64 = (bf16[128,2048]{1,0:T(8,128)(2,1)S(1)}, bf16[128,2048]{1,0:T(8,128)(2,1)S(1)}, u32[]{:S(2)}, u32[]{:S(2)}) collective-permute-start(bf16[128,2048]{1,0:T(8,128)(2,1)S(1)} %fusion.16), channel_id=1, source_target_pairs={{0,1},{1,2},{2,3},{3,0},{4,5},{5,6},{6,7},{7,4},{8,9},{9,10},{10,1... | collective-permute-start | bytes 1572872 | tf_op jit(solution)/shard_map/ppermute | solution.py:38
  689.9 16.0 %collective-permute-start.71 = (bf16[512,512]{1,0:T(8,128)(2,1)S(1)}, bf16[512,512]{1,0:T(8,128)(2,1)S(1)}, u32[]{:S(2)}, u32[]{:S(2)}) collective-permute-start(bf16[512,512]{1,0:T(8,128)(2,1)S(1)} %slice.524), channel_id=1, source_target_pairs={{0,8},{4,12},{8,0},{12,4},{16,24},{20,28},{24,16},{28,20},{1,9},{5... | collective-permute-start | bytes 1572872 | tf_op jit(solution)/shard_map/ppermute | solution.py:72
  (165 other events, 1496.5 us)
Sparse Core Ops, SparseCore 0:
  322.7 144.3 reduce-scatter.2
  658.8 56.3 reduce-scatter.4

commit v4 on v3

--- a/solution.py
+++ b/solution.py
@@ -564,13 +564,7 @@
             return cut
         return swap(cut, nc, m)
 
-    down_grad = None
-    for masks in (range(nc // 2), range(nc // 2, nc)):
-        part = contract_rows(
-            jnp.concatenate([activ[i][m] for m in masks for i in range(2)]),
-            jnp.concatenate([columns(m) for m in masks]),
-        )
-        down_grad = part if down_grad is None else down_grad + part
+    cuts = [columns(m) for m in range(nc)]
 
     attn_gain_part = jnp.sum(state_grad * attn_out * attn_rms[:, None], axis=0)
     attn_grad_b = norm_back(attn_out, attn_rms, attn_gain[None, :], state_grad).astype(BF)
@@ -666,6 +660,14 @@
         nf,
         started=started,
     )
+    down_grad = None
+    for m in range(nc):
+        cut = cuts[m] if m < nc // 2 else gate(cuts[m], *started)
+        for i in range(2):
+            tall = activ[i][m].shape[0]
+            part = contract_rows(activ[i][m], cut[i * tall : (i + 1) * tall])
+            down_grad = part if down_grad is None else down_grad + part
+
     k_rows, v_rows, *_ = lax.optimization_barrier((jnp.concatenate(key_grads), own, *started))
     k_part = contract_rows(x_rows, k_rows).astype(BF)
     v_part = contract_rows(x_rows, v_rows).astype(BF)

time: 738 us -> 736 us (level)
  local copies, waits for them, and re-layouts: 62.6 us -> 29.3 us
  waiting for transfers between devices: 317 us -> 333 us
  starting transfers between devices: 59.6 us -> 70.5 us
    unnamed x242 -> x262, local copies, waits for them, and re-layouts: 41.4 us -> 13.2 us
    ppermute x61, waiting for transfers between devices: 111 us -> 125 us  [swap(): return lax.ppermute(x, 'ctx', [(i, i ^ bit) for i in range(n)])]
    ppermute x61, starting transfers between devices: 37.1 us -> 44.8 us  [swap(): return lax.ppermute(x, 'ctx', [(i, i ^ bit) for i in range(n)])]
    dot_general x7 -> x21, matrix products: 42.9 us -> 43.7 us  [contract_rows(): lax.dot_general(left, right, (((0,), (0,)), ((), ())), preferred_element_...]
  transfers between devices with their start and end apart: 99 -> 99, of which waited for: 37 -> 39; matrix products, arithmetic and copies ran while one was open for 28% -> 25% of each run, Pallas kernels for 9% -> 10%
where the time goes in v4:
time: 736 us; the launch traced here: 731 us
  waiting for transfers between devices  333 us (45%)
  matrix products  154 us (21%)
  Pallas kernels  86 us (12%)
  starting transfers between devices  70.5 us (10%)
  other arithmetic  40.6 us (6%)
  local copies, waits for them, and re-layouts  29.3 us (4%)
  between operations  16.7 us (2%)
    ppermute x36, waiting for transfers between devices, shift(): return lax.ppermute(x, 'fsdp', [(i, (i + by) % n) for i in range(n)])  208 us
    ppermute x61, waiting for transfers between devices, swap(): return lax.ppermute(x, 'ctx', [(i, i ^ bit) for i in range(n)])  125 us
    dot_general x28, matrix products, contract_cols(): lax.dot_general(left, right, (((1,), (1,)), ((), ())), preferred_element_...  72 us
    ppermute x61, starting transfers between devices, swap(): return lax.ppermute(x, 'ctx', [(i, i ^ bit) for i in range(n)])  44.8 us
    dot_general x21, matrix products, contract_rows(): lax.dot_general(left, right, (((0,), (0,)), ((), ())), preferred_element_...  43.7 us
    pallas_call x4, Pallas kernels, attend_back(): pl.pallas_call(functools.partial(bwd_kernel, np_, slots, heads, first), g...  41.7 us
    dot_general x28, matrix products, mm(): return jnp.dot(left, right, preferred_element_type=F32)  38.6 us
    pallas_call x4, Pallas kernels, attend(): pl.pallas_call(functools.partial(fwd_kernel, np_, slots, first, last), gr...  28.9 us
  transfers between devices with their start and end apart: 99, of which 39 were waited for; matrix products, arithmetic and copies ran while one was open for 25% of the time, Pallas kernels for 10%

profile of v4, /device:TPU:0, one launch (start us, length us, event | category | flops | bytes accessed | tf_op | source)
XLA Modules:
  0.0 730.6 jit_solution(11378764355328307370)
XLA Ops:
  18.5 6.1 collective-permute-done
  48.0 8.9 %collective-permute-done.2 = bf16[128,2048]{1,0:T(8,128)(2,1)S(1)} collective-permute-done((bf16[128,2048]{1,0:T(8,128)(2,1)S(1)}, bf16[128,2048]{1,0:T(8,128)(2,1)S(1)}, u32[]{:S(2)}, u32[]{:S(2)}) %collective-permute-start.2) | collective-permute-done | bytes 524320 | tf_op jit(solution)/shard_map/ppermute | solution.py:38
  69.3 5.9 shard_map.237
  80.0 10.4 %collective-permute-done.12.refs_3_.refs_7_.refs_6_.refs_10_ = bf16[256,1024]{1,0:T(8,128)(2,1)} collective-permute-done((bf16[256,1024]{1,0:T(8,128)(2,1)}, bf16[256,1024]{1,0:T(8,128)(2,1)}, u32[]{:S(2)}, u32[]{:S(2)}) %collective-permute-start.12) | collective-permute-done | bytes 524320 | tf_op jit(solution)/shard_map/ppermute | solution.py:72
  90.4 10.7 %collective-permute-done.17.refs_5_.refs_9_.refs_8_.refs_12_ = bf16[256,1024]{1,0:T(8,128)(2,1)} collective-permute-done((bf16[256,1024]{1,0:T(8,128)(2,1)}, bf16[256,1024]{1,0:T(8,128)(2,1)}, u32[]{:S(2)}, u32[]{:S(2)}) %collective-permute-start.17) | collective-permute-done | bytes 524320 | tf_op jit(solution)/shard_map/ppermute | solution.py:72
  101.1 6.9 shard_map.238
  111.9 7.2 shard_map.239
  125.6 7.2 shard_map.240
  132.8 7.5 %shard_map.241 = (f32[512,512]{1,0:T(8,128)}, bf16[512,512]{1,0:T(8,128)(2,1)}, f32[4,1,512]{2,1,0:T(1,128)}) custom-call(s32[8]{0:T(128)} %pad_add_fusion.3.refs_0_, bf16[512,512]{1,0:T(8,128)(2,1)} %get-tuple-element.89.refs_1_, s32[1,512]{1,0:T(1,128)} %bitcast.310, bf16[256,1024]{1,0:T(8,128)(2,1)} %collective-permute-done.15.refs_3_.refs_7_.refs_6_.refs_10_, ...), custom_call_target="tpu_custom_call" | custom-call | flops 2147483648 | bytes 2097152 | tf_op jit(solution)/shard_map/pallas_call | solution.py:234
  142.7 16.1 %collective-permute-done.26 = bf16[128,2048]{1,0:T(8,128)(2,1)S(1)} collective-permute-done((bf16[128,2048]{1,0:T(8,128)(2,1)S(1)}, bf16[128,2048]{1,0:T(8,128)(2,1)S(1)}, u32[]{:S(2)}, u32[]{:S(2)}) %collective-permute-start.26) | collective-permute-done | bytes 524320 | tf_op jit(solution)/shard_map/ppermute | solution.py:38
  159.3 15.3 %collective-permute-done.27 = bf16[128,2048]{1,0:T(8,128)(2,1)S(1)} collective-permute-done((bf16[128,2048]{1,0:T(8,128)(2,1)S(1)}, bf16[128,2048]{1,0:T(8,128)(2,1)S(1)}, u32[]{:S(2)}, u32[]{:S(2)}) %collective-permute-start.27) | collective-permute-done | bytes 524320 | tf_op jit(solution)/shard_map/ppermute | solution.py:38
  175.1 14.4 %collective-permute-done.28 = bf16[128,2048]{1,0:T(8,128)(2,1)S(1)} collective-permute-done((bf16[128,2048]{1,0:T(8,128)(2,1)S(1)}, bf16[128,2048]{1,0:T(8,128)(2,1)S(1)}, u32[]{:S(2)}, u32[]{:S(2)}) %collective-permute-start.28) | collective-permute-done | bytes 524320 | tf_op jit(solution)/shard_map/ppermute | solution.py:38
  192.0 12.2 %collective-permute-done.29 = bf16[128,2048]{1,0:T(8,128)(2,1)S(1)} collective-permute-done((bf16[128,2048]{1,0:T(8,128)(2,1)S(1)}, bf16[128,2048]{1,0:T(8,128)(2,1)S(1)}, u32[]{:S(2)}, u32[]{:S(2)}) %collective-permute-start.29) | collective-permute-done | bytes 524320 | tf_op jit(solution)/shard_map/ppermute | solution.py:38
  209.4 11.4 %collective-permute-done.31 = bf16[128,2048]{1,0:T(8,128)(2,1)S(1)} collective-permute-done((bf16[128,2048]{1,0:T(8,128)(2,1)S(1)}, bf16[128,2048]{1,0:T(8,128)(2,1)S(1)}, u32[]{:S(2)}, u32[]{:S(2)}) %collective-permute-start.31) | collective-permute-done | bytes 524320 | tf_op jit(solution)/shard_map/ppermute | solution.py:38
  224.5 7.5 %collective-permute-done.30 = bf16[128,2048]{1,0:T(8,128)(2,1)S(1)} collective-permute-done((bf16[128,2048]{1,0:T(8,128)(2,1)S(1)}, bf16[128,2048]{1,0:T(8,128)(2,1)S(1)}, u32[]{:S(2)}, u32[]{:S(2)}) %collective-permute-start.30) | collective-permute-done | bytes 524320 | tf_op jit(solution)/shard_map/ppermute | solution.py:38
  233.5 9.7 %collective-permute-done.33 = bf16[128,2048]{1,0:T(8,128)(2,1)S(1)} collective-permute-done((bf16[128,2048]{1,0:T(8,128)(2,1)S(1)}, bf16[128,2048]{1,0:T(8,128)(2,1)S(1)}, u32[]{:S(2)}, u32[]{:S(2)}) %collective-permute-start.33) | collective-permute-done | bytes 524320 | tf_op jit(solution)/shard_map/ppermute | solution.py:38
  253.2 9.4 %collective-permute-done.34 = bf16[128,2048]{1,0:T(8,128)(2,1)S(1)} collective-permute-done((bf16[128,2048]{1,0:T(8,128)(2,1)S(1)}, bf16[128,2048]{1,0:T(8,128)(2,1)S(1)}, u32[]{:S(2)}, u32[]{:S(2)}) %collective-permute-start.34) | collective-permute-done | bytes 524320 | tf_op jit(solution)/shard_map/ppermute | solution.py:38
  265.8 4.0 multiply_convert_fusion.6
  269.8 7.7 %collective-permute-done.35 = bf16[128,2048]{1,0:T(8,128)(2,1)S(1)} collective-permute-done((bf16[128,2048]{1,0:T(8,128)(2,1)S(1)}, bf16[128,2048]{1,0:T(8,128)(2,1)S(1)}, u32[]{:S(2)}, u32[]{:S(2)}) %collective-permute-start.35) | collective-permute-done | bytes 524320 | tf_op jit(solution)/shard_map/ppermute | solution.py:38
  277.9 4.0 multiply_convert_fusion.4
  282.0 9.2 %collective-permute-done.37 = bf16[128,2048]{1,0:T(8,128)(2,1)S(1)} collective-permute-done((bf16[128,2048]{1,0:T(8,128)(2,1)S(1)}, bf16[128,2048]{1,0:T(8,128)(2,1)S(1)}, u32[]{:S(2)}, u32[]{:S(2)}) %collective-permute-start.37) | collective-permute-done | bytes 524320 | tf_op jit(solution)/shard_map/ppermute | solution.py:38
  295.2 6.9 collective-permute-done.39
  306.1 15.0 %convolution_convert_fusion = bf16[2048,4096]{1,0:T(8,128)(2,1)} fusion(bf16[128,2048]{1,0:T(8,128)(2,1)} %get-tuple-element.217, bf16[128,2048]{1,0:T(8,128)(2,1)} %get-tuple-element.132, bf16[128,2048]{1,0:T(8,128)(2,1)} %get-tuple-element.131, bf16[128,2048]{1,0:T(8,128)(2,1)} %get-tuple-element.110, bf16[128,2048]{1,0:T(8,128)(2,1)} %get-tuple-element.218, ...), kind=kOutput, calls=%fused_computation | convolution fusion | flops 8640266240 | bytes 23068672 | tf_op jit(solution)/shard_map/dot_general | solution.py:26
  331.8 8.1 %fusion.160 = f32[128,2048]{1,0:T(8,128)S(1)} fusion(bf16[128,2048]{1,0:T(8,128)(2,1)} %get-tuple-element.129, bf16[2048,2048]{1,0:T(8,128)(2,1)} %param.24), kind=kOutput, calls=%fused_computation.385 | convolution fusion | flops 1073741824 | bytes 9961472 | tf_op jit(solution)/shard_map/dot_general | solution.py:30
  340.0 7.9 %fusion.25 = bf16[128,2048]{1,0:T(8,128)(2,1)S(1)} fusion(f32[128,2048]{1,0:T(8,128)S(1)} %fusion.160, bf16[128,2048]{1,0:T(8,128)(2,1)S(1)} %copy-done.64, bf16[2048,2048]{1,0:T(8,128)(2,1)} %param.25), kind=kOutput, calls=%fused_computation.49 | convolution fusion | flops 1074266112 | bytes 10485760 | tf_op jit(solution)/shard_map/dot_general | solution.py:30
  348.0 6.4 fusion.163
  357.4 6.4 collective-permute-done.36
  375.3 6.8 collective-permute-done.38
  383.9 8.1 %collective-permute-done.81 = bf16[256,2048]{1,0:T(8,128)(2,1)} collective-permute-done((bf16[256,2048]{1,0:T(8,128)(2,1)}, bf16[256,2048]{1,0:T(8,128)(2,1)}, u32[]{:S(2)}, u32[]{:S(2)}) %collective-permute-start.81) | collective-permute-done | bytes 1048608 | tf_op jit(solution)/shard_map/ppermute | solution.py:72
  392.0 8.3 %collective-permute-done.80 = bf16[512,256]{1,0:T(8,128)(2,1)S(1)} collective-permute-done((bf16[512,256]{1,0:T(8,128)(2,1)S(1)}, bf16[512,256]{1,0:T(8,128)(2,1)S(1)}, u32[]{:S(2)}, u32[]{:S(2)}) %collective-permute-start.80) | collective-permute-done | bytes 262176 | tf_op jit(solution)/shard_map/ppermute | solution.py:72
  410.0 12.0 %collective-permute-done.41 = bf16[128,2048]{1,0:T(8,128)(2,1)S(1)} collective-permute-done((bf16[128,2048]{1,0:T(8,128)(2,1)S(1)}, bf16[128,2048]{1,0:T(8,128)(2,1)S(1)}, u32[]{:S(2)}, u32[]{:S(2)}) %collective-permute-start.41) | collective-permute-done | bytes 524320 | tf_op jit(solution)/shard_map/ppermute | solution.py:38
  426.5 10.4 %collective-permute-done.42 = bf16[128,2048]{1,0:T(8,128)(2,1)S(1)} collective-permute-done((bf16[128,2048]{1,0:T(8,128)(2,1)S(1)}, bf16[128,2048]{1,0:T(8,128)(2,1)S(1)}, u32[]{:S(2)}, u32[]{:S(2)}) %collective-permute-start.42) | collective-permute-done | bytes 524320 | tf_op jit(solution)/shard_map/ppermute | solution.py:38
  439.0 12.3 %collective-permute-done.43 = bf16[128,2048]{1,0:T(8,128)(2,1)S(1)} collective-permute-done((bf16[128,2048]{1,0:T(8,128)(2,1)S(1)}, bf16[128,2048]{1,0:T(8,128)(2,1)S(1)}, u32[]{:S(2)}, u32[]{:S(2)}) %collective-permute-start.43) | collective-permute-done | bytes 524320 | tf_op jit(solution)/shard_map/ppermute | solution.py:38
  453.0 10.2 %shard_map.242 = (f32[512,512]{1,0:T(8,128)}, bf16[256,1024]{1,0:T(8,128)(2,1)}, bf16[256,1024]{1,0:T(8,128)(2,1)}, bf16[256,1024]{1,0:T(8,128)(2,1)}, bf16[256,1024]{1,0:T(8,128)(2,1)}) custom-call(s32[8]{0:T(128)} %pad_add_fusion.3.refs_0_, bf16[512,512]{1,0:T(8,128)(2,1)} %get-tuple-element.89.refs_1_, bf16[512,512]{1,0:T(8,128)(2,1)} %pad_maximum_fusion.6.refs_2_, ...), custom_call_target="tpu_custom_call" | custom-call | flops 5368709120 | bytes 4194304 | tf_op jit(solution)/shard_map/pallas_call | solution.py:306
  467.0 4.1 convolution_convert_fusion.3
  471.9 10.5 %shard_map.243 = (f32[512,512]{1,0:T(8,128)}, bf16[256,1024]{1,0:T(8,128)(2,1)}, bf16[256,1024]{1,0:T(8,128)(2,1)}, bf16[256,1024]{1,0:T(8,128)(2,1)}, bf16[256,1024]{1,0:T(8,128)(2,1)}) custom-call(s32[8]{0:T(128)} %pad_add_fusion.6.refs_0_, bf16[512,512]{1,0:T(8,128)(2,1)} %get-tuple-element.89.refs_1_, bf16[512,512]{1,0:T(8,128)(2,1)} %pad_maximum_fusion.6.refs_2_, ...), custom_call_target="tpu_custom_call" | custom-call | flops 5368709120 | bytes 4194304 | tf_op jit(solution)/shard_map/pallas_call | solution.py:306
  489.5 10.4 %shard_map.244 = (f32[512,512]{1,0:T(8,128)}, bf16[256,1024]{1,0:T(8,128)(2,1)}, bf16[256,1024]{1,0:T(8,128)(2,1)}, bf16[256,1024]{1,0:T(8,128)(2,1)}, bf16[256,1024]{1,0:T(8,128)(2,1)}) custom-call(s32[8]{0:T(128)} %pad_add_fusion.5.refs_0_, bf16[512,512]{1,0:T(8,128)(2,1)} %get-tuple-element.89.refs_1_, bf16[512,512]{1,0:T(8,128)(2,1)} %pad_maximum_fusion.6.refs_2_, ...), custom_call_target="tpu_custom_call" | custom-call | flops 5368709120 | bytes 4194304 | tf_op jit(solution)/shard_map/pallas_call | solution.py:306
  506.8 10.5 %shard_map.245 = (f32[512,512]{1,0:T(8,128)}, bf16[256,1024]{1,0:T(8,128)(2,1)}, bf16[256,1024]{1,0:T(8,128)(2,1)}, bf16[256,1024]{1,0:T(8,128)(2,1)}, bf16[256,1024]{1,0:T(8,128)(2,1)}) custom-call(s32[8]{0:T(128)} %pad_add_fusion.4.refs_0_, bf16[512,512]{1,0:T(8,128)(2,1)} %get-tuple-element.89.refs_1_, bf16[512,512]{1,0:T(8,128)(2,1)} %pad_maximum_fusion.6.refs_2_, ...), custom_call_target="tpu_custom_call" | custom-call | flops 5368709120 | bytes 4194304 | tf_op jit(solution)/shard_map/pallas_call | solution.py:306
  517.4 4.9 shard_map.246
  553.5 4.1 collective-permute-done.56
  560.0 4.6 shard_map.247
  571.5 4.2 fusion.145
  575.8 26.0 %collective-permute-done.87 = bf16[256,2048]{1,0:T(8,128)(2,1)} collective-permute-done((bf16[256,2048]{1,0:T(8,128)(2,1)}, bf16[256,2048]{1,0:T(8,128)(2,1)}, u32[]{:S(2)}, u32[]{:S(2)}) %collective-permute-start.87) | collective-permute-done | bytes 1048608 | tf_op jit(solution)/shard_map/ppermute | solution.py:72
  611.3 36.1 %collective-permute-done.86 = bf16[512,256]{1,0:T(8,128)(2,1)S(1)} collective-permute-done((bf16[512,256]{1,0:T(8,128)(2,1)S(1)}, bf16[512,256]{1,0:T(8,128)(2,1)S(1)}, u32[]{:S(2)}, u32[]{:S(2)}) %collective-permute-start.86) | collective-permute-done | bytes 262176 | tf_op jit(solution)/shard_map/ppermute | solution.py:72
  656.2 4.2 collective-permute-done.89
  665.1 5.1 collective-permute-done.95
  691.4 10.6 %collective-permute-done.65 = bf16[128,2048]{1,0:T(8,128)(2,1)S(1)} collective-permute-done((bf16[128,2048]{1,0:T(8,128)(2,1)S(1)}, bf16[128,2048]{1,0:T(8,128)(2,1)S(1)}, u32[]{:S(2)}, u32[]{:S(2)}) %collective-permute-start.65) | collective-permute-done | bytes 524320 | tf_op jit(solution)/shard_map/ppermute | solution.py:38
  705.7 11.2 %collective-permute-done.66 = bf16[128,2048]{1,0:T(8,128)(2,1)S(1)} collective-permute-done((bf16[128,2048]{1,0:T(8,128)(2,1)S(1)}, bf16[128,2048]{1,0:T(8,128)(2,1)S(1)}, u32[]{:S(2)}, u32[]{:S(2)}) %collective-permute-start.66) | collective-permute-done | bytes 524320 | tf_op jit(solution)/shard_map/ppermute | solution.py:38
  (629 shorter events, 256.6 us)
Async XLA Ops:
  7.2 552.8 %reduce-scatter.3.cloned.1.call-start = ((), (), s32[]{:S(2)}) async-start(), calls=%async_computation.2 | async-start | bytes 18874368 | tf_op jit(solution)/shard_map/reduce_scatter | solution.py:523
  7.3 17.3 %collective-permute-start = (bf16[128,2048]{1,0:T(8,128)(2,1)}, bf16[128,2048]{1,0:T(8,128)(2,1)S(1)}, u32[]{:S(2)}, u32[]{:S(2)}) collective-permute-start(bf16[128,2048]{1,0:T(8,128)(2,1)} %param.14), channel_id=1, source_target_pairs={{0,1},{1,2},{2,3},{3,0},{4,5},{5,6},{6,7},{7,4},{8,9},{9,10},{10,1... | collective-permute-start | bytes 1572872 | tf_op jit(solution)/shard_map/ppermute | solution.py:38
  76.4 24.7 %collective-permute-start.17 = (bf16[256,1024]{1,0:T(8,128)(2,1)}, bf16[256,1024]{1,0:T(8,128)(2,1)}, u32[]{:S(2)}, u32[]{:S(2)}) collective-permute-start(bf16[256,1024]{1,0:T(8,128)(2,1)} %get-tuple-element.91.refs_5_.refs_9_.refs_8_.refs_12_), channel_id=1, source_target_pairs={{0,8},{4,12},{8,0},{12,4},{16,24},{20,28},{24,16},{28,20},{1,9},{5... | collective-permute-start | bytes 1572872 | tf_op jit(solution)/shard_map/ppermute | solution.py:72
  77.3 23.8 %collective-permute-start.14 = (bf16[256,1024]{1,0:T(8,128)(2,1)}, bf16[256,1024]{1,0:T(8,128)(2,1)}, u32[]{:S(2)}, u32[]{:S(2)}) collective-permute-start(bf16[256,1024]{1,0:T(8,128)(2,1)} %get-tuple-element.91.refs_5_.refs_9_.refs_8_.refs_12_), channel_id=1, source_target_pairs={{0,4},{4,0},{8,12},{12,8},{16,20},{20,16},{24,28},{28,24},{1,5},{5... | collective-permute-start | bytes 1572872 | tf_op jit(solution)/shard_map/ppermute | solution.py:72
  77.3 30.7 %collective-permute-start.20 = (bf16[256,1024]{1,0:T(8,128)(2,1)}, bf16[256,1024]{1,0:T(8,128)(2,1)}, u32[]{:S(2)}, u32[]{:S(2)}) collective-permute-start(bf16[256,1024]{1,0:T(8,128)(2,1)} %get-tuple-element.91.refs_5_.refs_9_.refs_8_.refs_12_), channel_id=1, source_target_pairs={{0,16},{4,20},{8,24},{12,28},{16,0},{20,4},{24,8},{28,12},{1,17},{... | collective-permute-start | bytes 1572872 | tf_op jit(solution)/shard_map/ppermute | solution.py:72
  79.2 32.2 %collective-permute-start.23 = (bf16[256,1024]{1,0:T(8,128)(2,1)}, bf16[256,1024]{1,0:T(8,128)(2,1)}, u32[]{:S(2)}, u32[]{:S(2)}) collective-permute-start(bf16[256,1024]{1,0:T(8,128)(2,1)} %get-tuple-element.90.refs_3_.refs_7_.refs_6_.refs_10_), channel_id=1, source_target_pairs={{0,16},{4,20},{8,24},{12,28},{16,0},{20,4},{24,8},{28,12},{1,17},{... | collective-permute-start | bytes 1572872 | tf_op jit(solution)/shard_map/ppermute | solution.py:72
  90.4 20.9 %collective-permute-start.16 = (bf16[256,1024]{1,0:T(8,128)(2,1)}, bf16[256,1024]{1,0:T(8,128)(2,1)}, u32[]{:S(2)}, u32[]{:S(2)}) collective-permute-start(bf16[256,1024]{1,0:T(8,128)(2,1)} %collective-permute-done.12.refs_3_.refs_7_.refs_6_.refs_10_), channel_id=1, source_target_pairs={{0,4},{4,0},{8,12},{12,8},{16,20},{20,16},{24,28},{28,24},{1,5},{5... | collective-permute-start | bytes 1572872 | tf_op jit(solution)/shard_map/ppermute | solution.py:72
  142.6 16.2 %collective-permute-start.26 = (bf16[128,2048]{1,0:T(8,128)(2,1)S(1)}, bf16[128,2048]{1,0:T(8,128)(2,1)S(1)}, u32[]{:S(2)}, u32[]{:S(2)}) collective-permute-start(bf16[128,2048]{1,0:T(8,128)(2,1)S(1)} %convolution_convert_fusion.6), channel_id=1, source_target_pairs={{0,1},{1,2},{2,3},{3,0},{4,5},{5,6},{6,7},{7,4},{8,9},{9,10},{10,1... | collective-permute-start | bytes 1572872 | tf_op jit(solution)/shard_map/ppermute | solution.py:38
  159.3 15.3 %collective-permute-start.27 = (bf16[128,2048]{1,0:T(8,128)(2,1)S(1)}, bf16[128,2048]{1,0:T(8,128)(2,1)S(1)}, u32[]{:S(2)}, u32[]{:S(2)}) collective-permute-start(bf16[128,2048]{1,0:T(8,128)(2,1)S(1)} %add_convert_fusion.26), channel_id=1, source_target_pairs={{0,1},{1,2},{2,3},{3,0},{4,5},{5,6},{6,7},{7,4},{8,9},{9,10},{10,1... | collective-permute-start | bytes 1572872 | tf_op jit(solution)/shard_map/ppermute | solution.py:38
  204.2 16.6 %collective-permute-start.31 = (bf16[128,2048]{1,0:T(8,128)(2,1)S(1)}, bf16[128,2048]{1,0:T(8,128)(2,1)S(1)}, u32[]{:S(2)}, u32[]{:S(2)}) collective-permute-start(bf16[128,2048]{1,0:T(8,128)(2,1)S(1)} %collective-permute-done.29), channel_id=1, source_target_pairs={{0,1},{1,2},{2,3},{3,0},{4,5},{5,6},{6,7},{7,4},{8,9},{9,10},{10,1... | collective-permute-start | bytes 1572872 | tf_op jit(solution)/shard_map/ppermute | solution.py:38
  209.3 22.7 %collective-permute-start.30 = (bf16[128,2048]{1,0:T(8,128)(2,1)S(1)}, bf16[128,2048]{1,0:T(8,128)(2,1)S(1)}, u32[]{:S(2)}, u32[]{:S(2)}) collective-permute-start(bf16[128,2048]{1,0:T(8,128)(2,1)S(1)} %convolution_convert_fusion.5), channel_id=1, source_target_pairs={{0,1},{1,2},{2,3},{3,0},{4,5},{5,6},{6,7},{7,4},{8,9},{9,10},{10,1... | collective-permute-start | bytes 1572872 | tf_op jit(solution)/shard_map/ppermute | solution.py:38
  222.1 21.2 %collective-permute-start.33 = (bf16[128,2048]{1,0:T(8,128)(2,1)S(1)}, bf16[128,2048]{1,0:T(8,128)(2,1)S(1)}, u32[]{:S(2)}, u32[]{:S(2)}) collective-permute-start(bf16[128,2048]{1,0:T(8,128)(2,1)S(1)} %collective-permute-done.31), channel_id=1, source_target_pairs={{0,1},{1,2},{2,3},{3,0},{4,5},{5,6},{6,7},{7,4},{8,9},{9,10},{10,1... | collective-permute-start | bytes 1572872 | tf_op jit(solution)/shard_map/ppermute | solution.py:38
  233.3 17.3 %collective-permute-start.32 = (bf16[128,2048]{1,0:T(8,128)(2,1)S(1)}, bf16[128,2048]{1,0:T(8,128)(2,1)S(1)}, u32[]{:S(2)}, u32[]{:S(2)}) collective-permute-start(bf16[128,2048]{1,0:T(8,128)(2,1)S(1)} %add_convert_fusion.24), channel_id=1, source_target_pairs={{0,1},{1,2},{2,3},{3,0},{4,5},{5,6},{6,7},{7,4},{8,9},{9,10},{10,1... | collective-permute-start | bytes 1572872 | tf_op jit(solution)/shard_map/ppermute | solution.py:38
  321.1 399.3 %reduce-scatter.5.cloned.1.call-start = ((), (), s32[]{:S(2)}) async-start(), calls=%async_computation.3 | async-start | bytes 4718592 | tf_op jit(solution)/shard_map/reduce_scatter | solution.py:523
  328.7 77.5 %collective-permute-start.79 = (bf16[256,2048]{1,0:T(8,128)(2,1)}, bf16[256,2048]{1,0:T(8,128)(2,1)}, u32[]{:S(2)}, u32[]{:S(2)}) collective-permute-start(bf16[256,2048]{1,0:T(8,128)(2,1)} %pad_maximum_fusion.4), channel_id=1, source_target_pairs={{0,8},{4,12},{8,0},{12,4},{16,24},{20,28},{24,16},{28,20},{1,9},{5... | collective-permute-start | bytes 3145736 | tf_op jit(solution)/shard_map/ppermute | solution.py:72
  329.7 92.3 %collective-permute-start.76 = (bf16[256,2048]{1,0:T(8,128)(2,1)}, bf16[256,2048]{1,0:T(8,128)(2,1)}, u32[]{:S(2)}, u32[]{:S(2)}) collective-permute-start(bf16[256,2048]{1,0:T(8,128)(2,1)} %pad_maximum_fusion.4), channel_id=1, source_target_pairs={{0,4},{4,0},{8,12},{12,8},{16,20},{20,16},{24,28},{28,24},{1,5},{5... | collective-permute-start | bytes 3145736 | tf_op jit(solution)/shard_map/ppermute | solution.py:72
  330.8 61.3 %collective-permute-start.81 = (bf16[256,2048]{1,0:T(8,128)(2,1)}, bf16[256,2048]{1,0:T(8,128)(2,1)}, u32[]{:S(2)}, u32[]{:S(2)}) collective-permute-start(bf16[256,2048]{1,0:T(8,128)(2,1)} %pad_maximum_fusion.5), channel_id=1, source_target_pairs={{0,8},{4,12},{8,0},{12,4},{16,24},{20,28},{24,16},{28,20},{1,9},{5... | collective-permute-start | bytes 3145736 | tf_op jit(solution)/shard_map/ppermute | solution.py:72
  347.9 15.9 %collective-permute-start.36 = (bf16[128,2048]{1,0:T(8,128)(2,1)S(1)}, bf16[128,2048]{1,0:T(8,128)(2,1)S(1)}, u32[]{:S(2)}, u32[]{:S(2)}) collective-permute-start(bf16[128,2048]{1,0:T(8,128)(2,1)S(1)} %fusion.25), channel_id=1, source_target_pairs={{0,1},{1,2},{2,3},{3,0},{4,5},{5,6},{6,7},{7,4},{8,9},{9,10},{10,1... | collective-permute-start | bytes 1572872 | tf_op jit(solution)/shard_map/ppermute | solution.py:38
  368.5 31.9 %collective-permute-start.80 = (bf16[512,256]{1,0:T(8,128)(2,1)S(1)}, bf16[512,256]{1,0:T(8,128)(2,1)S(1)}, u32[]{:S(2)}, u32[]{:S(2)}) collective-permute-start(bf16[512,256]{1,0:T(8,128)(2,1)S(1)} %get-tuple-element.198), channel_id=1, source_target_pairs={{0,8},{4,12},{8,0},{12,4},{16,24},{20,28},{24,16},{28,20},{1,9},{5... | collective-permute-start | bytes 786440 | tf_op jit(solution)/shard_map/ppermute | solution.py:72
  382.2 20.0 %collective-permute-start.40 = (bf16[128,2048]{1,0:T(8,128)(2,1)S(1)}, bf16[128,2048]{1,0:T(8,128)(2,1)S(1)}, u32[]{:S(2)}, u32[]{:S(2)}) collective-permute-start(bf16[128,2048]{1,0:T(8,128)(2,1)S(1)} %add_convert_fusion.20), channel_id=1, source_target_pairs={{0,1},{1,2},{2,3},{3,0},{4,5},{5,6},{6,7},{7,4},{8,9},{9,10},{10,1... | collective-permute-start | bytes 1572872 | tf_op jit(solution)/shard_map/ppermute | solution.py:38
  392.0 16.3 %collective-permute-start.78 = (bf16[256,2048]{1,0:T(8,128)(2,1)}, bf16[256,2048]{1,0:T(8,128)(2,1)S(1)}, u32[]{:S(2)}, u32[]{:S(2)}) collective-permute-start(bf16[256,2048]{1,0:T(8,128)(2,1)} %pad_maximum_fusion.5), channel_id=1, source_target_pairs={{0,4},{4,0},{8,12},{12,8},{16,20},{20,16},{24,28},{28,24},{1,5},{5... | collective-permute-start | bytes 3145736 | tf_op jit(solution)/shard_map/ppermute | solution.py:72
  400.3 63.5 %collective-permute-start.84 = (bf16[256,2048]{1,0:T(8,128)(2,1)}, bf16[256,2048]{1,0:T(8,128)(2,1)}, u32[]{:S(2)}, u32[]{:S(2)}) collective-permute-start(bf16[256,2048]{1,0:T(8,128)(2,1)} %collective-permute-done.81), channel_id=1, source_target_pairs={{0,4},{4,0},{8,12},{12,8},{16,20},{20,16},{24,28},{28,24},{1,5},{5... | collective-permute-start | bytes 3145736 | tf_op jit(solution)/shard_map/ppermute | solution.py:72
  406.2 15.8 %collective-permute-start.41 = (bf16[128,2048]{1,0:T(8,128)(2,1)S(1)}, bf16[128,2048]{1,0:T(8,128)(2,1)S(1)}, u32[]{:S(2)}, u32[]{:S(2)}) collective-permute-start(bf16[128,2048]{1,0:T(8,128)(2,1)S(1)} %subtract_convert_fusion), channel_id=1, source_target_pairs={{0,1},{1,2},{2,3},{3,0},{4,5},{5,6},{6,7},{7,4},{8,9},{9,10},{10,1... | collective-permute-start | bytes 1572872 | tf_op jit(solution)/shard_map/ppermute | solution.py:38
  408.3 55.5 %collective-permute-start.83 = (bf16[512,256]{1,0:T(8,128)(2,1)}, bf16[512,256]{1,0:T(8,128)(2,1)S(1)}, u32[]{:S(2)}, u32[]{:S(2)}) collective-permute-start(bf16[512,256]{1,0:T(8,128)(2,1)} %get-tuple-element.197), channel_id=1, source_target_pairs={{0,12},{4,8},{8,4},{12,0},{16,28},{20,24},{24,20},{28,16},{1,13},{... | collective-permute-start | bytes 786440 | tf_op jit(solution)/shard_map/ppermute | solution.py:72
  485.0 15.6 %collective-permute-start.58 = (bf16[256,1024]{1,0:T(8,128)(2,1)}, bf16[256,1024]{1,0:T(8,128)(2,1)}, u32[]{:S(2)}, u32[]{:S(2)}) collective-permute-start(bf16[256,1024]{1,0:T(8,128)(2,1)} %add_convert_fusion.10), channel_id=1, source_target_pairs={{0,8},{4,12},{8,0},{12,4},{16,24},{20,28},{24,16},{28,20},{1,9},{5... | collective-permute-start | bytes 1572872 | tf_op jit(solution)/shard_map/ppermute | solution.py:72
  488.4 36.3 %collective-permute-start.55 = (bf16[256,1024]{1,0:T(8,128)(2,1)}, bf16[256,1024]{1,0:T(8,128)(2,1)}, u32[]{:S(2)}, u32[]{:S(2)}) collective-permute-start(bf16[256,1024]{1,0:T(8,128)(2,1)} %add_convert_fusion.15), channel_id=1, source_target_pairs={{0,16},{4,20},{8,24},{12,28},{16,0},{20,4},{24,8},{28,12},{1,17},{... | collective-permute-start | bytes 1572872 | tf_op jit(solution)/shard_map/ppermute | solution.py:72
  502.7 45.0 %collective-permute-start.59 = (bf16[256,1024]{1,0:T(8,128)(2,1)}, bf16[256,1024]{1,0:T(8,128)(2,1)}, u32[]{:S(2)}, u32[]{:S(2)}) collective-permute-start(bf16[256,1024]{1,0:T(8,128)(2,1)} %add_convert_fusion.9), channel_id=1, source_target_pairs={{0,16},{4,20},{8,24},{12,28},{16,0},{20,4},{24,8},{28,12},{1,17},{... | collective-permute-start | bytes 1572872 | tf_op jit(solution)/shard_map/ppermute | solution.py:72
  506.5 47.0 %collective-permute-start.54 = (bf16[256,1024]{1,0:T(8,128)(2,1)}, bf16[256,1024]{1,0:T(8,128)(2,1)}, u32[]{:S(2)}, u32[]{:S(2)}) collective-permute-start(bf16[256,1024]{1,0:T(8,128)(2,1)} %add_convert_fusion.18), channel_id=1, source_target_pairs={{0,16},{4,20},{8,24},{12,28},{16,0},{20,4},{24,8},{28,12},{1,17},{... | collective-permute-start | bytes 1572872 | tf_op jit(solution)/shard_map/ppermute | solution.py:72
  533.1 15.8 %collective-permute-start.60 = (bf16[256,1024]{1,0:T(8,128)(2,1)}, bf16[256,1024]{1,0:T(8,128)(2,1)}, u32[]{:S(2)}, u32[]{:S(2)}) collective-permute-start(bf16[256,1024]{1,0:T(8,128)(2,1)} %add_convert_fusion.7), channel_id=1, source_target_pairs={{0,8},{4,12},{8,0},{12,4},{16,24},{20,28},{24,16},{28,20},{1,9},{5... | collective-permute-start | bytes 1572872 | tf_op jit(solution)/shard_map/ppermute | solution.py:72
  535.0 15.5 %collective-permute-start.57 = (bf16[256,1024]{1,0:T(8,128)(2,1)}, bf16[256,1024]{1,0:T(8,128)(2,1)}, u32[]{:S(2)}, u32[]{:S(2)}) collective-permute-start(bf16[256,1024]{1,0:T(8,128)(2,1)} %get-tuple-element.139), channel_id=1, source_target_pairs={{0,4},{4,0},{8,12},{12,8},{16,20},{20,16},{24,28},{28,24},{1,5},{5... | collective-permute-start | bytes 1572872 | tf_op jit(solution)/shard_map/ppermute | solution.py:72
  535.0 22.6 %collective-permute-start.56 = (bf16[256,1024]{1,0:T(8,128)(2,1)}, bf16[256,1024]{1,0:T(8,128)(2,1)}, u32[]{:S(2)}, u32[]{:S(2)}) collective-permute-start(bf16[256,1024]{1,0:T(8,128)(2,1)} %add_convert_fusion.14), channel_id=1, source_target_pairs={{0,8},{4,12},{8,0},{12,4},{16,24},{20,28},{24,16},{28,20},{1,9},{5... | collective-permute-start | bytes 1572872 | tf_op jit(solution)/shard_map/ppermute | solution.py:72
  548.9 62.3 %collective-permute-start.85 = (bf16[256,2048]{1,0:T(8,128)(2,1)}, bf16[256,2048]{1,0:T(8,128)(2,1)}, u32[]{:S(2)}, u32[]{:S(2)}) collective-permute-start(bf16[256,2048]{1,0:T(8,128)(2,1)} %pad_maximum_fusion.4), channel_id=1, source_target_pairs={{0,16},{4,20},{8,24},{12,28},{16,0},{20,4},{24,8},{28,12},{1,17},{... | collective-permute-start | bytes 3145736 | tf_op jit(solution)/shard_map/ppermute | solution.py:72
  550.5 51.3 %collective-permute-start.87 = (bf16[256,2048]{1,0:T(8,128)(2,1)}, bf16[256,2048]{1,0:T(8,128)(2,1)}, u32[]{:S(2)}, u32[]{:S(2)}) collective-permute-start(bf16[256,2048]{1,0:T(8,128)(2,1)} %pad_maximum_fusion.5), channel_id=1, source_target_pairs={{0,16},{4,20},{8,24},{12,28},{16,0},{20,4},{24,8},{28,12},{1,17},{... | collective-permute-start | bytes 3145736 | tf_op jit(solution)/shard_map/ppermute | solution.py:72
  566.6 39.1 %collective-permute-start.62 = (f32[4,640]{1,0:T(4,128)S(1)}, f32[4,640]{1,0:T(4,128)S(1)}, u32[]{:S(2)}, u32[]{:S(2)}) collective-permute-start(f32[4,640]{1,0:T(4,128)S(1)} %pad_maximum_fusion.13), channel_id=1, source_target_pairs={{0,2},{1,3},{2,0},{3,1},{4,6},{5,7},{6,4},{7,5},{8,10},{9,11},{10,... | collective-permute-start | bytes 30728 | tf_op jit(solution)/shard_map/ppermute | solution.py:38
  567.4 36.9 %collective-permute-start.61 = (f32[4,640]{1,0:T(4,128)S(1)}, f32[4,640]{1,0:T(4,128)S(1)}, u32[]{:S(2)}, u32[]{:S(2)}) collective-permute-start(f32[4,640]{1,0:T(4,128)S(1)} %pad_maximum_fusion.13), channel_id=1, source_target_pairs={{0,1},{1,2},{2,3},{3,0},{4,5},{5,6},{6,7},{7,4},{8,9},{9,10},{10,1... | collective-permute-start | bytes 30728 | tf_op jit(solution)/shard_map/ppermute | solution.py:38
  567.7 36.7 %collective-permute-start.63 = (f32[4,640]{1,0:T(4,128)S(1)}, f32[4,640]{1,0:T(4,128)S(1)}, u32[]{:S(2)}, u32[]{:S(2)}) collective-permute-start(f32[4,640]{1,0:T(4,128)S(1)} %pad_maximum_fusion.13), channel_id=1, source_target_pairs={{0,3},{1,0},{2,1},{3,2},{4,7},{5,4},{6,5},{7,6},{8,11},{9,8},{10,9... | collective-permute-start | bytes 30728 | tf_op jit(solution)/shard_map/ppermute | solution.py:38
  601.8 50.2 %collective-permute-start.91 = (bf16[256,2048]{1,0:T(8,128)(2,1)}, bf16[256,2048]{1,0:T(8,128)(2,1)S(1)}, u32[]{:S(2)}, u32[]{:S(2)}) collective-permute-start(bf16[256,2048]{1,0:T(8,128)(2,1)} %collective-permute-done.79), channel_id=1, source_target_pairs={{0,16},{4,20},{8,24},{12,28},{16,0},{20,4},{24,8},{28,12},{1,17},{... | collective-permute-start | bytes 3145736 | tf_op jit(solution)/shard_map/ppermute | solution.py:72
  604.3 43.1 %collective-permute-start.93 = (bf16[256,2048]{1,0:T(8,128)(2,1)}, bf16[256,2048]{1,0:T(8,128)(2,1)S(1)}, u32[]{:S(2)}, u32[]{:S(2)}) collective-permute-start(bf16[256,2048]{1,0:T(8,128)(2,1)} %collective-permute-done.87), channel_id=1, source_target_pairs={{0,8},{4,12},{8,0},{12,4},{16,24},{20,28},{24,16},{28,20},{1,9},{5... | collective-permute-start | bytes 3145736 | tf_op jit(solution)/shard_map/ppermute | solution.py:72
  604.4 43.1 %collective-permute-start.86 = (bf16[512,256]{1,0:T(8,128)(2,1)S(1)}, bf16[512,256]{1,0:T(8,128)(2,1)S(1)}, u32[]{:S(2)}, u32[]{:S(2)}) collective-permute-start(bf16[512,256]{1,0:T(8,128)(2,1)S(1)} %copy-done.94), channel_id=1, source_target_pairs={{0,16},{4,20},{8,24},{12,28},{16,0},{20,4},{24,8},{28,12},{1,17},{... | collective-permute-start | bytes 786440 | tf_op jit(solution)/shard_map/ppermute | solution.py:72
  605.7 42.3 %collective-permute-start.92 = (bf16[512,256]{1,0:T(8,128)(2,1)S(1)}, bf16[512,256]{1,0:T(8,128)(2,1)S(1)}, u32[]{:S(2)}, u32[]{:S(2)}) collective-permute-start(bf16[512,256]{1,0:T(8,128)(2,1)S(1)} %copy-done.93), channel_id=1, source_target_pairs={{0,24},{4,28},{8,16},{12,20},{16,8},{20,12},{24,0},{28,4},{1,25},{... | collective-permute-start | bytes 786440 | tf_op jit(solution)/shard_map/ppermute | solution.py:72
  611.2 61.4 %collective-permute-start.82 = (bf16[256,2048]{1,0:T(8,128)(2,1)}, bf16[256,2048]{1,0:T(8,128)(2,1)S(1)}, u32[]{:S(2)}, u32[]{:S(2)}) collective-permute-start(bf16[256,2048]{1,0:T(8,128)(2,1)} %collective-permute-done.79), channel_id=1, source_target_pairs={{0,4},{4,0},{8,12},{12,8},{16,20},{20,16},{24,28},{28,24},{1,5},{5... | collective-permute-start | bytes 3145736 | tf_op jit(solution)/shard_map/ppermute | solution.py:72
  647.5 27.5 %collective-permute-start.88 = (bf16[256,2048]{1,0:T(8,128)(2,1)}, bf16[256,2048]{1,0:T(8,128)(2,1)S(1)}, u32[]{:S(2)}, u32[]{:S(2)}) collective-permute-start(bf16[256,2048]{1,0:T(8,128)(2,1)} %collective-permute-done.85), channel_id=1, source_target_pairs={{0,4},{4,0},{8,12},{12,8},{16,20},{20,16},{24,28},{28,24},{1,5},{5... | collective-permute-start | bytes 3145736 | tf_op jit(solution)/shard_map/ppermute | solution.py:72
  648.0 22.5 %collective-permute-start.96 = (bf16[256,2048]{1,0:T(8,128)(2,1)S(1)}, bf16[256,2048]{1,0:T(8,128)(2,1)S(1)}, u32[]{:S(2)}, u32[]{:S(2)}) collective-permute-start(bf16[256,2048]{1,0:T(8,128)(2,1)S(1)} %collective-permute-done.93), channel_id=1, source_target_pairs={{0,4},{4,0},{8,12},{12,8},{16,20},{20,16},{24,28},{28,24},{1,5},{5... | collective-permute-start | bytes 3145736 | tf_op jit(solution)/shard_map/ppermute | solution.py:72
  660.4 15.5 %collective-permute-start.94 = (bf16[256,2048]{1,0:T(8,128)(2,1)S(1)}, bf16[256,2048]{1,0:T(8,128)(2,1)S(1)}, u32[]{:S(2)}, u32[]{:S(2)}) collective-permute-start(bf16[256,2048]{1,0:T(8,128)(2,1)S(1)} %collective-permute-done.91), channel_id=1, source_target_pairs={{0,4},{4,0},{8,12},{12,8},{16,20},{20,16},{24,28},{28,24},{1,5},{5... | collective-permute-start | bytes 3145736 | tf_op jit(solution)/shard_map/ppermute | solution.py:72
  670.2 16.0 %collective-permute-start.64 = (bf16[128,2048]{1,0:T(8,128)(2,1)S(1)}, bf16[128,2048]{1,0:T(8,128)(2,1)S(1)}, u32[]{:S(2)}, u32[]{:S(2)}) collective-permute-start(bf16[128,2048]{1,0:T(8,128)(2,1)S(1)} %fusion.26), channel_id=1, source_target_pairs={{0,1},{1,2},{2,3},{3,0},{4,5},{5,6},{6,7},{7,4},{8,9},{9,10},{10,1... | collective-permute-start | bytes 1572872 | tf_op jit(solution)/shard_map/ppermute | solution.py:38
  672.6 15.6 %collective-permute-start.70 = (bf16[1024,512]{1,0:T(8,128)(2,1)S(1)}, bf16[1024,512]{1,0:T(8,128)(2,1)S(1)}, u32[]{:S(2)}, u32[]{:S(2)}) collective-permute-start(bf16[1024,512]{1,0:T(8,128)(2,1)S(1)} %pad_maximum_fusion.3), channel_id=1, source_target_pairs={{0,4},{4,0},{8,12},{12,8},{16,20},{20,16},{24,28},{28,24},{1,5},{5... | collective-permute-start | bytes 3145736 | tf_op jit(solution)/shard_map/ppermute | solution.py:72
  675.0 15.5 %collective-permute-start.67 = (bf16[1024,512]{1,0:T(8,128)(2,1)S(1)}, bf16[1024,512]{1,0:T(8,128)(2,1)S(1)}, u32[]{:S(2)}, u32[]{:S(2)}) collective-permute-start(bf16[1024,512]{1,0:T(8,128)(2,1)S(1)} %pad_maximum_fusion.2), channel_id=1, source_target_pairs={{0,4},{4,0},{8,12},{12,8},{16,20},{20,16},{24,28},{28,24},{1,5},{5... | collective-permute-start | bytes 3145736 | tf_op jit(solution)/shard_map/ppermute | solution.py:72
  703.0 15.6 %collective-permute-start.72 = (bf16[256,512]{1,0:T(8,128)(2,1)S(1)}, bf16[256,512]{1,0:T(8,128)(2,1)S(1)}, u32[]{:S(2)}, u32[]{:S(2)}) collective-permute-start(bf16[256,512]{1,0:T(8,128)(2,1)S(1)} %slice.590), channel_id=1, source_target_pairs={{0,16},{4,20},{8,24},{12,28},{16,0},{20,4},{24,8},{28,12},{1,17},{... | collective-permute-start | bytes 786440 | tf_op jit(solution)/shard_map/ppermute | solution.py:72
  (181 other events, 1708.6 us)
Sparse Core Ops, SparseCore 0:
  321.2 133.7 reduce-scatter.2
  571.6 64.7 reduce-scatter.4
